TPU v7x, 32 devices: a whole 2x2x4 slice. The times are simulated.
32 devices in a mesh: section: 2 (over core), dp: 8 (over z, x), mp: 2 (over y).
Axes of the slice: x: 2, y: 2, z: 4, core: 2. Of those that a mesh axis runs over, the one named last changes fastest.
Arguments:
- images: bfloat16 [2, 16, 197, 1024], P(None, 'dp'), may hold values from -6 to 6
- cotangent: bfloat16 [2, 16, 197, 1024], P(None, 'dp'), may hold values from -6 to 6
- live_count: int32 [2, 8], P(None, 'dp'), may hold values from 1 to 2, as said below
- ln1_gain: bfloat16 [2, 1024], P('section', 'dp'), may hold values from 0.099609375 to 1.8984375
- ln1_bias: bfloat16 [2, 1024], P('section', 'dp'), may hold values from -3 to 3
- qkv_weight: bfloat16 [2, 3, 1024, 1024], P('section', None, 'dp', 'mp'), may hold values from -0.1875 to 0.1875
- qv_bias: bfloat16 [2, 2, 16, 64], P('section', None, 'mp', 'dp'), may hold values from -3 to 3
- out_weight: bfloat16 [2, 1024, 1024], P('section', 'mp', 'dp'), may hold values from -1.5 to 1.5
- out_bias: bfloat16 [2, 1024], P('section', 'dp'), may hold values from -3 to 3
- ln2_gain: bfloat16 [2, 1024], P('section', 'dp'), may hold values from 0.099609375 to 1.8984375
- ln2_bias: bfloat16 [2, 1024], P('section', 'dp'), may hold values from -3 to 3
- up_weight: bfloat16 [2, 1024, 4096], P('section', 'dp', 'mp'), may hold values from -0.1875 to 0.1875
- up_bias: bfloat16 [2, 16, 256], P('section', 'mp', 'dp'), may hold values from -3 to 3
- down_weight: bfloat16 [2, 4096, 1024], P('section', 'mp', 'dp'), may hold values from -0.09375 to 0.09375
- down_bias: bfloat16 [2, 1024], P('section', 'dp'), may hold values from -3 to 3
Outputs:
- activations: bfloat16 [2, 2, 16, 197, 1024], P('section', None, 'dp')
- input_grads: bfloat16 [2, 2, 16, 197, 1024], P('section', None, 'dp')
- grad_ln1_gain: float32 [2, 1024], P('section', 'dp')
- grad_ln1_bias: float32 [2, 1024], P('section', 'dp')
- grad_qkv_weight: float32 [2, 3, 1024, 1024], P('section', None, 'dp', 'mp')
- grad_qv_bias: float32 [2, 2, 16, 64], P('section', None, 'mp', 'dp')
- grad_out_weight: float32 [2, 1024, 1024], P('section', 'mp', 'dp')
- grad_out_bias: float32 [2, 1024], P('section', 'dp')
- grad_ln2_gain: float32 [2, 1024], P('section', 'dp')
- grad_ln2_bias: float32 [2, 1024], P('section', 'dp')
- grad_up_weight: float32 [2, 1024, 4096], P('section', 'dp', 'mp')
- grad_up_bias: float32 [2, 16, 256], P('section', 'mp', 'dp')
- grad_down_weight: float32 [2, 4096, 1024], P('section', 'mp', 'dp')
- grad_down_bias: float32 [2, 1024], P('section', 'dp')
Inputs may be any that keep to these rules, and one draw needn't show every extreme that they name: Micro-batch m has live_count[m, d] images on data device d, in its first slots; its other slots hold values that no output reads.
All inputs are finite; a program needn't handle non-finite values.
Results may differ from a plain program's by a relative error of at most 0.015.
Values may be sent and summed in bfloat16 or wider, within the bound.
A program may use at most 256 MiB of HBM per device.

v0:
```python
import math

import jax
import jax.numpy as jnp
from jax import lax
from jax.sharding import PartitionSpec as P

HD = 64


epsilon = 1e-06


def from_behind(x, axis, by):
    length = lax.axis_size(axis)
    pairs = [(i, i + by) for i in range(length) if 0 <= i + by < length]
    return lax.ppermute(x, axis, pairs)


def norm_parts(stream):
    centered = stream - jnp.mean(stream, axis=-1, keepdims=True)
    inverse = lax.rsqrt(jnp.mean(centered * centered, axis=-1, keepdims=True) + epsilon)
    return (centered * inverse, inverse)


def norm_back(grad_normed, normed, inverse):
    first_mean = jnp.mean(grad_normed, axis=-1, keepdims=True)
    second_mean = jnp.mean(grad_normed * normed, axis=-1, keepdims=True)
    return inverse * (grad_normed - first_mean - normed * second_mean)


def gelu_slope(preact):
    cumul = 0.5 * (1.0 + lax.erf(preact * 2.0 ** (-0.5)))
    density = jnp.exp(-0.5 * preact * preact) * (2.0 * math.pi) ** (-0.5)
    return cumul + preact * density


def unpack_weights(whole):
    return (
        whole[0][0].astype(jnp.float32),
        whole[1][0].astype(jnp.float32),
        whole[2][0],
        whole[3][0].reshape(2, -1).astype(jnp.float32),
        whole[4][0],
        whole[5][0].astype(jnp.float32),
        whole[6][0].astype(jnp.float32),
        whole[7][0].astype(jnp.float32),
        whole[8][0],
        whole[9][0].reshape(-1).astype(jnp.float32),
        whole[10][0],
        whole[11][0].astype(jnp.float32),
    )


def forward(stream, params, rows):
    (
        gain_one,
        shift_one,
        qkv_mat,
        qv_shift,
        out_mat,
        out_shift,
        gain_two,
        shift_two,
        up_mat,
        up_shift,
        down_mat,
        down_shift,
    ) = params
    batch_size, seq_len, model_width = stream.shape
    head_count = qkv_mat.shape[2] // HD
    scale = HD ** (-0.5)
    normed, inverse = norm_parts(stream)
    lowered = (normed * gain_one + shift_one).astype(jnp.bfloat16)
    projected = jnp.einsum("bld,cde->cble", lowered, qkv_mat, preferred_element_type=jnp.float32)
    split_shape = (batch_size, seq_len, head_count, HD)
    queries = (projected[0] + qv_shift[0]).astype(jnp.bfloat16).reshape(split_shape)
    keys_low = projected[1].astype(jnp.bfloat16).reshape(split_shape)
    values_low = (projected[2] + qv_shift[1]).astype(jnp.bfloat16).reshape(split_shape)
    scores = (
        jnp.einsum("blhe,bmhe->bhlm", queries, keys_low, preferred_element_type=jnp.float32) * scale
    )
    row_max = jnp.max(scores, axis=-1, keepdims=True)
    log_total = row_max + jnp.log(jnp.sum(jnp.exp(scores - row_max), axis=-1, keepdims=True))
    attn_probs = jnp.exp(scores - log_total)
    mixed = jnp.einsum(
        "bhlm,bmhe->blhe",
        attn_probs.astype(jnp.bfloat16),
        values_low,
        preferred_element_type=jnp.float32,
    )
    mixed = mixed.astype(jnp.bfloat16).reshape(batch_size, seq_len, -1)
    partial_attn = jnp.einsum("bld,de->ble", mixed, out_mat, preferred_element_type=jnp.float32)
    middle = stream + lax.psum(partial_attn, "mp") + out_shift
    normed_two, inverse_two = norm_parts(middle)
    lowered_two = (normed_two * gain_two + shift_two).astype(jnp.bfloat16)
    preact = (
        jnp.einsum("bld,df->blf", lowered_two, up_mat, preferred_element_type=jnp.float32)
        + up_shift
    )
    gelu_out = jax.nn.gelu(preact, approximate=False).astype(jnp.bfloat16)
    partial_mlp = jnp.einsum("blf,fd->bld", gelu_out, down_mat, preferred_element_type=jnp.float32)
    result = (middle + lax.psum(partial_mlp, "mp") + down_shift) * rows
    return (result, (stream, middle, queries, keys_low, values_low, log_total, mixed, preact))


def backward(seed, saved, params, shapes):
    (
        gain_one,
        shift_one,
        qkv_mat,
        qv_shift,
        out_mat,
        out_shift,
        gain_two,
        shift_two,
        up_mat,
        up_shift,
        down_mat,
        down_shift,
    ) = params
    stream, middle, queries, keys_low, values_low, log_total, mixed, preact = saved
    batch_size, seq_len, head_count, head_dim = queries.shape
    scale = HD ** (-0.5)
    normed, inverse = norm_parts(stream)
    lowered = (normed * gain_one + shift_one).astype(jnp.bfloat16)
    normed_two, inverse_two = norm_parts(middle)
    lowered_two = (normed_two * gain_two + shift_two).astype(jnp.bfloat16)
    gelu_out = jax.nn.gelu(preact, approximate=False).astype(jnp.bfloat16)
    grad_mlp = seed.astype(jnp.bfloat16)
    grad_down_shift = jnp.sum(grad_mlp.astype(jnp.float32), axis=(0, 1))
    grad_down_mat = jnp.einsum(
        "blf,bld->fd", gelu_out, grad_mlp, preferred_element_type=jnp.float32
    )
    grad_gelu = jnp.einsum("bld,fd->blf", grad_mlp, down_mat, preferred_element_type=jnp.float32)
    grad_pre = (grad_gelu * gelu_slope(preact)).astype(jnp.bfloat16)
    grad_up_shift = jnp.sum(grad_pre.astype(jnp.float32), axis=(0, 1))
    grad_up_mat = jnp.einsum(
        "bld,blf->df", lowered_two, grad_pre, preferred_element_type=jnp.float32
    )
    grad_low_two = lax.psum(
        jnp.einsum("blf,df->bld", grad_pre, up_mat, preferred_element_type=jnp.float32), "mp"
    )
    grad_gain_two = jnp.sum(grad_low_two * normed_two, axis=(0, 1))
    grad_shift_two = jnp.sum(grad_low_two, axis=(0, 1))
    grad_middle = seed + norm_back(grad_low_two * gain_two, normed_two, inverse_two)
    grad_attn = grad_middle.astype(jnp.bfloat16)
    grad_out_shift = jnp.sum(grad_attn.astype(jnp.float32), axis=(0, 1))
    grad_out_mat = jnp.einsum("bld,ble->de", mixed, grad_attn, preferred_element_type=jnp.float32)
    grad_mixed = jnp.einsum("ble,de->bld", grad_attn, out_mat, preferred_element_type=jnp.float32)
    grad_mixed = grad_mixed.astype(jnp.bfloat16).reshape(batch_size, seq_len, head_count, head_dim)
    scores = (
        jnp.einsum("blhe,bmhe->bhlm", queries, keys_low, preferred_element_type=jnp.float32) * scale
    )
    attn_probs = jnp.exp(scores - log_total)
    grad_probs = jnp.einsum(
        "blhe,bmhe->bhlm", grad_mixed, values_low, preferred_element_type=jnp.float32
    )
    grad_values = jnp.einsum(
        "bhlm,blhe->bmhe",
        attn_probs.astype(jnp.bfloat16),
        grad_mixed,
        preferred_element_type=jnp.float32,
    ).astype(jnp.bfloat16)
    grad_scores = (
        attn_probs * (grad_probs - jnp.sum(attn_probs * grad_probs, axis=-1, keepdims=True))
    ).astype(jnp.bfloat16)
    grad_queries = (
        jnp.einsum("bhlm,bmhe->blhe", grad_scores, keys_low, preferred_element_type=jnp.float32)
        * scale
    ).astype(jnp.bfloat16)
    grad_keys = (
        jnp.einsum("bhlm,blhe->bmhe", grad_scores, queries, preferred_element_type=jnp.float32)
        * scale
    ).astype(jnp.bfloat16)
    grad_proj = jnp.stack([grad_queries, grad_keys, grad_values]).reshape(
        3, batch_size, seq_len, -1
    )
    grad_qv_shift = jnp.stack(
        [
            jnp.sum(grad_queries.astype(jnp.float32), axis=(0, 1)),
            jnp.sum(grad_values.astype(jnp.float32), axis=(0, 1)),
        ]
    )
    grad_qkv_mat = jnp.einsum(
        "bld,cble->cde", lowered, grad_proj, preferred_element_type=jnp.float32
    )
    grad_lowered = lax.psum(
        jnp.einsum("cble,cde->bld", grad_proj, qkv_mat, preferred_element_type=jnp.float32), "mp"
    )
    grad_gain_one = jnp.sum(grad_lowered * normed, axis=(0, 1))
    grad_shift_one = jnp.sum(grad_lowered, axis=(0, 1))
    grad_stream = grad_middle + norm_back(grad_lowered * gain_one, normed, inverse)
    terms = [
        grad_gain_one,
        grad_shift_one,
        grad_qkv_mat,
        grad_qv_shift,
        grad_out_mat,
        grad_out_shift,
        grad_gain_two,
        grad_shift_two,
        grad_up_mat,
        grad_up_shift,
        grad_down_mat,
        grad_down_shift,
    ]
    return (grad_stream, [term.reshape(shape) for term, shape in zip(terms, shapes)])


def local(
    images,
    cotangent,
    live_count,
    ln1_gain,
    ln1_bias,
    qkv_weight,
    qv_bias,
    out_weight,
    out_bias,
    ln2_gain,
    ln2_bias,
    up_weight,
    up_bias,
    down_weight,
    down_bias,
):
    first_section = lax.axis_index("section") == 0
    micro_count = images.shape[0]
    slot_count = images.shape[1]
    slot_ids = jnp.arange(slot_count)
    gathered = (
        lax.all_gather(ln1_gain, "dp", axis=1, tiled=True),
        lax.all_gather(ln1_bias, "dp", axis=1, tiled=True),
        lax.all_gather(qkv_weight, "dp", axis=2, tiled=True),
        lax.all_gather(qv_bias, "dp", axis=3, tiled=True),
        lax.all_gather(out_weight, "dp", axis=2, tiled=True),
        lax.all_gather(out_bias, "dp", axis=1, tiled=True),
        lax.all_gather(ln2_gain, "dp", axis=1, tiled=True),
        lax.all_gather(ln2_bias, "dp", axis=1, tiled=True),
        lax.all_gather(up_weight, "dp", axis=1, tiled=True),
        lax.all_gather(up_bias, "dp", axis=2, tiled=True),
        lax.all_gather(down_weight, "dp", axis=2, tiled=True),
        lax.all_gather(down_bias, "dp", axis=1, tiled=True),
    )
    params = unpack_weights(gathered)
    shapes = [piece.shape for piece in gathered]

    def row_mask(batch_index, valid):
        alive = jnp.logical_and(slot_ids < live_count[batch_index, 0], valid)
        return alive.astype(jnp.float32).reshape(slot_count, 1, 1)

    def choose(for_first, for_second):
        return jnp.where(first_section, for_first, for_second)

    incoming = jnp.zeros(images.shape[1:], jnp.bfloat16)
    outputs = []
    kept = []
    for moment in range(micro_count + 1):
        own = images[min(moment, micro_count - 1)]
        source = choose(own, incoming).astype(jnp.float32)
        rows = choose(
            row_mask(min(moment, micro_count - 1), moment < micro_count),
            row_mask(max(moment - 1, 0), moment >= 1),
        )
        result, saved = forward(source, params, rows)
        result = result.astype(jnp.bfloat16)
        outputs.append(result)
        kept.append(saved)
        if moment < micro_count:
            incoming = from_behind(result, "section", 1)
    activations = jnp.stack(
        [choose(outputs[index], outputs[index + 1]) for index in range(micro_count)]
    )
    regathered = (
        lax.all_gather(ln1_gain, "dp", axis=1, tiled=True),
        lax.all_gather(ln1_bias, "dp", axis=1, tiled=True),
        lax.all_gather(qkv_weight, "dp", axis=2, tiled=True),
        lax.all_gather(qv_bias, "dp", axis=3, tiled=True),
        lax.all_gather(out_weight, "dp", axis=2, tiled=True),
        lax.all_gather(out_bias, "dp", axis=1, tiled=True),
        lax.all_gather(ln2_gain, "dp", axis=1, tiled=True),
        lax.all_gather(ln2_bias, "dp", axis=1, tiled=True),
        lax.all_gather(up_weight, "dp", axis=1, tiled=True),
        lax.all_gather(up_bias, "dp", axis=2, tiled=True),
        lax.all_gather(down_weight, "dp", axis=2, tiled=True),
        lax.all_gather(down_bias, "dp", axis=1, tiled=True),
    )
    params = unpack_weights(regathered)
    owned = [
        jnp.zeros(piece.shape, jnp.float32)
        for piece in (
            ln1_gain,
            ln1_bias,
            qkv_weight,
            qv_bias,
            out_weight,
            out_bias,
            ln2_gain,
            ln2_bias,
            up_weight,
            up_bias,
            down_weight,
            down_bias,
        )
    ]
    totals = [jnp.zeros(shape, jnp.float32) for shape in shapes]
    incoming = jnp.zeros(images.shape[1:], jnp.bfloat16)
    returned = []
    for moment in range(micro_count + 1):
        later_index = min(moment, micro_count - 1)
        rows = choose(
            row_mask(max(moment - 1, 0), moment >= 1), row_mask(later_index, moment < micro_count)
        )
        seed = choose(incoming, cotangent[later_index]).astype(jnp.float32) * rows
        saved = jax.tree.map(choose, kept[max(moment - 1, 0)], kept[min(moment + 1, micro_count)])
        grad_stream, terms = backward(seed, saved, params, shapes)
        grad_low = grad_stream.astype(jnp.bfloat16)
        returned.append(grad_low)
        if moment < micro_count:
            incoming = from_behind(grad_low, "section", -1)
        totals = [first_part + second_part for first_part, second_part in zip(totals, terms)]
    owned = (
        lax.psum_scatter(totals[0], "dp", scatter_dimension=1, tiled=True),
        lax.psum_scatter(totals[1], "dp", scatter_dimension=1, tiled=True),
        lax.psum_scatter(totals[2], "dp", scatter_dimension=2, tiled=True),
        lax.psum_scatter(totals[3], "dp", scatter_dimension=3, tiled=True),
        lax.psum_scatter(totals[4], "dp", scatter_dimension=2, tiled=True),
        lax.psum_scatter(totals[5], "dp", scatter_dimension=1, tiled=True),
        lax.psum_scatter(totals[6], "dp", scatter_dimension=1, tiled=True),
        lax.psum_scatter(totals[7], "dp", scatter_dimension=1, tiled=True),
        lax.psum_scatter(totals[8], "dp", scatter_dimension=1, tiled=True),
        lax.psum_scatter(totals[9], "dp", scatter_dimension=2, tiled=True),
        lax.psum_scatter(totals[10], "dp", scatter_dimension=2, tiled=True),
        lax.psum_scatter(totals[11], "dp", scatter_dimension=1, tiled=True),
    )
    input_grads = jnp.stack(
        [choose(returned[index + 1], returned[index]) for index in range(micro_count)]
    )
    return (
        activations[None],
        input_grads[None],
        owned[0],
        owned[1],
        owned[2],
        owned[3],
        owned[4],
        owned[5],
        owned[6],
        owned[7],
        owned[8],
        owned[9],
        owned[10],
        owned[11],
    )


def solution(mesh):
    return jax.shard_map(
        local,
        mesh=mesh,
        in_specs=(
            P(None, "dp", None, None),
            P(None, "dp", None, None),
            P(None, "dp"),
            P("section", "dp"),
            P("section", "dp"),
            P("section", None, "dp", "mp"),
            P("section", None, "mp", "dp"),
            P("section", "mp", "dp"),
            P("section", "dp"),
            P("section", "dp"),
            P("section", "dp"),
            P("section", "dp", "mp"),
            P("section", "mp", "dp"),
            P("section", "mp", "dp"),
            P("section", "dp"),
        ),
        out_specs=(
            P("section", None, "dp", None, None),
            P("section", None, "dp", None, None),
            P("section", "dp"),
            P("section", "dp"),
            P("section", None, "dp", "mp"),
            P("section", None, "mp", "dp"),
            P("section", "mp", "dp"),
            P("section", "dp"),
            P("section", "dp"),
            P("section", "dp"),
            P("section", "dp", "mp"),
            P("section", "mp", "dp"),
            P("section", "mp", "dp"),
            P("section", "dp"),
        ),
        check_vma=False,
    )
```

profile of v0, /device:TPU:0, one launch (start us, length us, event | category | flops | bytes accessed | tf_op | source)
XLA Modules:
  0.0 2072.1 jit_solution(12529934385351478101)
XLA Ops:
  8.7 22.7 %all_gather.45 = bf16[1,1024]{1,0:T(2,128)(2,1)S(1)} all-gather(bf16[1,128]{1,0:T(2,128)(2,1)} %param.19), channel_id=1, replica_groups=mesh['section'=2,'dp'=8,'mp'=2] {'dp'}, dimensions={1}, use_global_device_ids=true | all-gather | bytes 2304 | tf_op jit(solution)/shard_map/all_gather | solution.py:234
  31.4 16.6 all_gather.44
  51.5 31.1 %all_gather.47 = bf16[1,2,8,64]{2,1,0,3:T(2,128)(2,1)S(1)} all-gather(bf16[1,2,8,8]{2,1,0,3:T(2,128)(2,1)S(1)} %copy.267), channel_id=1, replica_groups=mesh['section'=2,'dp'=8,'mp'=2] {'dp'}, dimensions={3}, use_global_device_ids=true | all-gather | bytes 2304 | tf_op jit(solution)/shard_map/all_gather | solution.py:236
  96.0 17.5 all-gather.7.cloned.1.call-done
  118.0 18.4 all_gather.49
  136.4 30.5 %all_gather.53 = bf16[1,8,256]{1,0,2:T(2,128)(2,1)S(1)} all-gather(bf16[1,8,32]{1,0,2:T(2,128)(2,1)S(1)} %copy.274), channel_id=1, replica_groups=mesh['section'=2,'dp'=8,'mp'=2] {'dp'}, dimensions={2}, use_global_device_ids=true | all-gather | bytes 4608 | tf_op jit(solution)/shard_map/all_gather | solution.py:242
  167.1 16.3 all_gather.51
  183.4 19.0 all_gather.50
  205.8 37.9 %all-gather.9.cloned.1.call-done = bf16[1,1024,2048]{2,1,0:T(8,128)(2,1)} async-done(((bf16[1,128,2048]{2,1,0:T(8,128)(2,1)}), bf16[1,1024,2048]{2,1,0:T(8,128)(2,1)}) %all-gather.9.cloned.1.call-update) | async-done | bytes 4194320 | tf_op jit(solution)/shard_map/all_gather | solution.py:241
  243.7 7.5 fusion.499
  251.1 67.6 %all-gather.11.cloned.1.call-done = bf16[1,2048,1024]{2,1,0:T(8,128)(2,1)} async-done(((bf16[1,2048,128]{2,1,0:T(8,128)(2,1)}), bf16[1,2048,1024]{2,1,0:T(8,128)(2,1)}) %all-gather.11.cloned.1.call-update) | async-done | bytes 4194320 | tf_op jit(solution)/shard_map/all_gather | solution.py:243
  318.8 13.0 fusion.13
  331.9 17.9 all_gather.55
  351.1 32.1 %all-reduce.16.cloned.1.call-done = f32[2,197,1024]{2,1,0:T(8,128)} async-done(((f32[2,197,1024]{2,1,0:T(8,128)}), f32[2,197,1024]{2,1,0:T(8,128)}) %all-reduce.16.cloned.1.call-update) | async-done | bytes 1613840 | tf_op jit(solution)/shard_map/psum | solution.py:103
  415.6 45.9 %all-reduce.18.cloned.1.call-done = f32[2,197,1024]{2,1,0:T(8,128)} async-done(((f32[2,197,1024]{2,1,0:T(8,128)}), f32[2,197,1024]{2,1,0:T(8,128)}) %all-reduce.18.cloned.1.call-update) | async-done | bytes 1613840 | tf_op jit(solution)/shard_map/psum | solution.py:94
  468.8 10.3 fusion.496
  489.9 13.2 fusion.11
  503.1 37.9 %all-reduce.22.cloned.1.call-done = f32[2,197,1024]{2,1,0:T(8,128)} async-done(((f32[2,197,1024]{2,1,0:T(8,128)}), f32[2,197,1024]{2,1,0:T(8,128)}) %all-reduce.22.cloned.1.call-update) | async-done | bytes 1613840 | tf_op jit(solution)/shard_map/psum | solution.py:141
  567.6 4.7 fusion.389
  573.7 87.5 %all-reduce.32.cloned.1.call-done = (f32[2,197,1024]{2,1,0:T(8,128)}, f32[2,197,1024]{2,1,0:T(8,128)}) async-done(((f32[2,197,1024]{2,1,0:T(8,128)}, f32[2,197,1024]{2,1,0:T(8,128)}), (f32[2,197,1024]{2,1,0:T(8,128)}, f32[2,197,1024]{2,1,0:T(8,128)})) %all-reduce.32.cloned.1.call-update) | async-done | bytes 3227664 | tf_op jit(solution)/shard_map/psum | solution.py:103
  698.7 48.7 %all-reduce.20.cloned.1.call-done = f32[2,197,1024]{2,1,0:T(8,128)} async-done(((f32[2,197,1024]{2,1,0:T(8,128)}), f32[2,197,1024]{2,1,0:T(8,128)}) %all-reduce.20.cloned.1.call-update) | async-done | bytes 1613840 | tf_op jit(solution)/shard_map/psum | solution.py:94
  747.5 5.6 fusion.746
  761.7 11.2 fusion.497
  774.0 5.3 convert_reduce_fusion.1
  788.6 48.5 %all-reduce.24.cloned.1.call-done = f32[2,197,1024]{2,1,0:T(8,128)} async-done(((f32[2,197,1024]{2,1,0:T(8,128)}), f32[2,197,1024]{2,1,0:T(8,128)}) %all-reduce.24.cloned.1.call-update) | async-done | bytes 1613840 | tf_op jit(solution)/shard_map/psum | solution.py:141
  865.1 4.9 fusion.392
  870.8 52.4 %all-reduce.26.cloned.1.call-done = f32[2,197,1024]{2,1,0:T(8,128)} async-done(((f32[2,197,1024]{2,1,0:T(8,128)}), f32[2,197,1024]{2,1,0:T(8,128)}) %all-reduce.26.cloned.1.call-update) | async-done | bytes 1613840 | tf_op jit(solution)/shard_map/psum | solution.py:188
  945.4 13.2 fusion.9
  958.6 40.3 %all-reduce.28.cloned.1.call-done = f32[2,197,1024]{2,1,0:T(8,128)} async-done(((f32[2,197,1024]{2,1,0:T(8,128)}), f32[2,197,1024]{2,1,0:T(8,128)}) %all-reduce.28.cloned.1.call-update) | async-done | bytes 1613840 | tf_op jit(solution)/shard_map/psum | solution.py:141
  1027.7 6.8 fusion.433
  1034.6 4.9 fusion.436
  1045.1 70.7 %all-reduce.30.cloned.1.call-done = (f32[2,197,1024]{2,1,0:T(8,128)}, f32[2,197,1024]{2,1,0:T(8,128)}) async-done(((f32[2,197,1024]{2,1,0:T(8,128)}, f32[2,197,1024]{2,1,0:T(8,128)}), (f32[2,197,1024]{2,1,0:T(8,128)}, f32[2,197,1024]{2,1,0:T(8,128)})) %all-reduce.30.cloned.1.call-update) | async-done | bytes 3227664 | tf_op jit(solution)/shard_map/psum | solution.py:103
  1120.9 9.5 fusion.2
  1150.1 6.1 fusion.1
  1157.5 11.2 fusion.148
  1168.7 9.1 fusion.146
  1177.8 10.9 fusion
  1192.7 52.9 %reduce-scatter.45.cloned.1.call-done = f32[32,8]{1,0:T(8,128)} async-done(((f32[256,8]{1,0:T(8,128)}), f32[32,8]{1,0:T(8,128)}) %reduce-scatter.45.cloned.1.call-update) | async-done | bytes 1040
  1247.1 20.1 all-reduce
  1267.9 42.7 %reduce-scatter.39.cloned.1.call-done = f32[128,1]{1,0:T(8,128)} async-done(((f32[1024,1]{1,0:T(8,128)}), f32[128,1]{1,0:T(8,128)}) %reduce-scatter.39.cloned.1.call-update) | async-done | bytes 528
  1312.0 63.4 %reduce-scatter.41.cloned.1.call-done = f32[128,1]{1,0:T(8,128)} async-done(((f32[1024,1]{1,0:T(8,128)}), f32[128,1]{1,0:T(8,128)}) %reduce-scatter.41.cloned.1.call-update) | async-done | bytes 528
  1376.8 63.5 %reduce-scatter.43.cloned.1.call-done = f32[128,1]{1,0:T(8,128)} async-done(((f32[1024,1]{1,0:T(8,128)}), f32[128,1]{1,0:T(8,128)}) %reduce-scatter.43.cloned.1.call-update) | async-done | bytes 528
  1452.7 52.4 %reduce-scatter.35.cloned.1.call-done = f32[128,1]{1,0:T(8,128)} async-done(((f32[1024,1]{1,0:T(8,128)}), f32[128,1]{1,0:T(8,128)}) %reduce-scatter.35.cloned.1.call-update) | async-done | bytes 528
  1506.6 63.6 %reduce-scatter.37.cloned.1.call-done = f32[128,1]{1,0:T(8,128)} async-done(((f32[1024,1]{1,0:T(8,128)}), f32[128,1]{1,0:T(8,128)}) %reduce-scatter.37.cloned.1.call-update) | async-done | bytes 528
  1571.6 119.7 %reduce-scatter.27.cloned.1.call-done = f32[1,3,128,512]{2,3,1,0:T(8,128)} async-done(((f32[1,3,1024,512]{2,3,1,0:T(8,128)}), f32[1,3,128,512]{2,3,1,0:T(8,128)}) %reduce-scatter.27.cloned.1.call-update) | async-done | bytes 786448 | tf_op jit(solution)/shard_map/reduce_scatter | solution.py:326
  1693.5 70.1 %reduce-scatter.29.cloned.1.call-done = f32[1,512,128]{2,1,0:T(8,128)} async-done(((f32[1,512,1024]{2,1,0:T(8,128)}), f32[1,512,128]{2,1,0:T(8,128)}) %reduce-scatter.29.cloned.1.call-update) | async-done | bytes 262160 | tf_op jit(solution)/shard_map/reduce_scatter | solution.py:328
  1763.6 150.6 %reduce-scatter.31.cloned.1.call-done = f32[1,128,2048]{2,1,0:T(8,128)} async-done(((f32[1,1024,2048]{2,1,0:T(8,128)}), f32[1,128,2048]{2,1,0:T(8,128)}) %reduce-scatter.31.cloned.1.call-update) | async-done | bytes 1048592 | tf_op jit(solution)/shard_map/reduce_scatter | solution.py:332
  1914.2 151.2 %reduce-scatter.33.cloned.1.call-done = f32[1,2048,128]{2,1,0:T(8,128)} async-done(((f32[1,2048,1024]{2,1,0:T(8,128)}), f32[1,2048,128]{2,1,0:T(8,128)}) %reduce-scatter.33.cloned.1.call-update) | async-done | bytes 1048592 | tf_op jit(solution)/shard_map/reduce_scatter | solution.py:334
  (658 shorter events, 297.8 us)
Async XLA Ops:
  7.2 75.6 %all-gather.5.cloned.1.call-start = ((), (), s32[]{:S(2)}) async-start(), calls=%async_computation.11 | async-start | bytes 3538944 | tf_op jit(solution)/shard_map/all_gather | solution.py:235
  7.9 105.6 %all-gather.7.cloned.1.call-start = ((), (), s32[]{:S(2)}) async-start(), calls=%async_computation.12 | async-start | bytes 1179648 | tf_op jit(solution)/shard_map/all_gather | solution.py:237
  8.7 193.7 %all-reduce.14.cloned.1.call-start = ((), (), s32[]{:S(2)}) async-start(), calls=%async_computation.13 | async-start | bytes 3276800 | tf_op jit(solution)/shard_map/psum | solution.py:94
  31.4 360.5 %copy-start.150 = (f32[1,1024]{1,0:T(1,128)}, f32[1,1024]{1,0:T(1,128)S(1)}, u32[]{:S(2)}) copy-start(f32[1,1024]{1,0:T(1,128)S(1)} %convert_element_type.566) | copy-start | bytes 12292
  50.5 339.5 %copy-start.62 = (bf16[1,2,197,1024]{3,1,2,0:T(2,128)(2,1)}, bf16[1,2,197,1024]{3,1,2,0:T(2,128)(2,1)S(1)}, u32[]{:S(2)}) copy-start(bf16[1,2,197,1024]{3,1,2,0:T(2,128)(2,1)S(1)} %get-tuple-element.178) | copy-start | bytes 2420740
  82.7 314.5 %copy-start.102 = (f32[8,64]{1,0:T(8,128)}, f32[8,64]{1,0:T(8,128)S(1)}, u32[]{:S(2)}) copy-start(f32[8,64]{1,0:T(8,128)S(1)} %copy.268) | copy-start | bytes 6148
  82.8 317.8 %copy-start.100 = (f32[8,64]{1,0:T(8,128)}, f32[8,64]{1,0:T(8,128)S(1)}, u32[]{:S(2)}) copy-start(f32[8,64]{1,0:T(8,128)S(1)} %copy.270) | copy-start | bytes 6148
  91.3 469.7 %copy-start.23 = (bf16[1,2,197,512]{2,3,1,0:T(8,128)(2,1)}, bf16[1,2,197,512]{2,3,1,0:T(8,128)(2,1)S(1)}, u32[]{:S(2)}) copy-start(bf16[1,2,197,512]{2,3,1,0:T(8,128)(2,1)S(1)} %copy.271) | copy-start | bytes 1210372
  96.0 71.1 %copy-start.170 = (bf16[1,128]{1,0:T(2,128)(2,1)S(1)}, bf16[1,128]{1,0:T(2,128)(2,1)}, u32[]{:S(2)}) copy-start(bf16[1,128]{1,0:T(2,128)(2,1)} %param.25) | copy-start | bytes 772
  96.0 87.4 %copy-start.171 = (bf16[1,128]{1,0:T(2,128)(2,1)S(1)}, bf16[1,128]{1,0:T(2,128)(2,1)}, u32[]{:S(2)}) copy-start(bf16[1,128]{1,0:T(2,128)(2,1)} %param.24) | copy-start | bytes 772
  116.7 127.0 %all-gather.9.cloned.1.call-start = ((), (), s32[]{:S(2)}) async-start(), calls=%async_computation.14 | async-start | bytes 4718592 | tf_op jit(solution)/shard_map/all_gather | solution.py:241
  117.3 201.5 %all-gather.11.cloned.1.call-start = ((), (), s32[]{:S(2)}) async-start(), calls=%async_computation.15 | async-start | bytes 4718592 | tf_op jit(solution)/shard_map/all_gather | solution.py:243
  117.9 265.2 %all-reduce.16.cloned.1.call-start = ((), (), s32[]{:S(2)}) async-start(), calls=%async_computation.16 | async-start | bytes 3276800 | tf_op jit(solution)/shard_map/psum | solution.py:103
  167.1 301.7 %copy-start.158 = (f32[1,2,8,128]{3,1,2,0:T(2,128)}, f32[1,2,8,128]{3,1,2,0:T(2,128)S(1)}, u32[]{:S(2)}) copy-start(f32[1,2,8,128]{3,1,2,0:T(2,128)S(1)} %copy.371) | copy-start | bytes 24580
  183.4 285.4 %copy-start.125 = (f32[1,1024]{1,0:T(1,128)}, f32[1,1024]{1,0:T(1,128)S(1)}, u32[]{:S(2)}) copy-start(f32[1,1024]{1,0:T(1,128)S(1)} %convert_element_type.569) | copy-start | bytes 12292
  331.8 129.6 %all-reduce.18.cloned.1.call-start = ((), (), s32[]{:S(2)}) async-start(), calls=%async_computation.17 | async-start | bytes 3276800 | tf_op jit(solution)/shard_map/psum | solution.py:94
  386.4 3.6 collective-permute-start
  408.3 132.7 %all-reduce.22.cloned.1.call-start = ((), (), s32[]{:S(2)}) async-start(), calls=%async_computation.19 | async-start | bytes 3276800 | tf_op jit(solution)/shard_map/psum | solution.py:141
  409.6 134.9 %copy-start.167 = (f32[2]{0:T(128)}, f32[2]{0:T(128)S(1)}, u32[]{:S(2)}) copy-start(f32[2]{0:T(128)S(1)} %broadcast_select_fusion.29) | copy-start | bytes 28
  487.9 173.3 %all-reduce.32.cloned.1.call-start = ((), (), s32[]{:S(2)}) async-start(), calls=%async_computation.35 | async-start | bytes 6553600 | tf_op jit(solution)/shard_map/psum | solution.py:103
  572.3 88.9 %copy-start.105 = (f32[1,1024]{1,0:T(1,128)S(1)}, f32[1,1024]{1,0:T(1,128)}, u32[]{:S(2)}) copy-start(f32[1,1024]{1,0:T(1,128)} %copy-done.104) | copy-start | bytes 12292
  572.4 175.1 %all-reduce.20.cloned.1.call-start = ((), (), s32[]{:S(2)}) async-start(), calls=%async_computation.18 | async-start | bytes 3276800 | tf_op jit(solution)/shard_map/psum | solution.py:94
  665.8 3.3 collective-permute-start.1
  694.4 142.8 %all-reduce.24.cloned.1.call-start = ((), (), s32[]{:S(2)}) async-start(), calls=%async_computation.20 | async-start | bytes 3276800 | tf_op jit(solution)/shard_map/psum | solution.py:141
  759.6 13.3 collective-permute-start.2
  783.7 139.5 %all-reduce.26.cloned.1.call-start = ((), (), s32[]{:S(2)}) async-start(), calls=%async_computation.21 | async-start | bytes 3276800 | tf_op jit(solution)/shard_map/psum | solution.py:188
  870.1 128.9 %all-reduce.28.cloned.1.call-start = ((), (), s32[]{:S(2)}) async-start(), calls=%async_computation.22 | async-start | bytes 3276800 | tf_op jit(solution)/shard_map/psum | solution.py:141
  930.7 4.3 collective-permute-start.3
  945.0 170.9 %all-reduce.30.cloned.1.call-start = ((), (), s32[]{:S(2)}) async-start(), calls=%async_computation.34 | async-start | bytes 6553600 | tf_op jit(solution)/shard_map/psum | solution.py:103
  1027.0 164.3 %reduce-scatter.47.cloned.1.call-start = ((), (), s32[]{:S(2)}) async-start(), calls=%async_computation.33 | async-start | bytes 589824
  1039.6 76.3 %copy-start.108 = (f32[2,197]{1,0:T(2,128)S(1)}, f32[2,197]{1,0:T(2,128)}, u32[]{:S(2)}) copy-start(f32[2,197]{1,0:T(2,128)} %copy-done.107) | copy-start | bytes 4732
  1040.7 205.0 %reduce-scatter.45.cloned.1.call-start = ((), (), s32[]{:S(2)}) async-start(), calls=%async_computation.32 | async-start | bytes 147456
  1041.6 76.6 %copy-start.135 = (f32[1024]{0:T(1024)S(1)}, f32[1024]{0:T(1024)}, u32[]{:S(2)}) copy-start(f32[1024]{0:T(1024)} %get-tuple-element.98) | copy-start | bytes 12292
  1041.6 76.6 %copy-start.147 = (f32[1024]{0:T(1024)S(1)}, f32[1024]{0:T(1024)}, u32[]{:S(2)}) copy-start(f32[1024]{0:T(1024)} %get-tuple-element.100) | copy-start | bytes 12292
  1041.6 269.0 %reduce-scatter.39.cloned.1.call-start = ((), (), s32[]{:S(2)}) async-start(), calls=%async_computation.29 | async-start | bytes 589824
  1042.8 76.6 %copy-start.134 = (f32[1024]{0:T(1024)S(1)}, f32[1024]{0:T(1024)}, u32[]{:S(2)}) copy-start(f32[1024]{0:T(1024)} %get-tuple-element.111) | copy-start | bytes 12292
  1042.8 76.6 %copy-start.146 = (f32[1024]{0:T(1024)S(1)}, f32[1024]{0:T(1024)}, u32[]{:S(2)}) copy-start(f32[1024]{0:T(1024)} %get-tuple-element.112) | copy-start | bytes 12292
  1042.8 332.6 %reduce-scatter.41.cloned.1.call-start = ((), (), s32[]{:S(2)}) async-start(), calls=%async_computation.30 | async-start | bytes 589824
  1043.9 76.9 %copy-start.87 = (bf16[1,2,197,512]{3,2,0,1:T(8,128)(2,1)S(1)}, bf16[1,2,197,512]{3,2,0,1:T(8,128)(2,1)}, u32[]{:S(2)}) copy-start(bf16[1,2,197,512]{3,2,0,1:T(8,128)(2,1)} %copy.317) | copy-start | bytes 1210372
  1044.0 396.4 %reduce-scatter.43.cloned.1.call-start = ((), (), s32[]{:S(2)}) async-start(), calls=%async_computation.31 | async-start | bytes 589824
  1045.1 460.1 %reduce-scatter.35.cloned.1.call-start = ((), (), s32[]{:S(2)}) async-start(), calls=%async_computation.27 | async-start | bytes 589824
  1119.3 450.9 %reduce-scatter.37.cloned.1.call-start = ((), (), s32[]{:S(2)}) async-start(), calls=%async_computation.28 | async-start | bytes 589824
  1120.4 570.8 %reduce-scatter.27.cloned.1.call-start = ((), (), s32[]{:S(2)}) async-start(), calls=%async_computation.23 | async-start | bytes 7077888 | tf_op jit(solution)/shard_map/reduce_scatter | solution.py:326
  1130.4 633.2 %reduce-scatter.29.cloned.1.call-start = ((), (), s32[]{:S(2)}) async-start(), calls=%async_computation.24 | async-start | bytes 2359296 | tf_op jit(solution)/shard_map/reduce_scatter | solution.py:328
  1142.7 771.4 %reduce-scatter.31.cloned.1.call-start = ((), (), s32[]{:S(2)}) async-start(), calls=%async_computation.25 | async-start | bytes 9437184 | tf_op jit(solution)/shard_map/reduce_scatter | solution.py:332
  1156.2 909.1 %reduce-scatter.33.cloned.1.call-start = ((), (), s32[]{:S(2)}) async-start(), calls=%async_computation.26 | async-start | bytes 9437184 | tf_op jit(solution)/shard_map/reduce_scatter | solution.py:334
  1188.8 253.0 %copy-start.56 = (bf16[2,197,1024]{2,1,0:T(8,128)(2,1)S(1)}, bf16[2,197,1024]{2,1,0:T(8,128)(2,1)}, u32[]{:S(2)}) copy-start(bf16[2,197,1024]{2,1,0:T(8,128)(2,1)} %copy-done.55) | copy-start | bytes 2420740
  1188.8 253.0 %copy-start.106 = (f32[1,1024]{1,0:T(1,128)S(1)}, f32[1,1024]{1,0:T(1,128)}, u32[]{:S(2)}) copy-start(f32[1,1024]{1,0:T(1,128)} %copy-done.104) | copy-start | bytes 12292
  (174 other events, 1696.9 us)
Sparse Core Ops, SparseCore 0:
  10.2 63.1 all-gather.4
  75.4 38.0 all-gather.6
  116.9 51.9 all-reduce.13
  170.9 72.7 all-gather.8
  245.6 73.1 all-gather.10
  331.9 51.1 all-reduce.15
  408.4 52.9 all-reduce.17
  488.0 52.9 all-reduce.21
  572.5 88.6 all-reduce.31
  694.5 52.9 all-reduce.19
  783.8 53.2 all-reduce.23
  870.2 52.9 all-reduce.25
  945.1 53.7 all-reduce.27
  1027.1 88.6 all-reduce.29
  1119.0 62.5 reduce-scatter.46
  1184.8 60.7 reduce-scatter.44
  1248.9 61.6 reduce-scatter.38
  1313.7 61.5 reduce-scatter.40
  1378.7 61.5 reduce-scatter.42
  1443.5 61.5 reduce-scatter.34
  1508.5 61.6 reduce-scatter.36
  1573.8 117.4 reduce-scatter.26
  1695.4 68.1 reduce-scatter.28
  1767.6 146.4 reduce-scatter.30
  1918.4 146.9 reduce-scatter.32
where the time goes:
time: 2080 us; the launch traced here: 2070 us
  waiting for transfers between devices  1420 us (68%)
  matrix products  240 us (12%)
  blocking collectives  193 us (9%)
  local copies, waits for them, and re-layouts  97.5 us (5%)
  other arithmetic  92.3 us (4%)
    unnamed x32, waiting for transfers between devices  341 us
    psum x3, waiting for transfers between devices, forward(): result = (middle + lax.psum(partial_mlp, 'mp') + down_shift) * rows  190 us
    reduce_scatter x1, waiting for transfers between devices, local(): lax.psum_scatter(totals[10], 'dp', scatter_dimension=2, tiled=True)  151 us
    reduce_scatter x1, waiting for transfers between devices, local(): lax.psum_scatter(totals[8], 'dp', scatter_dimension=1, tiled=True)  151 us
    psum x3, waiting for transfers between devices, backward(): lax.psum(jnp.einsum('blf,df->bld', grad_pre, up_mat, preferred_element_ty...  127 us
    reduce_scatter x1, waiting for transfers between devices, local(): lax.psum_scatter(totals[2], 'dp', scatter_dimension=2, tiled=True)  120 us
    psum x3, waiting for transfers between devices, forward(): middle = stream + lax.psum(partial_attn, 'mp') + out_shift  94.6 us
    reduce_scatter x1, waiting for transfers between devices, local(): lax.psum_scatter(totals[4], 'dp', scatter_dimension=2, tiled=True)  70.1 us
  transfers between devices with their start and end apart: 29, of which 25 were waited for; matrix products, arithmetic and copies ran while one was open for 10% of the time, Pallas kernels for 0%

commit v1 on v0

--- a/solution.py
+++ b/solution.py
@@ -9,6 +9,63 @@
 
 
 epsilon = 1e-06
+
+
+def gather_all(small, big):
+    flat = jnp.concatenate([piece.reshape(-1) for piece in small])
+    packed = lax.all_gather(flat, "dp", axis=0, tiled=False)
+    count = packed.shape[0]
+    whole, offset = [], 0
+    for piece, axis in zip(small, (1, 1, 3, 1, 1, 1, 2, 1)):
+        part = packed[:, offset : offset + piece.size].reshape((count,) + piece.shape)
+        offset += piece.size
+        part = jnp.moveaxis(part, 0, axis)
+        shape = list(piece.shape)
+        shape[axis] *= count
+        whole.append(part.reshape(shape))
+    qkv, out, up, down = (
+        lax.all_gather(piece, "dp", axis=axis, tiled=True) for piece, axis in zip(big, (2, 2, 1, 2))
+    )
+    return (
+        whole[0],
+        whole[1],
+        qkv,
+        whole[2],
+        out,
+        whole[3],
+        whole[4],
+        whole[5],
+        up,
+        whole[6],
+        down,
+        whole[7],
+    )
+
+
+def scatter_all(totals, shards):
+    small_at = (0, 1, 3, 5, 6, 7, 9, 11)
+    count = lax.axis_size("dp")
+    rows = []
+    for index, axis in zip(small_at, (1, 1, 3, 1, 1, 1, 2, 1)):
+        piece = totals[index]
+        shape = list(piece.shape)
+        shape[axis : axis + 1] = [count, shape[axis] // count]
+        rows.append(jnp.moveaxis(piece.reshape(shape), axis, 0).reshape(count, -1))
+    packed = lax.psum_scatter(jnp.concatenate(rows, axis=1), "dp", scatter_dimension=0, tiled=False)
+    owned, offset = [None] * 12, 0
+    for index in small_at:
+        size = shards[index].size
+        owned[index] = packed[offset : offset + size].reshape(shards[index].shape)
+        offset += size
+    for index, axis in zip((2, 4, 8, 10), (2, 2, 1, 2)):
+        owned[index] = lax.psum_scatter(
+            totals[index].astype(jnp.bfloat16), "dp", scatter_dimension=axis, tiled=True
+        ).astype(jnp.float32)
+    return owned
+
+
+def both_halves(partial):
+    return lax.psum(partial.astype(jnp.bfloat16), "mp").astype(jnp.float32)
 
 
 def from_behind(x, axis, by):
@@ -91,7 +148,7 @@
     )
     mixed = mixed.astype(jnp.bfloat16).reshape(batch_size, seq_len, -1)
     partial_attn = jnp.einsum("bld,de->ble", mixed, out_mat, preferred_element_type=jnp.float32)
-    middle = stream + lax.psum(partial_attn, "mp") + out_shift
+    middle = stream + both_halves(partial_attn) + out_shift
     normed_two, inverse_two = norm_parts(middle)
     lowered_two = (normed_two * gain_two + shift_two).astype(jnp.bfloat16)
     preact = (
@@ -100,7 +157,7 @@
     )
     gelu_out = jax.nn.gelu(preact, approximate=False).astype(jnp.bfloat16)
     partial_mlp = jnp.einsum("blf,fd->bld", gelu_out, down_mat, preferred_element_type=jnp.float32)
-    result = (middle + lax.psum(partial_mlp, "mp") + down_shift) * rows
+    result = (middle + both_halves(partial_mlp) + down_shift) * rows
     return (result, (stream, middle, queries, keys_low, values_low, log_total, mixed, preact))
 
 
@@ -138,8 +195,8 @@
     grad_up_mat = jnp.einsum(
         "bld,blf->df", lowered_two, grad_pre, preferred_element_type=jnp.float32
     )
-    grad_low_two = lax.psum(
-        jnp.einsum("blf,df->bld", grad_pre, up_mat, preferred_element_type=jnp.float32), "mp"
+    grad_low_two = both_halves(
+        jnp.einsum("blf,df->bld", grad_pre, up_mat, preferred_element_type=jnp.float32)
     )
     grad_gain_two = jnp.sum(grad_low_two * normed_two, axis=(0, 1))
     grad_shift_two = jnp.sum(grad_low_two, axis=(0, 1))
@@ -185,8 +242,8 @@
     grad_qkv_mat = jnp.einsum(
         "bld,cble->cde", lowered, grad_proj, preferred_element_type=jnp.float32
     )
-    grad_lowered = lax.psum(
-        jnp.einsum("cble,cde->bld", grad_proj, qkv_mat, preferred_element_type=jnp.float32), "mp"
+    grad_lowered = both_halves(
+        jnp.einsum("cble,cde->bld", grad_proj, qkv_mat, preferred_element_type=jnp.float32)
     )
     grad_gain_one = jnp.sum(grad_lowered * normed, axis=(0, 1))
     grad_shift_one = jnp.sum(grad_lowered, axis=(0, 1))
@@ -229,20 +286,8 @@
     micro_count = images.shape[0]
     slot_count = images.shape[1]
     slot_ids = jnp.arange(slot_count)
-    gathered = (
-        lax.all_gather(ln1_gain, "dp", axis=1, tiled=True),
-        lax.all_gather(ln1_bias, "dp", axis=1, tiled=True),
-        lax.all_gather(qkv_weight, "dp", axis=2, tiled=True),
-        lax.all_gather(qv_bias, "dp", axis=3, tiled=True),
-        lax.all_gather(out_weight, "dp", axis=2, tiled=True),
-        lax.all_gather(out_bias, "dp", axis=1, tiled=True),
-        lax.all_gather(ln2_gain, "dp", axis=1, tiled=True),
-        lax.all_gather(ln2_bias, "dp", axis=1, tiled=True),
-        lax.all_gather(up_weight, "dp", axis=1, tiled=True),
-        lax.all_gather(up_bias, "dp", axis=2, tiled=True),
-        lax.all_gather(down_weight, "dp", axis=2, tiled=True),
-        lax.all_gather(down_bias, "dp", axis=1, tiled=True),
-    )
+    small = (ln1_gain, ln1_bias, qv_bias, out_bias, ln2_gain, ln2_bias, up_bias, down_bias)
+    gathered = gather_all(small, (qkv_weight, out_weight, up_weight, down_weight))
     params = unpack_weights(gathered)
     shapes = [piece.shape for piece in gathered]
 
@@ -272,38 +317,6 @@
     activations = jnp.stack(
         [choose(outputs[index], outputs[index + 1]) for index in range(micro_count)]
     )
-    regathered = (
-        lax.all_gather(ln1_gain, "dp", axis=1, tiled=True),
-        lax.all_gather(ln1_bias, "dp", axis=1, tiled=True),
-        lax.all_gather(qkv_weight, "dp", axis=2, tiled=True),
-        lax.all_gather(qv_bias, "dp", axis=3, tiled=True),
-        lax.all_gather(out_weight, "dp", axis=2, tiled=True),
-        lax.all_gather(out_bias, "dp", axis=1, tiled=True),
-        lax.all_gather(ln2_gain, "dp", axis=1, tiled=True),
-        lax.all_gather(ln2_bias, "dp", axis=1, tiled=True),
-        lax.all_gather(up_weight, "dp", axis=1, tiled=True),
-        lax.all_gather(up_bias, "dp", axis=2, tiled=True),
-        lax.all_gather(down_weight, "dp", axis=2, tiled=True),
-        lax.all_gather(down_bias, "dp", axis=1, tiled=True),
-    )
-    params = unpack_weights(regathered)
-    owned = [
-        jnp.zeros(piece.shape, jnp.float32)
-        for piece in (
-            ln1_gain,
-            ln1_bias,
-            qkv_weight,
-            qv_bias,
-            out_weight,
-            out_bias,
-            ln2_gain,
-            ln2_bias,
-            up_weight,
-            up_bias,
-            down_weight,
-            down_bias,
-        )
-    ]
     totals = [jnp.zeros(shape, jnp.float32) for shape in shapes]
     incoming = jnp.zeros(images.shape[1:], jnp.bfloat16)
     returned = []
@@ -320,20 +333,21 @@
         if moment < micro_count:
             incoming = from_behind(grad_low, "section", -1)
         totals = [first_part + second_part for first_part, second_part in zip(totals, terms)]
-    owned = (
-        lax.psum_scatter(totals[0], "dp", scatter_dimension=1, tiled=True),
-        lax.psum_scatter(totals[1], "dp", scatter_dimension=1, tiled=True),
-        lax.psum_scatter(totals[2], "dp", scatter_dimension=2, tiled=True),
-        lax.psum_scatter(totals[3], "dp", scatter_dimension=3, tiled=True),
-        lax.psum_scatter(totals[4], "dp", scatter_dimension=2, tiled=True),
-        lax.psum_scatter(totals[5], "dp", scatter_dimension=1, tiled=True),
-        lax.psum_scatter(totals[6], "dp", scatter_dimension=1, tiled=True),
-        lax.psum_scatter(totals[7], "dp", scatter_dimension=1, tiled=True),
-        lax.psum_scatter(totals[8], "dp", scatter_dimension=1, tiled=True),
-        lax.psum_scatter(totals[9], "dp", scatter_dimension=2, tiled=True),
-        lax.psum_scatter(totals[10], "dp", scatter_dimension=2, tiled=True),
-        lax.psum_scatter(totals[11], "dp", scatter_dimension=1, tiled=True),
-    )
+    shards = (
+        ln1_gain,
+        ln1_bias,
+        qkv_weight,
+        qv_bias,
+        out_weight,
+        out_bias,
+        ln2_gain,
+        ln2_bias,
+        up_weight,
+        up_bias,
+        down_weight,
+        down_bias,
+    )
+    owned = scatter_all(totals, shards)
     input_grads = jnp.stack(
         [choose(returned[index + 1], returned[index]) for index in range(micro_count)]
     )

time: 2080 us -> 1210 us (0.58)
  waiting for transfers between devices: 1420 us -> 669 us
  blocking collectives: 193 us -> 71.1 us
  local copies, waits for them, and re-layouts: 97.5 us -> 137 us
    reduce_scatter x4 -> x1, waiting for transfers between devices: 492 us -> 87.8 us  [scatter_all(): lax.psum_scatter(totals[index].astype(jnp.bfloat16), 'dp', scatter_dimens...]
    unnamed x32 -> x20, waiting for transfers between devices: 341 us -> 110 us
    psum x10 -> x9, waiting for transfers between devices: 464 us -> 283 us  [both_halves(): return lax.psum(partial.astype(jnp.bfloat16), 'mp').astype(jnp.float32)]
    all_gather x8 -> x1, blocking collectives: 173 us -> 32.9 us  [gather_all(): packed = lax.all_gather(flat, 'dp', axis=0, tiled=False)]
    all_gather x4, waiting for transfers between devices: 123 us -> 186 us  [gather_all(): lax.all_gather(piece, 'dp', axis=axis, tiled=True)]
    unnamed x408 -> x407, local copies, waits for them, and re-layouts: 43.7 us -> 79.7 us
  transfers between devices with their start and end apart: 29 -> 21, of which waited for: 25 -> 16; matrix products, arithmetic and copies ran while one was open for 10% -> 20% of each run, Pallas kernels for 0% -> 0%
where the time goes in v1:
time: 1210 us; the launch traced here: 1200 us
  waiting for transfers between devices  669 us (55%)
  matrix products  222 us (18%)
  local copies, waits for them, and re-layouts  137 us (11%)
  other arithmetic  78.5 us (6%)
  blocking collectives  71.1 us (6%)
  between operations  16.9 us (1%)
    psum x9, waiting for transfers between devices, both_halves(): return lax.psum(partial.astype(jnp.bfloat16), 'mp').astype(jnp.float32)  283 us
    all_gather x4, waiting for transfers between devices, gather_all(): lax.all_gather(piece, 'dp', axis=axis, tiled=True)  186 us
    unnamed x20, waiting for transfers between devices  110 us
    reduce_scatter x1, waiting for transfers between devices, scatter_all(): lax.psum_scatter(totals[index].astype(jnp.bfloat16), 'dp', scatter_dimens...  87.8 us
    unnamed x407, local copies, waits for them, and re-layouts  79.7 us
    unnamed x1, blocking collectives  38.2 us
    dot_general x3, matrix products, forward(): jnp.einsum('blf,fd->bld', gelu_out, down_mat, preferred_element_type=jnp....  37.7 us
    all_gather x1, blocking collectives, gather_all(): packed = lax.all_gather(flat, 'dp', axis=0, tiled=False)  32.9 us
  transfers between devices with their start and end apart: 21, of which 16 were waited for; matrix products, arithmetic and copies ran while one was open for 20% of the time, Pallas kernels for 0%

profile of v1, /device:TPU:0, one launch (start us, length us, event | category | flops | bytes accessed | tf_op | source)
XLA Modules:
  0.0 1204.3 jit_solution(4596555902169269443)
XLA Ops:
  15.5 32.9 %all-gather.1 = bf16[8,1,1152]{2,1,0:T(2,128)(2,1)S(1)} all-gather(bf16[1,1,1152]{2,1,0:T(2,128)(2,1)S(1)} %reshape.803), channel_id=2, replica_groups=mesh['section'=2,'dp'=8,'mp'=2] {'dp'}, dimensions={0}, use_global_device_ids=true | all-gather | bytes 20736 | tf_op jit(solution)/shard_map/all_gather | solution.py:16
  52.2 20.9 %all-gather.7.cloned.1.call-done = bf16[1,3,1024,512]{3,2,1,0:T(8,128)(2,1)} async-done(((bf16[1,3,128,512]{3,2,1,0:T(8,128)(2,1)}), bf16[1,3,1024,512]{3,2,1,0:T(8,128)(2,1)}) %all-gather.7.cloned.1.call-update) | async-done | bytes 3145744 | tf_op jit(solution)/shard_map/all_gather | solution.py:27
  73.1 3.7 fusion.157
  87.2 26.0 %all-gather.9.cloned.1.call-done = bf16[1,512,1024]{2,1,0:T(8,128)(2,1)} async-done(((bf16[1,512,128]{2,1,0:T(8,128)(2,1)}), bf16[1,512,1024]{2,1,0:T(8,128)(2,1)}) %all-gather.9.cloned.1.call-update) | async-done | bytes 1048592 | tf_op jit(solution)/shard_map/all_gather | solution.py:27
  118.3 32.0 %all-reduce.14.cloned.1.call-done = bf16[2,197,1024]{2,1,0:T(8,128)(2,1)} async-done(((bf16[2,197,1024]{2,1,0:T(8,128)(2,1)}), bf16[2,197,1024]{2,1,0:T(8,128)(2,1)}) %all-reduce.14.cloned.1.call-update) | async-done | bytes 806928 | tf_op jit(solution)/shard_map/psum | solution.py:68
  153.7 71.4 %all-gather.11.cloned.1.call-done = bf16[1,1024,2048]{2,1,0:T(8,128)(2,1)} async-done(((bf16[1,128,2048]{2,1,0:T(8,128)(2,1)}), bf16[1,1024,2048]{2,1,0:T(8,128)(2,1)}) %all-gather.11.cloned.1.call-update) | async-done | bytes 4194320 | tf_op jit(solution)/shard_map/all_gather | solution.py:27
  225.1 7.2 fusion.571
  232.2 67.9 %all-gather.13.cloned.1.call-done = bf16[1,2048,1024]{2,1,0:T(8,128)(2,1)} async-done(((bf16[1,2048,128]{2,1,0:T(8,128)(2,1)}), bf16[1,2048,1024]{2,1,0:T(8,128)(2,1)}) %all-gather.13.cloned.1.call-update) | async-done | bytes 4194320 | tf_op jit(solution)/shard_map/all_gather | solution.py:27
  300.2 13.1 %fusion.460 = bf16[2,197,1024]{2,1,0:T(8,128)(2,1)} fusion(bf16[1,2048,1024]{2,1,0:T(8,128)(2,1)} %all-gather.13.cloned.1.call-done, f32[2,197,2048]{2,1,0:T(8,128)} %get-tuple-element.200, u8[197,2048]{1,0:T(8,128)(4,1)S(1)} %get-tuple-element.75, u8[197,2048]{1,0:T(8,128)(4,1)S(1)} %get-tuple-element.74), kind=kOutput, calls=%fused_computation.599 | convolution fusion | flops 1709443072 | bytes 9035776 | tf_op jit(solution)/shard_map/blf,fd->bld/dot_general | solution.py:159
  314.6 32.1 %all-reduce.16.cloned.1.call-done = bf16[2,197,1024]{2,1,0:T(8,128)(2,1)} async-done(((bf16[2,197,1024]{2,1,0:T(8,128)(2,1)}), bf16[2,197,1024]{2,1,0:T(8,128)(2,1)}) %all-reduce.16.cloned.1.call-update) | async-done | bytes 806928 | tf_op jit(solution)/shard_map/psum | solution.py:68
  372.0 32.1 %all-reduce.18.cloned.1.call-done = bf16[2,197,1024]{2,1,0:T(8,128)(2,1)} async-done(((bf16[2,197,1024]{2,1,0:T(8,128)(2,1)}), bf16[2,197,1024]{2,1,0:T(8,128)(2,1)}) %all-reduce.18.cloned.1.call-update) | async-done | bytes 806928 | tf_op jit(solution)/shard_map/psum | solution.py:68
  409.2 7.5 fusion.568
  416.7 4.5 convert_reduce_fusion.2
  424.0 11.5 fusion.465
  441.0 47.7 %all-reduce.30.cloned.1.call-done = (bf16[2,197,1024]{2,1,0:T(8,128)(2,1)}, bf16[2,197,1024]{2,1,0:T(8,128)(2,1)}) async-done(((bf16[2,197,1024]{2,1,0:T(8,128)(2,1)}, bf16[2,197,1024]{2,1,0:T(8,128)(2,1)}), (bf16[2,197,1024]{2,1,0:T(8,128)(2,1)}, bf16[2,197,1024]{2,1,0:T(8,128)(2,1)})) %all-reduce.30.cloned.1.call-update) | async-done | bytes 1613840 | tf_op jit(solution)/shard_map/psum | solution.py:68
  498.0 4.2 convert_reduce_fusion.22
  518.7 4.7 bitcast_convert_fusion.2
  543.1 3.6 fusion.611
  546.8 47.9 %all-reduce.28.cloned.1.call-done = (bf16[2,197,1024]{2,1,0:T(8,128)(2,1)}, bf16[2,197,1024]{2,1,0:T(8,128)(2,1)}) async-done(((bf16[2,197,1024]{2,1,0:T(8,128)(2,1)}, bf16[2,197,1024]{2,1,0:T(8,128)(2,1)}), (bf16[2,197,1024]{2,1,0:T(8,128)(2,1)}, bf16[2,197,1024]{2,1,0:T(8,128)(2,1)})) %all-reduce.28.cloned.1.call-update) | async-done | bytes 1613840 | tf_op jit(solution)/shard_map/psum | solution.py:68
  596.2 5.4 fusion.834
  605.4 10.2 fusion.569
  616.7 5.2 convert_reduce_fusion.1
  628.1 33.2 %all-reduce.20.cloned.1.call-done = bf16[2,197,1024]{2,1,0:T(8,128)(2,1)} async-done(((bf16[2,197,1024]{2,1,0:T(8,128)(2,1)}), bf16[2,197,1024]{2,1,0:T(8,128)(2,1)}) %all-reduce.20.cloned.1.call-update) | async-done | bytes 806928 | tf_op jit(solution)/shard_map/psum | solution.py:68
  671.9 4.4 convert_reduce_fusion.20
  688.8 4.6 bitcast_convert_fusion.1
  693.6 35.2 %all-reduce.22.cloned.1.call-done = bf16[2,197,1024]{2,1,0:T(8,128)(2,1)} async-done(((bf16[2,197,1024]{2,1,0:T(8,128)(2,1)}), bf16[2,197,1024]{2,1,0:T(8,128)(2,1)}) %all-reduce.22.cloned.1.call-update) | async-done | bytes 806928 | tf_op jit(solution)/shard_map/psum | solution.py:68
  749.7 13.1 %fusion.470 = bf16[2,197,1024]{2,1,0:T(8,128)(2,1)} fusion(bf16[1,2048,1024]{2,1,0:T(8,128)(2,1)} %all-gather.13.cloned.1.call-done, f32[2,197,2048]{2,1,0:T(8,128)} %get-tuple-element.208, u8[197,2048]{1,0:T(8,128)(4,1)} %get-tuple-element.150, u8[197,2048]{1,0:T(8,128)(4,1)} %get-tuple-element.151), kind=kOutput, calls=%fused_computation.601 | convolution fusion | flops 1709443072 | bytes 9035776 | tf_op jit(solution)/shard_map/blf,fd->bld/dot_general | solution.py:159
  763.2 22.6 %all-reduce.24.cloned.1.call-done = bf16[2,197,1024]{2,1,0:T(8,128)(2,1)} async-done(((bf16[2,197,1024]{2,1,0:T(8,128)(2,1)}), bf16[2,197,1024]{2,1,0:T(8,128)(2,1)}) %all-reduce.24.cloned.1.call-update) | async-done | bytes 806928 | tf_op jit(solution)/shard_map/psum | solution.py:68
  796.5 4.4 convert_reduce_fusion.18
  808.9 4.6 bitcast_convert_fusion
  815.1 3.6 fusion.604
  825.2 3.9 copy.285
  838.4 4.0 fusion.101
  842.4 7.8 copy.283
  850.2 5.0 copy.296
  855.4 11.3 fusion.169
  866.8 9.1 fusion.167
  875.9 10.6 fusion.100
  886.5 20.6 %copy.287 = bf16[1,2048,1024]{1,0,2:T(2,128)(2,1)} copy(bf16[1,2048,1024]{2,1,0:T(8,128)(2,1)} %fusion.100) | data formatting | bytes 8388608
  907.1 8.0 copy.409
  915.8 4.6 fusion.510
  920.4 5.9 fusion.511
  926.3 8.0 fusion.99
  939.2 3.7 fusion.515
  949.5 38.2 %all-reduce = f32[8,1152]{1,0:T(8,128)S(1)} all-reduce(f32[8,1152]{1,0:T(8,128)S(1)} %constant_dynamic-update-slice_fusion), channel_id=3, replica_groups=mesh['section'=2,'dp'=8,'mp'=2] {'dp'}, use_global_device_ids=true, to_apply=%region_84.85.clone | all-reduce | flops 9216 | bytes 73728
  993.0 19.8 %reduce-scatter.13.cloned.1.call-done = bf16[128,1536]{1,0:T(8,128)(2,1)} async-done(((bf16[1024,1536]{1,0:T(8,128)(2,1)}), bf16[128,1536]{1,0:T(8,128)(2,1)}) %reduce-scatter.13.cloned.1.call-update) | async-done | bytes 393232
  1015.9 87.8 %reduce-scatter.17.cloned.1.call-done = bf16[128,2048]{1,0:T(8,128)(2,1)} async-done(((bf16[1024,2048]{1,0:T(8,128)(2,1)}), bf16[128,2048]{1,0:T(8,128)(2,1)}) %reduce-scatter.17.cloned.1.call-update) | async-done | bytes 524304
  1107.3 87.8 %reduce-scatter.11.cloned.1.call-done = bf16[1,128,2048]{2,1,0:T(8,128)(2,1)} async-done(((bf16[1,1024,2048]{2,1,0:T(8,128)(2,1)}), bf16[1,128,2048]{2,1,0:T(8,128)(2,1)}) %reduce-scatter.11.cloned.1.call-update) | async-done | bytes 524304 | tf_op jit(solution)/shard_map/reduce_scatter | solution.py:61
  (644 shorter events, 234.1 us)
Async XLA Ops:
  7.2 65.9 %all-gather.7.cloned.1.call-start = ((), (), s32[]{:S(2)}) async-start(), calls=%async_computation.4 | async-start | bytes 3538944 | tf_op jit(solution)/shard_map/all_gather | solution.py:27
  7.9 105.3 %all-gather.9.cloned.1.call-start = ((), (), s32[]{:S(2)}) async-start(), calls=%async_computation.5 | async-start | bytes 1179648 | tf_op jit(solution)/shard_map/all_gather | solution.py:27
  8.7 141.6 %all-reduce.14.cloned.1.call-start = ((), (), s32[]{:S(2)}) async-start(), calls=%async_computation.6 | async-start | bytes 1638400 | tf_op jit(solution)/shard_map/psum | solution.py:68
  48.5 176.6 %copy-start.148 = (f32[1024]{0:T(1024)}, f32[1024]{0:T(1024)S(1)}, u32[]{:S(2)}) copy-start(f32[1024]{0:T(1024)S(1)} %get-tuple-element.190) | copy-start | bytes 12292
  48.5 298.2 %copy-start.112 = (f32[1024]{0:T(1024)}, f32[1024]{0:T(1024)S(1)}, u32[]{:S(2)}) copy-start(f32[1024]{0:T(1024)S(1)} %get-tuple-element.189) | copy-start | bytes 12292
  48.5 306.4 %copy-start.152 = (f32[1024]{0:T(1024)}, f32[1024]{0:T(1024)S(1)}, u32[]{:S(2)}) copy-start(f32[1024]{0:T(1024)S(1)} %get-tuple-element.194) | copy-start | bytes 12292
  48.5 556.9 %copy-start.103 = (f32[1024]{0:T(1024)}, f32[1024]{0:T(1024)S(1)}, u32[]{:S(2)}) copy-start(f32[1024]{0:T(1024)S(1)} %get-tuple-element.192) | copy-start | bytes 12292
  51.0 302.0 %copy-start.66 = (bf16[1,2,197,1024]{3,1,2,0:T(2,128)(2,1)}, bf16[1,2,197,1024]{3,1,2,0:T(2,128)(2,1)S(1)}, u32[]{:S(2)}) copy-start(bf16[1,2,197,1024]{3,1,2,0:T(2,128)(2,1)S(1)} %get-tuple-element.173) | copy-start | bytes 2420740
  52.1 306.7 %copy-start.110 = (f32[8,64]{1,0:T(8,128)}, f32[8,64]{1,0:T(8,128)S(1)}, u32[]{:S(2)}) copy-start(f32[8,64]{1,0:T(8,128)S(1)} %add.600) | copy-start | bytes 6148
  52.2 309.4 %copy-start.108 = (f32[8,64]{1,0:T(8,128)}, f32[8,64]{1,0:T(8,128)S(1)}, u32[]{:S(2)}) copy-start(f32[8,64]{1,0:T(8,128)S(1)} %add.603) | copy-start | bytes 6148
  86.4 29.5 %copy-start.51 = (bf16[2,197,8,64]{1,3,2,0:T(8,128)(2,1)}, bf16[2,197,8,64]{1,3,2,0:T(8,128)(2,1)S(1)}, u32[]{:S(2)}) copy-start(bf16[2,197,8,64]{1,3,2,0:T(8,128)(2,1)S(1)} %add_convert_fusion.14) | copy-start | bytes 1210372
  87.2 66.5 %copy-start.79 = (bf16[2,8,64,197]{3,2,1,0:T(8,128)(2,1)}, bf16[2,8,64,197]{3,2,1,0:T(8,128)(2,1)S(1)}, u32[]{:S(2)}) copy-start(bf16[2,8,64,197]{3,2,1,0:T(8,128)(2,1)S(1)} %fusion.484) | copy-start | bytes 1210372
  116.0 109.1 %all-gather.11.cloned.1.call-start = ((), (), s32[]{:S(2)}) async-start(), calls=%async_computation.7 | async-start | bytes 4718592 | tf_op jit(solution)/shard_map/all_gather | solution.py:27
  116.6 183.6 %all-gather.13.cloned.1.call-start = ((), (), s32[]{:S(2)}) async-start(), calls=%async_computation.8 | async-start | bytes 4718592 | tf_op jit(solution)/shard_map/all_gather | solution.py:27
  117.2 229.5 %all-reduce.16.cloned.1.call-start = ((), (), s32[]{:S(2)}) async-start(), calls=%async_computation.9 | async-start | bytes 1638400 | tf_op jit(solution)/shard_map/psum | solution.py:68
  118.3 114.0 %copy-start.160 = (f32[2048]{0:T(1024)}, f32[2048]{0:T(1024)S(1)}, u32[]{:S(2)}) copy-start(f32[2048]{0:T(1024)S(1)} %reshape.797) | copy-start | bytes 24580
  150.3 74.8 %copy-start.15 = (bf16[2,197,1024]{2,1,0:T(8,128)(2,1)S(1)}, bf16[2,197,1024]{2,1,0:T(8,128)(2,1)}, u32[]{:S(2)}) copy-start(bf16[2,197,1024]{2,1,0:T(8,128)(2,1)} %all-reduce.14.cloned.1.call-done) | copy-start | bytes 2420740
  300.2 13.2 %copy-start.166 = (s32[2,1]{0,1:T(1,128)S(1)}, s32[2,1]{0,1:T(1,128)}, u32[]{:S(2)}) copy-start(s32[2,1]{0,1:T(1,128)} %param.17) | copy-start | bytes 28
  313.3 90.8 %all-reduce.18.cloned.1.call-start = ((), (), s32[]{:S(2)}) async-start(), calls=%async_computation.10 | async-start | bytes 1638400 | tf_op jit(solution)/shard_map/psum | solution.py:68
  349.3 3.6 collective-permute-start
  368.8 119.8 %all-reduce.30.cloned.1.call-start = ((), (), s32[]{:S(2)}) async-start(), calls=%async_computation.20 | async-start | bytes 3276800 | tf_op jit(solution)/shard_map/psum | solution.py:68
  369.7 121.6 %copy-start.167 = (f32[2]{0:T(128)}, f32[2]{0:T(128)S(1)}, u32[]{:S(2)}) copy-start(f32[2]{0:T(128)S(1)} %broadcast_select_fusion.29) | copy-start | bytes 28
  372.0 37.1 %copy-start.119 = (f32[2,197]{1,0:T(2,128)}, f32[2,197]{1,0:T(2,128)S(1)}, u32[]{:S(2)}) copy-start(f32[2,197]{1,0:T(2,128)S(1)} %broadcast_multiply_fusion.14) | copy-start | bytes 4732
  372.0 37.1 %copy-start.149 = (f32[1024]{0:T(1024)S(1)}, f32[1024]{0:T(1024)}, u32[]{:S(2)}) copy-start(f32[1024]{0:T(1024)} %copy-done.148) | copy-start | bytes 12292
  372.0 37.1 %copy-start.161 = (f32[2048]{0:T(1024)S(1)}, f32[2048]{0:T(1024)}, u32[]{:S(2)}) copy-start(f32[2048]{0:T(1024)} %copy-done.160) | copy-start | bytes 24580
  409.1 82.2 %copy-start.6 = (f32[2,197,1024]{2,1,0:T(8,128)}, f32[2,197,1024]{2,1,0:T(8,128)S(1)}, u32[]{:S(2)}) copy-start(f32[2,197,1024]{2,1,0:T(8,128)S(1)} %get-tuple-element.145) | copy-start | bytes 4841476
  435.5 159.2 %all-reduce.28.cloned.1.call-start = ((), (), s32[]{:S(2)}) async-start(), calls=%async_computation.19 | async-start | bytes 3276800 | tf_op jit(solution)/shard_map/psum | solution.py:68
  440.6 53.5 %copy-start.115 = (f32[2,197]{1,0:T(2,128)}, f32[2,197]{1,0:T(2,128)S(1)}, u32[]{:S(2)}) copy-start(f32[2,197]{1,0:T(2,128)S(1)} %broadcast_multiply_fusion.17) | copy-start | bytes 4732
  441.0 53.2 %copy-start.121 = (f32[2,197]{1,0:T(2,128)}, f32[2,197]{1,0:T(2,128)S(1)}, u32[]{:S(2)}) copy-start(f32[2,197]{1,0:T(2,128)S(1)} %add_rsqrt_fusion.5) | copy-start | bytes 4732
  507.3 16.0 %collective-permute-start.1 = (bf16[2,197,1024]{2,0,1:T(2,128)(2,1)}, bf16[2,197,1024]{2,0,1:T(2,128)(2,1)}, u32[]{:S(2)}, u32[]{:S(2)}) collective-permute-start(bf16[2,197,1024]{2,0,1:T(2,128)(2,1)} %copy.214), channel_id=1, source_target_pairs={{0,16},{1,17},{2,18},{3,19},{4,20},{5,21},{6,22},{7,23},{8,24},{9,... | collective-permute-start | bytes 2420744 | tf_op jit(solution)/shard_map/ppermute | solution.py:74
  541.5 119.7 %all-reduce.20.cloned.1.call-start = ((), (), s32[]{:S(2)}) async-start(), calls=%async_computation.11 | async-start | bytes 1638400 | tf_op jit(solution)/shard_map/psum | solution.py:68
  543.1 58.5 %copy-start.127 = (f32[2,197]{1,0:T(2,128)}, f32[2,197]{1,0:T(2,128)S(1)}, u32[]{:S(2)}) copy-start(f32[2,197]{1,0:T(2,128)S(1)} %add_rsqrt_fusion.4) | copy-start | bytes 4732
  543.1 53.1 %copy-start.16 = (bf16[2,197,1024]{2,1,0:T(8,128)(2,1)S(1)}, bf16[2,197,1024]{2,1,0:T(8,128)(2,1)}, u32[]{:S(2)}) copy-start(bf16[2,197,1024]{2,1,0:T(8,128)(2,1)} %all-reduce.14.cloned.1.call-done) | copy-start | bytes 2420740
  543.1 53.1 %copy-start.120 = (f32[2,197]{1,0:T(2,128)S(1)}, f32[2,197]{1,0:T(2,128)}, u32[]{:S(2)}) copy-start(f32[2,197]{1,0:T(2,128)} %copy-done.119) | copy-start | bytes 4732
  603.8 12.9 %copy-start.170 = (bf16[1,2048,1024]{2,1,0:T(8,128)(2,1)S(1)}, bf16[1,2048,1024]{2,1,0:T(8,128)(2,1)}, u32[]{:S(2)}) copy-start(bf16[1,2048,1024]{2,1,0:T(8,128)(2,1)} %all-gather.13.cloned.1.call-done) | copy-start | bytes 12582916
  603.8 11.8 collective-permute-start.2
  626.0 102.7 %all-reduce.22.cloned.1.call-start = ((), (), s32[]{:S(2)}) async-start(), calls=%async_computation.12 | async-start | bytes 1638400 | tf_op jit(solution)/shard_map/psum | solution.py:68
  626.3 41.1 %copy-start.117 = (f32[2,197]{1,0:T(2,128)}, f32[2,197]{1,0:T(2,128)S(1)}, u32[]{:S(2)}) copy-start(f32[2,197]{1,0:T(2,128)S(1)} %broadcast_multiply_fusion.11) | copy-start | bytes 4732
  628.0 39.3 %copy-start.123 = (f32[2,197]{1,0:T(2,128)}, f32[2,197]{1,0:T(2,128)S(1)}, u32[]{:S(2)}) copy-start(f32[2,197]{1,0:T(2,128)S(1)} %add_rsqrt_fusion.3) | copy-start | bytes 4732
  693.5 92.3 %all-reduce.24.cloned.1.call-start = ((), (), s32[]{:S(2)}) async-start(), calls=%async_computation.13 | async-start | bytes 1638400 | tf_op jit(solution)/shard_map/psum | solution.py:68
  693.6 40.6 %copy-start.125 = (f32[2,197]{1,0:T(2,128)}, f32[2,197]{1,0:T(2,128)S(1)}, u32[]{:S(2)}) copy-start(f32[2,197]{1,0:T(2,128)S(1)} %add_rsqrt_fusion.2) | copy-start | bytes 4732
  735.0 4.8 collective-permute-start.3
  749.7 187.3 %all-reduce.26.cloned.1.call-start = ((), (), s32[]{:S(2)}) async-start(), calls=%async_computation.18 | async-start | bytes 3276800 | tf_op jit(solution)/shard_map/psum | solution.py:68
  749.7 13.1 %copy-start.3 = (f32[2,197,1024]{2,1,0:T(8,128)S(1)}, f32[2,197,1024]{2,1,0:T(8,128)}, u32[]{:S(2)}) copy-start(f32[2,197,1024]{2,1,0:T(8,128)} %get-tuple-element.137) | copy-start | bytes 4841476
  813.5 177.6 %reduce-scatter.15.cloned.1.call-start = ((), (), s32[]{:S(2)}) async-start(), calls=%async_computation.16 | async-start | bytes 1179648
  832.1 180.8 %reduce-scatter.13.cloned.1.call-start = ((), (), s32[]{:S(2)}) async-start(), calls=%async_computation.15 | async-start | bytes 3538944
  855.3 248.5 %reduce-scatter.17.cloned.1.call-start = ((), (), s32[]{:S(2)}) async-start(), calls=%async_computation.17 | async-start | bytes 4718592
  915.1 280.0 %reduce-scatter.11.cloned.1.call-start = ((), (), s32[]{:S(2)}) async-start(), calls=%async_computation.14 | async-start | bytes 4718592 | tf_op jit(solution)/shard_map/reduce_scatter | solution.py:61
  (163 other events, 647.9 us)
Sparse Core Ops, SparseCore 0:
  10.2 62.8 all-gather.6
  75.1 38.0 all-gather.8
  116.1 34.0 all-reduce.13
  152.2 72.7 all-gather.10
  227.0 73.1 all-gather.12
  313.4 33.2 all-reduce.15
  369.0 35.1 all-reduce.17
  435.6 52.9 all-reduce.29
  541.7 52.9 all-reduce.27
  626.1 35.0 all-reduce.19
  693.6 35.0 all-reduce.21
  749.8 35.9 all-reduce.23
  813.7 52.9 all-reduce.25
  870.5 64.1 reduce-scatter.14
  938.2 74.6 reduce-scatter.12
  1016.3 87.3 reduce-scatter.16
  1107.2 87.9 reduce-scatter.10

commit v2 on v1

--- a/solution.py
+++ b/solution.py
@@ -1,8 +1,12 @@
+import functools
+import heapq
 import math
 
 import jax
 import jax.numpy as jnp
 from jax import lax
+from jax.experimental import pallas as pl
+from jax.experimental.pallas import tpu as pltpu
 from jax.sharding import PartitionSpec as P
 
 HD = 64
@@ -369,9 +373,1137 @@
     )
 
 
+MESH = pl.DeviceIdType.MESH
+BF = jnp.bfloat16
+F32 = jnp.float32
+Z = 4
+EPS = 1e-06
+L = 197
+LP = 208
+R = 2 * LP
+SMALL, Q, K, V, OUT, UP, DOWN = range(7)
+MATS = (Q, K, V, OUT, UP, DOWN)
+BY_ROWS = (Q, K, V, UP)
+X_FIRST = (K, OUT)
+WIDTH = {Q: 512, K: 512, V: 512, OUT: 512, UP: 2048, DOWN: 2048}
+SELF, NEAR, INNER, FAR = range(4)
+
+
+class Clock:
+    def __init__(self):
+        self.now, self.queue, self.count = 0.0, [], 0
+
+    def add(self, ready, step, cost=0.2):
+        heapq.heappush(self.queue, (ready, self.count, cost, step))
+        self.count += 1
+
+    def pop(self):
+        ready, _, cost, step = heapq.heappop(self.queue)
+        self.now = max(self.now, ready)
+        step()
+        self.now += cost
+
+    def flush(self, until):
+        while self.queue and self.queue[0][0] <= until:
+            self.pop()
+
+    def run(self, cost, step, *args):
+        self.flush(self.now)
+        step(*args)
+        self.now += cost
+
+    def wait(self, until, step, *args):
+        self.flush(until)
+        self.now = max(self.now, until)
+        step(*args)
+
+    def drain(self, done):
+        while not done():
+            self.pop()
+
+
+def lanes(d, n=128):
+    return pl.ds(pl.multiple_of(d * 128, 128), n)
+
+
+def dot(a, b, ca, cb):
+    return lax.dot_general(a, b, (((ca,), (cb,)), ((), ())), preferred_element_type=F32)
+
+
+def half(m, ref, s, h):
+    n = WIDTH[m] // 2
+    at = pl.ds(pl.multiple_of(h * n, n), n)
+    return ref.at[s, :, at] if m in BY_ROWS else ref.at[s, at, :]
+
+
+def block(m, ref, s, d, h=None):
+    if m == SMALL:
+        return ref.at[s, d] if h is None else ref.at[s, d, pl.ds(h * 16, 16), :]
+    own = pl.ds(pl.multiple_of(d * 128, 128), 128)
+    n = WIDTH[m] // 2
+    other = pl.ds(0, 2 * n) if h is None else pl.ds(pl.multiple_of(h * n, n), n)
+    return ref.at[s, own, other] if m in BY_ROWS else ref.at[s, other, own]
+
+
+def kernel(
+    small_ref, qkv_ref, out_ref, up_ref, down_ref, x_ref, cot_ref, live_ref,
+    act_out, gin_out, gqkv_out, gout_out, gup_out, gdown_out, gvec_out,
+    wsmall, wq, wk, wv, wout, wup, wdown,
+    rq, rk, rv, rout, rup, rdown, xq, xk, xv, xout, xup, xdown,
+    zq, zk, zv, zout, zup, zdown, fq, fk, fv, fout, fup, fdown,
+    xs, qkvs, mixs, nrm2s, gels, slps, inv2s,
+    low, mid, gb, gpre, gqkv, ys, yr, acc, vec, sv, svc, svx, svz,
+    asem_s, asem_c, asem_z, asem_x, rsem_cs, rsem_c, rsem_xs, rsem_x, rsem_zs, rsem_z, rsem_fs, rsem_f,
+    ysem, ysem_s, osem, osem_r, osem_s, isem, vsem, vsem_s, free_c, free_x, free_z,
+):
+    shards = (small_ref, qkv_ref.at[0], qkv_ref.at[1], qkv_ref.at[2], out_ref, up_ref, down_ref)
+    wqkv = (wq, wk, wv)
+    w = (wsmall, wq, wk, wv, wout, wup, wdown)
+    rbuf = (None, rq, rk, rv, rout, rup, rdown)
+    xbuf = (None, xq, xk, xv, xout, xup, xdown)
+    zbuf = (None, zq, zk, zv, zout, zup, zdown)
+    fbuf = (None, fq, fk, fv, fout, fup, fdown)
+
+    c = lax.axis_index("section")
+    me = lax.axis_index("dp")
+    y = lax.axis_index("mp")
+    z, x = me // 2, lax.rem(me, 2)
+    to_x = {"dp": z * 2 + 1 - x}
+    to_c = {"section": 1 - c}
+    to_y = {"mp": 1 - y}
+
+    inner = jnp.logical_or(z == 1, z == 2)
+    near = z + 1 - 2 * lax.rem(z, 2)
+    lower = (z < 2).astype(jnp.int32)
+    places = (z, near, 1 + lower, 3 * lower)
+    inner_i = jnp.where(inner, 1, 0)
+
+    def at_dp(k, col):
+        return places[k] * 2 + (x if col == 0 else 1 - x)
+
+    def to_z(zi):
+        return {"dp": zi * 2 + x}
+
+    def remote(a, b, ss, rs, dev):
+        return pltpu.make_async_remote_copy(
+            src_ref=a, dst_ref=b, send_sem=ss, recv_sem=rs, device_id=dev, device_id_type=MESH
+        )
+
+    barrier = pltpu.get_barrier_semaphore()
+    for dev in [to_z(places[k]) for k in (NEAR, INNER, FAR)] + [to_x, to_c, to_y]:
+        pl.semaphore_signal(barrier, inc=1, device_id=dev, device_id_type=MESH)
+    pl.semaphore_wait(barrier, Z + 2)
+
+    def number(per):
+        table = {}
+        for key, count in per:
+            for i in range(count):
+                table[key, i] = len(table)
+        return table
+
+    pieces = [(s, m) for s in range(2) for m in range(7)]
+    az = number((p, 6 if p[1] in X_FIRST else 3) for p in pieces)
+    ax = number((p, 1 if p[1] in X_FIRST else 4) for p in pieces)
+    rz = number((p, 8 if p[1] in X_FIRST else 4) for p in pieces if p[1])
+    rx = number((p, 1 if p[1] in X_FIRST else 4) for p in pieces if p[1])
+
+    def wait_bytes(m, count, sem):
+        if m == SMALL:
+            v = inv2s.at[0, pl.ds(0, 8 * count), :]
+        else:
+            v = wdown.at[:, pl.ds(0, count * WIDTH[m] // 32), :]
+        pltpu.make_async_copy(v, v, sem).wait()
+
+    def ag_share(s, m):
+        p = s * 7 + m
+
+        @pl.when(c == s)
+        def _():
+            dst = block(m, w[m], s, me)
+            remote(shards[m], dst, asem_s.at[p], asem_c.at[p, 0], to_c).start()
+            pltpu.make_async_copy(shards[m], dst, asem_c.at[p, 0]).start()
+
+    def ag_shared(s, m):
+        whole = block(m, w[m], s, me)
+        pltpu.make_async_copy(whole, whole, asem_c.at[s * 7 + m, 0]).wait()
+
+    def ag_own_z(s, m, col):
+        p, first = s * 7 + m, az[(s, m), col * 3]
+        b = block(m, w[m], s, at_dp(SELF, col), c)
+        slot = jnp.where(inner, INNER, FAR) - 1
+        remote(b, b, asem_s.at[p], asem_z.at[first], to_z(near)).start()
+        remote(b, b, asem_s.at[p], asem_z.at[first + slot], to_z(places[INNER])).start()
+
+    def ag_to_x(s, m, k):
+        b = block(m, w[m], s, at_dp(k, 0), c)
+        remote(b, b, asem_s.at[s * 7 + m], asem_x.at[ax[(s, m), k]], to_x).start()
+
+    def ag_to_c(s, m, k, col):
+        p = s * 7 + m
+        b = block(m, w[m], s, at_dp(k, col), c)
+        remote(b, b, asem_s.at[p], asem_c.at[p, 1], to_c).start()
+
+    def ag_z(s, m, k, col):
+        b = block(m, w[m], s, at_dp(k, col), c)
+        cp = remote(b, b, asem_s.at[s * 7 + m], asem_z.at[az[(s, m), col * 3 + k - 1]], to_z(near))
+        cp.wait_recv()
+        if k != NEAR:
+
+            @pl.when(inner)
+            def _():
+                cp.start()
+
+        if m not in X_FIRST:
+            ag_to_x(s, m, k)
+        ag_to_c(s, m, k, col)
+
+    def ag_x(s, m, k):
+        b = block(m, w[m], s, at_dp(k, 1), c)
+        remote(b, b, asem_s.at[s * 7 + m], asem_x.at[ax[(s, m), k]], to_x).wait_recv()
+        if m in X_FIRST:
+            ag_own_z(s, m, 1)
+        ag_to_c(s, m, k, 1)
+
+    def ag_need(s, m):
+        wait_bytes(m, 7, asem_c.at[s * 7 + m, 1])
+
+    def ag_sent(s, m):
+        count = 7 + (1 + 4 if m in X_FIRST else 4 + 2)
+        extra = 4 if m in X_FIRST else 2
+        for ins in range(2):
+            for own in range(2):
+
+                @pl.when(jnp.logical_and(inner_i == ins, jnp.where(c == s, 1, 0) == own))
+                def _():
+                    wait_bytes(m, count + extra * ins + 2 * own, asem_s.at[s * 7 + m])
+
+    def rows_of(b):
+        return pl.ds(b * LP, LP)
+
+    def y_src(k):
+        return slps.at[1, :, pl.ds(0, 1024)] if k == 7 else ys
+
+    def y_start(k, b, n):
+        cols = lanes(n * 2, 256)
+        src = y_src(k).at[rows_of(b), cols]
+        remote(src, yr.at[k % 2, rows_of(b), cols], ysem_s.at[k * 2 + b], ysem.at[k * 2 + b], to_y).start()
+
+    def y_wait(k, b):
+        src = y_src(k).at[rows_of(b), pl.ds(0, 1024)]
+        cp = remote(src, yr.at[k % 2, rows_of(b), :], ysem_s.at[k * 2 + b], ysem.at[k * 2 + b], to_y)
+        cp.wait_recv()
+        cp.wait_send()
+
+    def y_sum(k, rows):
+        return y_src(k)[rows, :].astype(F32) + yr[k % 2, rows, :].astype(F32)
+
+    def unpack_small(s):
+        total = jnp.zeros((32, 128), F32)
+        for d in range(2 * Z):
+            piece = wsmall[s, d].astype(F32)
+            total = total + piece
+            for r in range(6):
+                vec[s, r : r + 1, d * 128 : d * 128 + 128] = piece[r : r + 1, :]
+        for k in range(8):
+            vec[s, 6:7, k * 128 : k * 128 + 128] = total[6 + k : 7 + k, :]
+            vec[s, 7:8, k * 128 : k * 128 + 128] = total[14 + k : 15 + k, :]
+            vec[s, 8:9, k * 128 : k * 128 + 128] = total[22 + k : 23 + k, :]
+
+    def row(s, r):
+        return vec[s, r : r + 1, :]
+
+    CH = 16
+
+    def norm_chunk(v):
+        mean = jnp.mean(v, axis=-1, keepdims=True)
+        cen = v - mean
+        inv = lax.rsqrt(jnp.mean(cen * cen, axis=-1, keepdims=True) + EPS)
+        return cen * inv, inv
+
+    def chunks(b):
+        def wrap(body):
+            @pl.loop(0, LP // CH)
+            def _(i):
+                body(pl.ds(pl.multiple_of(b * LP + i * CH, CH), CH))
+
+        return wrap
+
+    def ln1(s, b):
+        gain, shift = row(s, 0), row(s, 1)
+
+        @chunks(b)
+        def _(rows):
+            nrm, _ = norm_chunk(xs[s, rows, :].astype(F32))
+            low[rows, :] = (nrm * gain + shift).astype(BF)
+
+    def unweave(src, dst, b, alive):
+        r = lax.broadcasted_iota(jnp.int32, (LP, R), 0)
+        q = lax.broadcasted_iota(jnp.int32, (LP, R), 1)
+        take = jnp.where(q == 2 * r + b, 1.0, 0.0)
+        if alive is not None:
+            take = take * alive
+        take = take.astype(BF)
+
+        @pl.loop(0, 4)
+        def _(n):
+            cols = lanes(n * 2, 256)
+            dst[rows_of(b), cols] = dot(take, src[:, cols], 1, 0).astype(BF)
+
+    def alive_of(b):
+        return jnp.where(live_ref[c, 0] > b, 1.0, 0.0)
+
+    def project(s, b):
+        for t in range(3):
+            @pl.loop(0, 2)
+            def _(n):
+                cols = lanes(n * 2, 256)
+                a = dot(low[rows_of(b), :], wqkv[t][s, :, cols], 1, 0)
+                if t != 1:
+                    base = 0 if t == 0 else 512
+                    a = a + vec[s, 6:7, pl.ds(pl.multiple_of(base + n * 256, 256), 256)]
+                qkvs[s, t, rows_of(b), cols] = a.astype(BF)
+
+    left = lax.broadcasted_iota(jnp.int32, (1, 128), 1) < 64
+    live_col = lax.broadcasted_iota(jnp.int32, (1, LP), 1) < L
+
+    def pick(h, v):
+        return jnp.where(left if h == 0 else jnp.logical_not(left), v, jnp.zeros_like(v))
+
+    def softmax(q, k):
+        sc = dot(q, k, 1, 1) * (64.0 ** -0.5)
+        sc = jnp.where(live_col, sc, -1e30)
+        top = jnp.max(sc, axis=-1, keepdims=True)
+        e = jnp.exp(sc - top)
+        return e * (1.0 / jnp.sum(e, axis=-1, keepdims=True))
+
+    def attention(s, b):
+        rows = rows_of(b)
+
+        @pl.loop(0, 4)
+        def _(i):
+            cols = lanes(i)
+            q, k, v = (qkvs[s, t, rows, cols] for t in range(3))
+            parts = [dot(softmax(pick(h, q), k).astype(BF), v, 1, 0) for h in range(2)]
+            mixs[s, rows, cols] = jnp.where(left, parts[0], parts[1]).astype(BF)
+
+    def out_project(s, b, k):
+        @pl.loop(0, 4)
+        def _(n):
+            cols = lanes(n * 2, 256)
+            ys[rows_of(b), cols] = dot(mixs[s, rows_of(b), :], wout[s, :, cols], 1, 0).astype(BF)
+            y_start(k, b, n)
+
+    def middle(s, b, k):
+        shift, gain2, shift2 = row(s, 2), row(s, 3), row(s, 4)
+
+        @chunks(b)
+        def _(rows):
+            v = xs[s, rows, :].astype(F32) + y_sum(k, rows) + shift
+            if s == 0:
+                mid[rows, :] = v
+            else:
+                gb[0, rows, :] = v.astype(BF)
+            nrm, inv = norm_chunk(v)
+            nrm2s[s, rows, :] = nrm.astype(BF)
+            inv2s[s, rows, :] = jnp.broadcast_to(inv, (CH, 128))
+            low[rows, :] = (nrm * gain2 + shift2).astype(BF)
+
+    def up_project(s, b):
+        @pl.loop(0, 8)
+        def _(n):
+            cols = lanes(n * 2, 256)
+            acc[...] = dot(low[rows_of(b), :], wup[s, :, cols], 1, 0)
+            at = pl.ds(pl.multiple_of(lax.rem(n, 4) * 256, 256), 256)
+            bias = jnp.where(n < 4, vec[s, 7:8, at], vec[s, 8:9, at])
+
+            @pl.loop(0, LP // 16)
+            def _(i):
+                rows = pl.ds(pl.multiple_of(b * LP + i * 16, 16), 16)
+                a = acc[pl.ds(pl.multiple_of(i * 16, 16), 16), :] + bias
+                phi = 0.5 * (1.0 + lax.erf(a * (2.0 ** -0.5)))
+                dens = jnp.exp(-0.5 * a * a) * ((2.0 * math.pi) ** -0.5)
+                gels[s, rows, cols] = (a * phi).astype(BF)
+                slps[s, rows, cols] = (phi + a * dens).astype(BF)
+
+    def down_project(s, b, k, send):
+        @pl.loop(0, 4)
+        def _(n):
+            cols = lanes(n * 2, 256)
+            y_src(k)[rows_of(b), cols] = dot(gels[s, rows_of(b), :], wdown[s, :, cols], 1, 0).astype(BF)
+            if send:
+                y_start(k, b, n)
+
+    def finish(s, b, k, dst):
+        shift, alive = row(s, 5), alive_of(b)
+
+        @chunks(b)
+        def _(rows):
+            base = mid[rows, :] if s == 0 else slps[1, rows, 1024:2048].astype(F32)
+            dst[rows, :] = ((base + y_sum(k, rows) + shift) * alive).astype(BF)
+
+    def keep_middle(b):
+        @chunks(b)
+        def _(rows):
+            slps[1, rows, 1024:2048] = gb[0, rows, :]
+
+    def emit(which, s, src):
+        target = (act_out, gin_out)[which].at[c]
+        q = which * 2 + s
+
+        @pl.when(c == s)
+        def _():
+            pltpu.make_async_copy(src, target, osem.at[q]).start()
+
+        @pl.when(c != s)
+        def _():
+            remote(src, target, osem_s.at[q], osem_r.at[q], to_c).start()
+
+    def emit_sent(which, s, src):
+        target = (act_out, gin_out)[which].at[c]
+        q = which * 2 + s
+
+        @pl.when(c == s)
+        def _():
+            pltpu.make_async_copy(src, target, osem.at[q]).wait()
+
+        @pl.when(c != s)
+        def _():
+            remote(src, target, osem_s.at[q], osem_r.at[q], to_c).wait_send()
+
+    def emit_got(which, s, src):
+        target = (act_out, gin_out)[which].at[1 - c]
+        q = which * 2 + s
+
+        @pl.when(c == s)
+        def _():
+            remote(src, target, osem_s.at[q], osem_r.at[q], to_c).wait_recv()
+
+    def relower(s, b):
+        gain2, shift2 = row(s, 3), row(s, 4)
+
+        @chunks(b)
+        def _(rows):
+            low[rows, :] = (nrm2s[s, rows, :].astype(F32) * gain2 + shift2).astype(BF)
+
+    def colsum(v):
+        return jnp.sum(v, axis=0, keepdims=True)
+
+    def sum_rows(ref_slice, width):
+        def step(i, tot):
+            rows = pl.ds(pl.multiple_of(i * CH, CH), CH)
+            return tot + colsum(ref_slice(rows).astype(F32))
+
+        return lax.fori_loop(0, R // CH, step, jnp.zeros((1, width), F32))
+
+    def total(s, r, b, v):
+        sv[s, r : r + 1, :] = v if b == 0 else sv[s, r : r + 1, :] + v
+
+    def grad_gelu(s, b):
+        @pl.loop(0, 8)
+        def _(n):
+            cols = lanes(n * 2, 256)
+            rows_w = pl.ds(pl.multiple_of(n * 256, 256), 256)
+            a = dot(gb[s, rows_of(b), :], wdown[s, rows_w, :], 1, 1)
+            gpre[rows_of(b), cols] = (a * slps[s, rows_of(b), cols].astype(F32)).astype(BF)
+
+    def grad_mlp_biases(s):
+        sv[s, 5:6, :] = sum_rows(lambda r: gb[s, r, :], 1024)
+        sv[s, 7:8, :] = sum_rows(lambda r: gpre[r, 0:1024], 1024)
+        sv[s, 8:9, :] = sum_rows(lambda r: gpre[r, 1024:2048], 1024)
+
+    def grad_down(s):
+        @pl.loop(0, 8)
+        def _(i):
+            cols = lanes(i * 2, 256)
+            rows_w = pl.ds(pl.multiple_of(i * 256, 256), 256)
+            wdown[s, rows_w, :] = dot(gels[s, :, cols], gb[s], 0, 0).astype(BF)
+
+    def grad_low_two(s, b, k):
+        @pl.loop(0, 4)
+        def _(n):
+            cols = lanes(n * 2, 256)
+            rows_w = pl.ds(pl.multiple_of(n * 256, 256), 256)
+            ys[rows_of(b), cols] = dot(gpre[rows_of(b), :], wup[s, rows_w, :], 1, 1).astype(BF)
+            y_start(k, b, n)
+
+    def grad_up(s):
+        @pl.loop(0, 4)
+        def _(i):
+            cols = lanes(i * 2, 256)
+            rows_w = pl.ds(pl.multiple_of(i * 256, 256), 256)
+            for q in range(2):
+                wup[s, rows_w, q * 1024 : q * 1024 + 1024] = dot(
+                    low[:, cols], gpre[:, q * 1024 : q * 1024 + 1024], 0, 0
+                ).astype(BF)
+
+    def loop_sums(b, count, step):
+        zero = jnp.zeros((1, 1024), F32)
+
+        def body(i, tots):
+            return step(pl.ds(pl.multiple_of(b * LP + i * CH, CH), CH), tots)
+
+        return lax.fori_loop(0, LP // CH, body, (zero,) * count)
+
+    def grad_middle(s, b, k):
+        gain = row(s, 3)
+
+        def step(rows, tots):
+            t_gain, t_shift, t_out = tots
+            g2 = y_sum(k, rows)
+            nrm = nrm2s[s, rows, :].astype(F32)
+            t = g2 * gain
+            m1 = jnp.mean(t, axis=-1, keepdims=True)
+            m2 = jnp.mean(t * nrm, axis=-1, keepdims=True)
+            inv = inv2s[s, rows, :][:, 0:1]
+            gm = gb[s, rows, :].astype(F32) + inv * (t - m1 - nrm * m2)
+            mid[rows, :] = gm
+            ga = gm.astype(BF)
+            low[rows, :] = ga
+            return (t_gain + colsum(g2 * nrm), t_shift + colsum(g2), t_out + colsum(ga.astype(F32)))
+
+        for r, v in zip((3, 4, 2), loop_sums(b, 3, step)):
+            total(s, r, b, v)
+
+    def grad_mixed(s, b):
+        @pl.loop(0, 2)
+        def _(n):
+            cols = lanes(n * 2, 256)
+            rows_w = pl.ds(pl.multiple_of(n * 256, 256), 256)
+            gpre[rows_of(b), cols] = dot(low[rows_of(b), :], wout[s, rows_w, :], 1, 1).astype(BF)
+
+    def grad_out(s):
+        @pl.loop(0, 2)
+        def _(i):
+            cols = lanes(i * 2, 256)
+            rows_w = pl.ds(pl.multiple_of(i * 256, 256), 256)
+            wout[s, rows_w, :] = dot(mixs[s, :, cols], low[...], 0, 0).astype(BF)
+
+    def grad_attention(s, b):
+        rows = rows_of(b)
+
+        @pl.loop(0, 4)
+        def _(i):
+            cols = lanes(i)
+            q, k, v = (qkvs[s, t, rows, cols] for t in range(3))
+            gm = gpre[rows, cols]
+            res = []
+            for h in range(2):
+                probs = softmax(pick(h, q), k)
+                gp = dot(pick(h, gm), v, 1, 1)
+                gv = dot(probs.astype(BF), gm, 0, 0)
+                gs = (probs * (gp - jnp.sum(probs * gp, axis=-1, keepdims=True))).astype(BF)
+                gq = dot(gs, k, 1, 0) * (64.0 ** -0.5)
+                gk = dot(gs, q, 0, 0) * (64.0 ** -0.5)
+                res.append((gq, gk, gv))
+            for t in range(3):
+                gqkv[t, rows, cols] = jnp.where(left, res[0][t], res[1][t]).astype(BF)
+
+    def grad_qv_bias(s):
+        sv[s, 6:7, 0:512] = sum_rows(lambda r: gqkv[0, r, :], 512)
+        sv[s, 6:7, 512:1024] = sum_rows(lambda r: gqkv[2, r, :], 512)
+
+    def grad_lowered(s, b, k):
+        rows = rows_of(b)
+
+        @pl.loop(0, 4)
+        def _(n):
+            cols = lanes(n * 2, 256)
+            rows_w = pl.ds(pl.multiple_of(n * 256, 256), 256)
+            a = dot(gqkv[0, rows, :], wqkv[0][s, rows_w, :], 1, 1)
+            a = a + dot(gqkv[1, rows, :], wqkv[1][s, rows_w, :], 1, 1)
+            a = a + dot(gqkv[2, rows, :], wqkv[2][s, rows_w, :], 1, 1)
+            ys[rows, cols] = a.astype(BF)
+            y_start(k, b, n)
+
+    def grad_qkv(s, t):
+        @pl.loop(0, 4)
+        def _(i):
+            cols = lanes(i * 2, 256)
+            rows_w = pl.ds(pl.multiple_of(i * 256, 256), 256)
+            wqkv[t][s, rows_w, :] = dot(low[:, cols], gqkv[t], 0, 0).astype(BF)
+
+    def grad_stream(s, b, k, dst):
+        gain = row(s, 0)
+
+        def step(rows, tots):
+            t_gain, t_shift = tots
+            g1 = y_sum(k, rows)
+            nrm, inv = norm_chunk(xs[s, rows, :].astype(F32))
+            t = g1 * gain
+            m1 = jnp.mean(t, axis=-1, keepdims=True)
+            m2 = jnp.mean(t * nrm, axis=-1, keepdims=True)
+            dst[rows, :] = (mid[rows, :] + inv * (t - m1 - nrm * m2)).astype(BF)
+            return (t_gain + colsum(g1 * nrm), t_shift + colsum(g1))
+
+        for r, v in zip((0, 1), loop_sums(b, 2, step)):
+            total(s, r, b, v)
+
+    def add_rows(dst, src, count, chunk):
+        @pl.loop(0, count // chunk)
+        def _(i):
+            rows = pl.ds(pl.multiple_of(i * chunk, chunk), chunk)
+            dst[rows, :] = dst[rows, :] + src[rows, :]
+
+    def shape_of(m):
+        if m in BY_ROWS:
+            return 128, (16 if m == UP else 64)
+        return WIDTH[m] // 2, 128
+
+    def add_block(m, dst, src):
+        add_rows(dst, src, *shape_of(m))
+
+    def r_view(s, m, h):
+        return rbuf[m] if s == 1 else half(m, w[m], 1, h)
+
+    def x_view(s, m, k, col):
+        if m in X_FIRST:
+            return xbuf[m].at[s]
+        if s == 0:
+            return block(m, w[m], 1, at_dp(k, col), c)
+        at = pl.ds(k * 128, 128)
+        return xbuf[m].at[at, :] if m in BY_ROWS else xbuf[m].at[:, at]
+
+    def z_view(s, m, slot, col, place):
+        if s == 0:
+            return block(m, w[m], 1, place * 2 + (x if col == 0 else 1 - x), c)
+        return zbuf[m].at[col * 4 + slot]
+
+    def rs_c(s, m):
+        q = s * 6 + m - 1
+        if s == 0:
+            pl.semaphore_wait(free_c.at[m - 1], 1)
+        remote(half(m, w[m], s, 1 - c), r_view(s, m, c), rsem_cs.at[q], rsem_c.at[q], to_c).start()
+
+    def rs_sum(s, m):
+        q = s * 6 + m - 1
+        mine, got = half(m, w[m], s, c), r_view(s, m, 1 - c)
+        cp = remote(mine, got, rsem_cs.at[q], rsem_c.at[q], to_c)
+        cp.wait_recv()
+        cp.wait_send()
+        if s == 1:
+            pl.semaphore_signal(free_c.at[m - 1], inc=1, device_id=to_c, device_id_type=MESH)
+        rows = 1024 if m in BY_ROWS else WIDTH[m] // 2
+        add_rows(mine, got, rows, 16 if m not in (Q, K, V) else 64)
+
+    def rs_to_x(s, m):
+        if s == 0:
+            pl.semaphore_wait(free_x.at[m - 1], 1)
+        for k in (INNER, FAR, NEAR, SELF):
+            q = s * 6 + m - 1
+            b = block(m, w[m], s, at_dp(k, 1), c)
+            remote(b, x_view(s, m, k, 0), rsem_xs.at[q], rsem_x.at[rx[(s, m), k]], to_x).start()
+
+    def rs_from_x(s, m, k):
+        q = s * 6 + m - 1
+        b = block(m, w[m], s, at_dp(k, 0), c)
+        got = x_view(s, m, k, 1)
+        remote(b, got, rsem_xs.at[q], rsem_x.at[rx[(s, m), k]], to_x).wait_recv()
+        if k == SELF:
+            wait_bytes(m, 4, rsem_xs.at[q])
+        add_block(m, b, got)
+
+    def x_freed(m):
+        pl.semaphore_signal(free_x.at[m - 1], inc=1, device_id=to_x, device_id_type=MESH)
+
+    def z_ready(m):
+        @pl.when(inner)
+        def _():
+            pl.semaphore_wait(free_z.at[m - 1], 3)
+
+        @pl.when(jnp.logical_not(inner))
+        def _():
+            pl.semaphore_wait(free_z.at[m - 1], 1)
+
+    def rs_to_z(s, m, k, col):
+        q = s * 6 + m - 1
+        b = block(m, w[m], s, at_dp(k, col), c)
+        if k == NEAR:
+            remote(b, z_view(s, m, 0, col, z), rsem_zs.at[q, col], rsem_z.at[rz[(s, m), col * 4]], to_z(near)).start()
+        else:
+
+            @pl.when(jnp.logical_not(inner))
+            def _():
+                remote(b, z_view(s, m, k, col, places[k]), rsem_zs.at[q, col], rsem_z.at[rz[(s, m), col * 4 + k]], to_z(near)).start()
+
+    def rs_pass(s, m, k, col):
+        q = s * 6 + m - 1
+
+        @pl.when(inner)
+        def _():
+            b = block(m, w[m], s, at_dp(k, col), c)
+            got = z_view(s, m, k, col, places[k])
+            remote(b, got, rsem_zs.at[q, col], rsem_z.at[rz[(s, m), col * 4 + k]], to_z(near)).wait_recv()
+            add_block(m, b, got)
+            remote(b, z_view(s, m, 1, col, places[k]), rsem_zs.at[q, col], rsem_z.at[rz[(s, m), col * 4 + 1]], to_z(places[k])).start()
+
+    def z_arrived(s, m, col):
+        q = s * 6 + m - 1
+        got = [z_view(s, m, 0, col, near), z_view(s, m, 1, col, z)]
+        for slot in range(2):
+            remote(got[slot], got[slot], rsem_zs.at[q, col], rsem_z.at[rz[(s, m), col * 4 + slot]], to_z(near)).wait_recv()
+        return got
+
+    def z_sent(s, m, col):
+        wait_bytes(m, 3, rsem_zs.at[s * 6 + m - 1, col])
+
+    def z_freed(m):
+        for k in (NEAR, INNER):
+            pl.semaphore_signal(free_z.at[m - 1], inc=1, device_id=to_z(places[k]), device_id_type=MESH)
+
+    def rs_fold(s, m):
+        q = s * 6 + m - 1
+        b = block(m, w[m], s, at_dp(SELF, 1), c)
+        for got in z_arrived(s, m, 1):
+            add_block(m, b, got)
+        remote(b, xbuf[m].at[s], rsem_xs.at[q], rsem_x.at[rx[(s, m), 0]], to_x).start()
+
+    def f_target(m):
+        n = WIDTH[m] // 2
+        at = pl.ds(pl.multiple_of(c * n, n), n)
+        if m in (Q, K, V):
+            return gqkv_out.at[m - 1, :, at]
+        if m == UP:
+            return gup_out.at[:, at]
+        return (gout_out if m == OUT else gdown_out).at[at, :]
+
+    def rs_f(s, m):
+        q = s * 6 + m - 1
+        mine = block(m, w[m], s, me, c)
+        parts = [mine] + z_arrived(s, m, 0)
+        if m in X_FIRST:
+            cp = remote(mine, xbuf[m].at[s], rsem_xs.at[q], rsem_x.at[rx[(s, m), 0]], to_x)
+            cp.wait_recv()
+            cp.wait_send()
+            parts.append(xbuf[m].at[s])
+        count, chunk = shape_of(m)
+        chunk = min(chunk, 64)
+
+        @pl.loop(0, count // chunk)
+        def _(i):
+            rows = pl.ds(pl.multiple_of(i * chunk, chunk), chunk)
+            a = parts[0][rows, :].astype(F32)
+            for part in parts[1:]:
+                a = a + part[rows, :].astype(F32)
+            fbuf[m][rows, :] = a
+
+        for col in range(2) if m in X_FIRST else (0,):
+            z_sent(s, m, col)
+        if s == 1:
+            z_freed(m)
+
+        @pl.when(c == s)
+        def _():
+            pltpu.make_async_copy(fbuf[m], f_target(m), rsem_fs.at[q]).start()
+
+        @pl.when(c != s)
+        def _():
+            remote(fbuf[m], f_target(m), rsem_fs.at[q], rsem_f.at[q], to_c).start()
+
+    def rs_f_sent(s, m):
+        q = s * 6 + m - 1
+
+        @pl.when(c == s)
+        def _():
+            pltpu.make_async_copy(fbuf[m], f_target(m), rsem_fs.at[q]).wait()
+
+        @pl.when(c != s)
+        def _():
+            remote(fbuf[m], f_target(m), rsem_fs.at[q], rsem_f.at[q], to_c).wait_send()
+
+    def rs_end(s, m):
+        q = s * 6 + m - 1
+
+        @pl.when(c == s)
+        def _():
+            remote(fbuf[m], fbuf[m], rsem_fs.at[q], rsem_f.at[q], to_c).wait_recv()
+
+    def vec_copies(i):
+        if i == 0:
+            return [remote(sv.at[1 - c], svc, vsem_s.at[0], vsem.at[0], to_c)]
+        if i == 1:
+            return [remote(sv.at[c], svx, vsem_s.at[1], vsem.at[1], to_x)]
+        if i == 2:
+            return [
+                remote(svc, svz.at[j - 1], vsem_s.at[1 + j], vsem.at[1 + j], to_z(lax.rem(z + j, Z)))
+                for j in range(1, Z)
+            ]
+        return [pltpu.make_async_copy(sv.at[c], gvec_out, isem.at[2])]
+
+    def vec_step(i):
+        if i:
+            for cp in vec_copies(i - 1):
+                cp.wait_recv()
+                cp.wait_send()
+        if i == 1:
+            sv[c] = sv[c] + svc[...]
+        if i == 2:
+            svc[...] = sv[c] + svx[...]
+        if i == 3:
+            sv[c] = svc[...] + svz[0] + svz[1] + svz[2]
+        for cp in vec_copies(i):
+            cp.start()
+
+    clock = Clock()
+    size = {SMALL: 8e3, Q: 131e3, K: 131e3, V: 131e3, OUT: 131e3, UP: 524e3, DOWN: 524e3}
+    RATE = 88e3
+    HOP = 1.8
+    free = {"x": 0.0, "z": 0.0, "y": 0.0}
+    got = {}
+
+    def link(name, nbytes):
+        free[name] = max(free[name], clock.now) + nbytes / RATE
+        return free[name] + HOP
+
+    in_x = pltpu.make_async_copy(x_ref.at[c], ys, isem.at[0])
+    in_g = pltpu.make_async_copy(cot_ref.at[c], gpre.at[:, pl.ds(0, 1024)], isem.at[1])
+    in_x.start()
+    in_g.start()
+
+    order = (SMALL, Q, K, V, OUT, UP, DOWN)
+    for s in range(2):
+        for m in order:
+            ag_share(s, m)
+    clock.now = 2.0
+
+    def plan_gather(s, m):
+        x_first = m in X_FIRST
+
+        def at_x(k):
+            ag_x(s, m, k)
+            got[s, m] = got.get((s, m), 0) + 1
+            if x_first:
+                along_z(1)
+
+        def at_z(k, col):
+            ag_z(s, m, k, col)
+            if x_first:
+                got[s, m] = got.get((s, m), 0) + 1
+            else:
+                clock.add(link("x", size[m]), functools.partial(at_x, k))
+
+        def along_z(col):
+            begin = max(free["z"], clock.now)
+            t = size[m] / RATE
+            free["z"] = begin + 3 * t
+            for k in (NEAR, INNER, FAR):
+                clock.add(begin + k * t + (HOP if k == NEAR else 2 * HOP), functools.partial(at_z, k, col))
+
+        def own():
+            if not x_first:
+                ag_shared(s, m)
+            ag_own_z(s, m, 0)
+            along_z(0)
+            if not x_first:
+                ag_to_x(s, m, SELF)
+                clock.add(link("x", size[m]), functools.partial(at_x, SELF))
+
+        def early():
+            ag_shared(s, m)
+            ag_to_x(s, m, SELF)
+            clock.add(max(link("x", size[m]), z_begin[s, m] - LEAD + 0.1), functools.partial(at_x, SELF))
+
+        if x_first:
+            clock.add(x_begin[s, m], early)
+        clock.add(max(z_begin[s, m] - LEAD, 2.0), own)
+
+    LEAD = 5.0
+    z_begin, x_begin, at = {}, {}, 3.0
+    for s in range(2):
+        for m in order:
+            z_begin[s, m] = at
+            at += size[m] / RATE * (6 if m in X_FIRST else 3)
+            x_begin[s, m] = max(2.0, z_begin[s, m] - 14.0)
+    for s in range(2):
+        for m in order:
+            plan_gather(s, m)
+
+    def need(s, m):
+        clock.drain(lambda: got.get((s, m), 0) == (7 if m in X_FIRST else 4))
+        clock.now += 1.5
+        ag_need(s, m)
+
+    def y_sent():
+        return link("y", 426e3 * 2) + 1.0
+
+    passed = set()
+
+    def reduce(s, m):
+        x_first = m in X_FIRST
+        t = size[m] / RATE
+        order = (INNER, FAR, NEAR)
+
+        def z_start(k, col):
+            rs_to_z(s, m, k, col)
+            ready = link("z", size[m])
+            if k != NEAR:
+                clock.add(ready, functools.partial(z_pass, k, col), 0.4)
+
+        def z_pass(k, col):
+            rs_pass(s, m, k, col)
+            done.append((k, col))
+            if len([d for d in done if d[1] == col]) == 2:
+                ready = max(clock.now, free["z"] - 2 * t) + 2 * t + 2 * HOP
+                if x_first and col == 1:
+                    clock.add(ready, fold, 0.4)
+                elif not x_first:
+                    clock.add(ready, finish_sum, 0.6)
+
+        done = []
+
+        def fold():
+            rs_fold(s, m)
+            clock.add(max(link("x", size[m]), clock.now + 2.0), finish_sum, 0.6)
+
+        def sum_step():
+            rs_sum(s, m)
+            passed.add(("c", s, m))
+            if x_first:
+                if s == 0:
+                    clock.drain(lambda: ("z", m) in passed)
+                    z_ready(m)
+                for col in (1, 0):
+                    for k in order:
+                        z_start(k, col)
+            else:
+                if s == 0:
+                    clock.drain(lambda: ("x", m) in passed)
+                rs_to_x(s, m)
+                for k in order + (SELF,):
+                    clock.add(link("x", size[m]), functools.partial(from_x, k), 0.3)
+
+        def from_x(k):
+            rs_from_x(s, m, k)
+            if k == SELF:
+                done.append((SELF, -1))
+                if s == 1:
+                    x_freed(m)
+                    passed.add(("x", m))
+                return
+            if k == INNER and s == 0:
+                clock.drain(lambda: ("z", m) in passed)
+                z_ready(m)
+            z_start(k, 0)
+
+        def finish_sum():
+            clock.drain(lambda: ready_to_finish())
+            if s == 0:
+                rs_f_sent(1, m)
+            rs_f(s, m)
+            if s == 1:
+                passed.add(("z", m))
+
+        def ready_to_finish():
+            return x_first or (SELF, -1) in done
+
+        if s == 0:
+            clock.drain(lambda: ("c", 1, m) in passed)
+        rs_c(s, m)
+        clock.add(clock.now + 4 * size[m] / 500e3 + 2.0, sum_step, 0.8)
+
+    for i in range(5):
+        clock.flush(clock.now)
+        clock.now += 0.4
+    in_x.wait()
+    in_g.wait()
+    for b in range(2):
+        clock.run(0.6, unweave, ys, xs.at[0], b, None)
+    for b in range(2):
+        clock.run(0.6, unweave, gpre, gb.at[1], b, alive_of(b))
+    y_at = {}
+    for s in range(2):
+        last = s == 1
+        need(s, SMALL)
+        unpack_small(s)
+        for b in range(2):
+            if last:
+                clock.wait(y_at[1, b], y_wait, 1, b)
+                clock.run(1.0, finish, 0, b, 1, xs.at[1])
+                if b == 1:
+                    emit(0, 0, xs.at[1])
+            clock.run(2.3, ln1, s, b)
+            if b == 0:
+                for m in (Q, K, V):
+                    need(s, m)
+            clock.run(1.4, project, s, b)
+            clock.run(3.6, attention, s, b)
+            if b == 0:
+                need(s, OUT)
+            clock.run(0.7, out_project, s, b, s * 2)
+            y_at[s * 2, b] = y_sent()
+        for b in range(2):
+            clock.wait(y_at[s * 2, b], y_wait, s * 2, b)
+            clock.run(2.5, middle, s, b, s * 2)
+            if b == 0:
+                need(s, UP)
+            clock.run(2.7, up_project, s, b)
+        need(s, DOWN)
+        if not last:
+            for b in range(2):
+                clock.run(1.5, down_project, 0, b, 1, True)
+                y_at[1, b] = y_sent()
+
+    for s in range(2):
+        for m in order:
+            ag_sent(s, m)
+    for s in (1, 0):
+        k = 3 if s == 1 else 5
+        for b in range(2):
+            if s == 0:
+                clock.wait(y_at[4, b], y_wait, 4, b)
+                clock.run(3.5, grad_stream, 1, b, 4, gb.at[0])
+                if b == 1:
+                    emit(1, 1, gb.at[0])
+            clock.run(2.2, grad_gelu, s, b)
+            clock.run(1.5, grad_low_two, s, b, k)
+            y_at[k, b] = y_sent()
+        if s == 0:
+            for b in range(2):
+                clock.run(0.5, relower, 0, b)
+        clock.run(3.0, grad_up, s)
+        reduce(s, UP)
+        if s == 1:
+            for b in range(2):
+                clock.run(0.3, keep_middle, b)
+                clock.run(1.5, down_project, 1, b, 7, False)
+        clock.run(3.8, grad_down, s)
+        reduce(s, DOWN)
+        clock.run(1.0, grad_mlp_biases, s)
+        for b in range(2):
+            clock.wait(y_at[k, b], y_wait, k, b)
+            clock.run(1.6, grad_middle, s, b, k)
+            clock.run(0.5, grad_mixed, s, b)
+            if b == 1:
+                clock.run(0.9, grad_out, s)
+                reduce(s, OUT)
+            clock.run(5.1, grad_attention, s, b)
+            clock.run(1.2, grad_lowered, s, b, k + 1)
+            y_at[k + 1, b] = y_sent()
+        for b in range(2):
+            clock.run(2.3, ln1, s, b)
+        for t in range(3):
+            clock.run(1.4, grad_qkv, s, t)
+            reduce(s, Q + t)
+        clock.run(0.5, grad_qv_bias, s)
+    for b in range(2):
+        clock.wait(y_at[6, b], y_wait, 6, b)
+        clock.run(3.5, grad_stream, 0, b, 6, low)
+    emit(1, 0, low)
+    for i in range(4):
+        clock.add(clock.now + 3.0 * i, functools.partial(vec_step, i), 0.5)
+    for b in range(2):
+        for n in range(4):
+            y_start(7, b, n)
+        y_at[7, b] = y_sent()
+    for b in range(2):
+        clock.wait(y_at[7, b], y_wait, 7, b)
+        clock.run(1.0, finish, 1, b, 7, gb.at[1])
+    emit(0, 1, gb.at[1])
+    clock.drain(lambda: not clock.queue)
+    for cp in vec_copies(3):
+        cp.wait()
+    for m in MATS:
+        rs_f_sent(0, m)
+    for s in range(2):
+        for m in MATS:
+            rs_end(s, m)
+    emit_sent(0, 0, xs.at[1])
+    emit_sent(0, 1, gb.at[1])
+    emit_sent(1, 1, gb.at[0])
+    emit_sent(1, 0, low)
+    for which in range(2):
+        for s in range(2):
+            emit_got(which, s, low)
+
+
+def run_kernel(small, qkv, out, up, down, xin, cot, live):
+    any_spec = pl.BlockSpec(memory_space=pl.ANY)
+    V = pltpu.VMEM
+    D_ = pltpu.SemaphoreType.DMA
+    REG = pltpu.SemaphoreType.REGULAR
+    S = jax.ShapeDtypeStruct
+    mats = ((1024, 512), (1024, 512), (1024, 512), (512, 1024), (1024, 2048), (2048, 1024))
+    by_rows = (True, True, True, False, True, False)
+    first = (False, True, False, True, False, False)
+
+    def halved(shape, rows, cut):
+        return (shape[0] // cut, shape[1] // 2) if rows else (shape[0] // 2, shape[1] // cut)
+
+    scratch = [V((2, 8, 32, 128), BF)]
+    scratch += [V((2,) + shape, BF) for shape in mats]
+    scratch += [V(halved(shape, rows, 1), BF) for shape, rows in zip(mats, by_rows)]
+    scratch += [
+        V((2,) + halved(shape, rows, 8) if f else halved(shape, rows, 2), BF)
+        for shape, rows, f in zip(mats, by_rows, first)
+    ]
+    scratch += [V((8 if f else 4,) + halved(shape, rows, 8), BF) for shape, rows, f in zip(mats, by_rows, first)]
+    scratch += [V(halved(shape, rows, 8), F32) for shape, rows in zip(mats, by_rows)]
+    scratch += [
+        V((2, R, 1024), BF), V((2, 3, R, 512), BF), V((2, R, 512), BF), V((2, R, 1024), BF),
+        V((2, R, 2048), BF), V((2, R, 2048), BF), V((2, R, 128), F32),
+        V((R, 1024), BF), V((R, 1024), F32), V((2, R, 1024), BF), V((R, 2048), BF), V((3, R, 512), BF),
+        V((R, 1024), BF), V((2, R, 1024), BF), V((LP, 256), F32),
+        V((2, 16, 1024), F32), V((2, 16, 1024), F32), V((16, 1024), F32), V((16, 1024), F32), V((3, 16, 1024), F32),
+        D_((14,)), D_((14, 2)), D_((54,)), D_((44,)),
+        D_((12,)), D_((12,)), D_((12,)), D_((36,)), D_((12, 2)), D_((64,)), D_((12,)), D_((12,)),
+        D_((16,)), D_((16,)), D_((4,)), D_((4,)), D_((4,)), D_((3,)), D_((5,)), D_((5,)),
+        REG((6,)), REG((6,)), REG((6,)),
+    ]
+    return pl.pallas_call(
+        kernel,
+        out_shape=[
+            S((2, R, 1024), BF), S((2, R, 1024), BF), S((3, 128, 512), F32), S((512, 128), F32),
+            S((128, 2048), F32), S((2048, 128), F32), S((16, 1024), F32),
+        ],
+        in_specs=[any_spec] * 7 + [pl.BlockSpec(memory_space=pltpu.SMEM)],
+        out_specs=[any_spec] * 7,
+        scratch_shapes=scratch,
+        compiler_params=pltpu.CompilerParams(
+            collective_id=1, has_side_effects=True, vmem_limit_bytes=67043328
+        ),
+        name="sections",
+    )(small, qkv, out, up, down, xin, cot, live)
+
+
+def local_fast(images, cotangent, live_count, ln1_gain, ln1_bias, qkv_weight, qv_bias, out_weight, out_bias,
+               ln2_gain, ln2_bias, up_weight, up_bias, down_weight, down_bias):
+    d = lax.axis_index("dp")
+
+    def woven(a):
+        a = jnp.transpose(a, (0, 2, 1, 3)).reshape(2, 2 * L, 1024)
+        return jnp.pad(a, ((0, 0), (0, R - 2 * L), (0, 0)))
+
+    def spread(a, width):
+        n = a.shape[-1]
+        z8 = jnp.where((jnp.arange(8) == d)[:, None], a[..., None, :], jnp.zeros_like(a[..., None, :]))
+        return z8.reshape(a.shape[:-1] + (8 * n,))
+
+    at = lax.broadcasted_iota(jnp.int32, (32, 128), 0)
+    small = jnp.pad(spread(qv_bias[0], 64).reshape(8, 128), ((6, 18), (0, 0)))
+    small = small + jnp.pad(spread(up_bias[0], 256).reshape(16, 128), ((14, 2), (0, 0)))
+    for i, v in enumerate((ln1_gain, ln1_bias, out_bias, ln2_gain, ln2_bias, down_bias)):
+        small = jnp.where(at == i, v, small)
+    act, gin, gqkv, gout, gup, gdown, gvec = run_kernel(
+        small, qkv_weight[0], out_weight[0], up_weight[0], down_weight[0], woven(images), woven(cotangent), live_count
+    )
+
+    def cut(v, axis, n):
+        return lax.dynamic_slice_in_dim(v, d * n, n, axis=axis)
+
+    act = act.reshape(2, 2, LP, 1024)[None, :, :, :L]
+    gin = gin.reshape(2, 2, LP, 1024)[None, :, :, :L]
+    vecs = cut(gvec[:6], 1, 128)
+    qv = cut(gvec[6].reshape(2, 8, 64), 2, 8)
+    upb = cut(gvec[7:9].reshape(8, 256), 1, 32)
+    return (
+        act, gin, vecs[0:1], vecs[1:2], gqkv[None], qv[None], gout[None], vecs[2:3], vecs[3:4], vecs[4:5],
+        gup[None], upb[None], gdown[None], vecs[5:6],
+    )
+
+
 def solution(mesh):
+    fast = dict(mesh.shape) == {"section": 2, "dp": 8, "mp": 2}
     return jax.shard_map(
-        local,
+        local_fast if fast else local,
         mesh=mesh,
         in_specs=(
             P(None, "dp", None, None),

time: 1210 us -> 361 us (0.30)
  waiting for transfers between devices: 669 us -> 0 us
  Pallas kernels: 0 us -> 332 us
  matrix products: 222 us -> 0 us
  local copies, waits for them, and re-layouts: 137 us -> 25.1 us
  other arithmetic: 78.5 us -> 2.98 us
  blocking collectives: 71.1 us -> 0 us
  between operations: 16.9 us -> 0.76 us
    pallas_call x0 -> x1, Pallas kernels: none -> 332 us  [run_kernel(): pl.pallas_call(kernel, out_shape=[S((2, R, 1024), BF), S((2, R, 1024), BF...]
    psum x9 -> x0, waiting for transfers between devices: 283 us -> none  [both_halves(): return lax.psum(partial.astype(jnp.bfloat16), 'mp').astype(jnp.float32)]
    dot_general x57 -> x0, matrix products: 222 us -> none  [the longest x3 37.7 us: forward(): jnp.einsum('blf,fd->bld', gelu_out, down_mat, preferred_element_type=jnp....]
    all_gather x4 -> x0, waiting for transfers between devices: 186 us -> none  [gather_all(): lax.all_gather(piece, 'dp', axis=axis, tiled=True)]
    unnamed x20 -> x0, waiting for transfers between devices: 110 us -> none
    reduce_scatter x1 -> x0, waiting for transfers between devices: 87.8 us -> none  [scatter_all(): lax.psum_scatter(totals[index].astype(jnp.bfloat16), 'dp', scatter_dimens...]
    unnamed x407 -> x21, local copies, waits for them, and re-layouts: 79.7 us -> 10.5 us
    reduce_sum x29 -> x0, other arithmetic: 51 us -> none  [the longest x9 17.5 us: norm_parts(): centered = stream - jnp.mean(stream, axis=-1, keepdims=True)]
  transfers between devices with their start and end apart: 21 -> 0, of which waited for: 16 -> 0; matrix products, arithmetic and copies ran while one was open for 20% -> 0% of each run, Pallas kernels for 0% -> 0%
where the time goes in v2:
time: 361 us
  Pallas kernels  332 us (92%)
  local copies, waits for them, and re-layouts  25.1 us (7%)
    pallas_call x1, Pallas kernels, run_kernel(): pl.pallas_call(kernel, out_shape=[S((2, R, 1024), BF), S((2, R, 1024), BF...  332 us
    unnamed x21, local copies, waits for them, and re-layouts  10.5 us

profile of v2, /device:TPU:0, one launch (start us, length us, event | category | flops | bytes accessed | tf_op | source)
XLA Modules:
  0.0 360.6 jit_solution(9189489080595398346)
XLA Ops:
  0.7 0.8 broadcast_select_fusion
  1.4 0.1 select_n.45
  1.5 0.8 broadcast_select_fusion.1
  2.3 0.1 select_n.47
  2.4 1.4 select_select_fusion.small_ref
  3.8 3.1 copy.32
  6.9 0.4 copy.33
  7.4 0.0 copy-start
  7.4 1.4 pad.17.x_ref
  8.8 0.7 copy-done
  9.4 1.7 copy.34
  11.1 0.4 copy.35
  11.5 0.0 copy-start.6
  11.6 1.3 pad.18.cot_ref
  12.9 0.0 copy-done.6
  12.9 0.6 copy.36.live_ref
  13.5 331.8 %sections.1 = (bf16[2,416,1024]{2,1,0:T(8,128)(2,1)}, bf16[2,416,1024]{2,1,0:T(8,128)(2,1)}, f32[3,128,512]{2,1,0:T(8,128)}, f32[512,128]{1,0:T(8,128)}, f32[128...) custom-call(bf16[32,128]{1,0:T(8,128)(2,1)} %select_select_fusion.small_ref, bf16[3,128,512]{2,1,0:T(8,128)(2,1)} %bitcast.47, ...), custom_call_target="tpu_custom_call" | custom-call | tf_op jit(solution)/shard_map/sections/pallas_call | solution.py:1451
  345.3 0.8 slice.35
  346.1 0.5 fusion
  346.6 0.8 slice_reduce_fusion
  347.4 0.1 reshape_squeeze.3
  347.4 0.7 dynamic-slice_bitcast_fusion
  348.1 0.8 slice.42
  349.0 0.7 dynamic-slice_bitcast_fusion.1
  349.7 1.6 slice.45
  351.2 0.0 copy-start.1
  351.2 2.8 copy.43
  354.0 0.0 copy-done.1
  354.0 0.2 slice.44
  354.2 0.0 copy-start.4
  354.2 0.0 copy-start.5
  354.3 2.8 copy.44
  357.1 0.0 copy-start.3
  357.1 0.0 copy-done.4
  357.1 0.9 copy.49
  358.0 0.0 copy-done.5
  358.0 0.0 copy-start.2
  358.0 0.7 copy.50
  358.7 0.0 copy-done.3
  358.7 1.0 copy.51
  359.6 0.0 copy-done.2
  359.6 1.0 copy.52
  (6 shorter events, 0.0 us)
Async XLA Ops:
  7.4 2.0 copy-start
  11.5 1.4 copy-start.6
  351.2 2.8 copy-start.1
  354.2 2.8 copy-start.4
  354.2 3.7 %copy-start.5 = (f32[512,128]{1,0:T(8,128)S(1)}, f32[512,128]{1,0:T(8,128)}, u32[]{:S(2)}) copy-start(f32[512,128]{1,0:T(8,128)} %get-tuple-element.25) | copy-start | bytes 786436
  357.1 1.6 copy-start.3
  358.0 1.7 copy-start.2

commit v3 on v2

--- a/solution.py
+++ b/solution.py
@@ -446,22 +446,23 @@
 
 
 def kernel(
-    small_ref, qkv_ref, out_ref, up_ref, down_ref, x_ref, cot_ref, live_ref,
+    gain1_ref, shift1_ref, bias_o_ref, gain2_ref, shift2_ref, bias_d_ref, qv_ref, upb_ref,
+    qkv_ref, out_ref, up_ref, down_ref, x_ref, cot_ref, live_ref,
     act_out, gin_out, gqkv_out, gout_out, gup_out, gdown_out, gvec_out,
     wsmall, wq, wk, wv, wout, wup, wdown,
     rq, rk, rv, rout, rup, rdown, xq, xk, xv, xout, xup, xdown,
-    zq, zk, zv, zout, zup, zdown, fq, fk, fv, fout, fup, fdown,
-    xs, qkvs, mixs, nrm2s, gels, slps, inv2s,
-    low, mid, gb, gpre, gqkv, ys, yr, acc, vec, sv, svc, svx, svz,
+    zq, zk, zv, zout, fq, fk, fv, fout, fup, fdown,
+    xs, qkvs, mixs, nrm2s, gels, slps, stats,
+    low, mid, gb, gpre, gqkv, ys, yr, acc, vec, sv, svc, svx, svz, woven, stage, pack, raw, rawq, rawu,
     asem_s, asem_c, asem_z, asem_x, rsem_cs, rsem_c, rsem_xs, rsem_x, rsem_zs, rsem_z, rsem_fs, rsem_f,
-    ysem, ysem_s, osem, osem_r, osem_s, isem, vsem, vsem_s, free_c, free_x, free_z,
+    ysem, ysem_s, osem, osem_r, osem_s, isem, vsem, vsem_s, free_c, free_x, free_z, free_up, free_r, free_y,
 ):
-    shards = (small_ref, qkv_ref.at[0], qkv_ref.at[1], qkv_ref.at[2], out_ref, up_ref, down_ref)
+    shards = (pack, qkv_ref.at[0], qkv_ref.at[1], qkv_ref.at[2], out_ref, up_ref, down_ref)
     wqkv = (wq, wk, wv)
     w = (wsmall, wq, wk, wv, wout, wup, wdown)
     rbuf = (None, rq, rk, rv, rout, rup, rdown)
     xbuf = (None, xq, xk, xv, xout, xup, xdown)
-    zbuf = (None, zq, zk, zv, zout, zup, zdown)
+    zbuf = (None, zq, zk, zv, zout)
     fbuf = (None, fq, fk, fv, fout, fup, fdown)
 
     c = lax.axis_index("section")
@@ -509,7 +510,7 @@
 
     def wait_bytes(m, count, sem):
         if m == SMALL:
-            v = inv2s.at[0, pl.ds(0, 8 * count), :]
+            v = stats.at[pl.ds(0, 8 * count), :]
         else:
             v = wdown.at[:, pl.ds(0, count * WIDTH[m] // 32), :]
         pltpu.make_async_copy(v, v, sem).wait()
@@ -596,6 +597,37 @@
 
     def y_sum(k, rows):
         return y_src(k)[rows, :].astype(F32) + yr[k % 2, rows, :].astype(F32)
+
+    small_in = [
+        pltpu.make_async_copy(ref, raw.at[i], isem.at[2 + i])
+        for i, ref in enumerate((gain1_ref, shift1_ref, bias_o_ref, gain2_ref, shift2_ref, bias_d_ref))
+    ] + [pltpu.make_async_copy(qv_ref, rawq, isem.at[8]), pltpu.make_async_copy(upb_ref, rawu, isem.at[9])]
+
+    def pack_small():
+        for cp in small_in:
+            cp.wait()
+
+        def iota(shape, axis):
+            return lax.broadcasted_iota(jnp.int32, shape, axis)
+
+        def hot(test):
+            return jnp.where(test, 1.0, 0.0).astype(BF)
+
+        r = iota((32, 128), 0)
+        v = jnp.zeros((32, 128), F32)
+        for i in range(6):
+            v = jnp.where(r == i, raw[i].astype(F32), v)
+        for t in range(2):
+            for e in range(2):
+                pick_rows = hot(iota((32, 8), 1) == 2 * (iota((32, 8), 0) - 6 - 4 * t) + e)
+                spread = hot(iota((8, 128), 1) == e * 64 + me * 8 + iota((8, 128), 0))
+                rows = dot(pick_rows, rawq[t], 1, 0).astype(BF)
+                v = v + dot(rows, spread, 1, 0)
+        odd = me // 4
+        pick_rows = hot(2 * iota((32, 8), 1) + odd == iota((32, 8), 0) - 14)
+        spread = hot(iota((32, 128), 1) == lax.rem(me, 4) * 32 + iota((32, 128), 0))
+        v = v + dot(dot(pick_rows, rawu[...], 1, 0).astype(BF), spread, 1, 0)
+        pack[...] = v.astype(BF)
 
     def unpack_small(s):
         total = jnp.zeros((32, 128), F32)
@@ -614,27 +646,75 @@
 
     CH = 16
 
+    lane = lax.broadcasted_iota(jnp.int32, (1, 128), 1)
+    left = lane < 64
+    live_col = lax.broadcasted_iota(jnp.int32, (1, LP), 1) < L
+    INV2, MEAN1, INV1 = range(3)
+
+    def stat_at(s, which):
+        return 16 + 4 * s + which
+
+    def put_stats(rows, *pairs):
+        v = stats[rows, :]
+        for at, value in pairs:
+            v = jnp.where(lane == at, value, v)
+        stats[rows, :] = v
+
+    def stat(s, which, rows):
+        at = stat_at(s, which)
+        return stats[rows, :][:, at : at + 1]
+
     def norm_chunk(v):
         mean = jnp.mean(v, axis=-1, keepdims=True)
         cen = v - mean
         inv = lax.rsqrt(jnp.mean(cen * cen, axis=-1, keepdims=True) + EPS)
-        return cen * inv, inv
-
-    def chunks(b):
+        return cen * inv, mean, inv
+
+    def chunks(b, pair=1):
+        def at(i):
+            return pl.ds(pl.multiple_of(b * LP + i * CH, CH), CH)
+
         def wrap(body):
-            @pl.loop(0, LP // CH)
+            count = LP // CH
+
+            @pl.loop(0, count // pair)
             def _(i):
-                body(pl.ds(pl.multiple_of(b * LP + i * CH, CH), CH))
+                for j in range(pair):
+                    body(at(i * pair + j))
+
+            for j in range(count % pair):
+                body(at(count - 1 - j))
 
         return wrap
 
     def ln1(s, b):
         gain, shift = row(s, 0), row(s, 1)
 
+        @chunks(b, 2)
+        def _(rows):
+            nrm, mean, inv = norm_chunk(xs[s, rows, :].astype(F32))
+            put_stats(rows, (stat_at(s, MEAN1), mean), (stat_at(s, INV1), inv))
+            low[rows, :] = (nrm * gain + shift).astype(BF)
+
+    def norm1(s, rows):
+        return (xs[s, rows, :].astype(F32) - stat(s, MEAN1, rows)) * stat(s, INV1, rows)
+
+    def relow1(s, b, dst):
+        gain, shift = row(s, 0), row(s, 1)
+
         @chunks(b)
         def _(rows):
-            nrm, _ = norm_chunk(xs[s, rows, :].astype(F32))
-            low[rows, :] = (nrm * gain + shift).astype(BF)
+            dst[rows, :] = (norm1(s, rows) * gain + shift).astype(BF)
+
+    def load_woven(ref, sem, dst):
+        cp = pltpu.make_async_copy(ref.at[c], woven.at[pl.ds(0, L)], sem)
+        cp.start()
+        cp.wait()
+        woven[L:LP] = jnp.zeros((LP - L, 2, 1024), BF)
+
+        @pl.loop(0, LP // 16)
+        def _(i):
+            dst[pl.ds(pl.multiple_of(i * 32, 32), 32), 0:1024] = woven[pl.ds(i * 16, 16)].reshape(32, 1024)
 
     def unweave(src, dst, b, alive):
         r = lax.broadcasted_iota(jnp.int32, (LP, R), 0)
@@ -649,8 +729,22 @@
             cols = lanes(n * 2, 256)
             dst[rows_of(b), cols] = dot(take, src[:, cols], 1, 0).astype(BF)
 
+    def weave(src, tmp):
+        r = lax.broadcasted_iota(jnp.int32, (R, R), 0)
+        q = lax.broadcasted_iota(jnp.int32, (R, R), 1)
+        put = jnp.where(q == lax.rem(r, 2) * LP + r // 2, 1.0, 0.0).astype(BF)
+
+        @pl.loop(0, 4)
+        def _(n):
+            cols = lanes(n * 2, 256)
+            tmp[:, cols] = dot(put, src[:, cols], 1, 0).astype(BF)
+
+        @pl.loop(0, LP // 16)
+        def _(i):
+            woven[pl.ds(i * 16, 16)] = tmp[pl.ds(pl.multiple_of(i * 32, 32), 32), 0:1024].reshape(16, 2, 1024)
+
     def alive_of(b):
-        return jnp.where(live_ref[c, 0] > b, 1.0, 0.0)
+        return jnp.where(live_ref[c] > b, 1.0, 0.0)
 
     def project(s, b):
         for t in range(3):
@@ -663,18 +757,11 @@
                     a = a + vec[s, 6:7, pl.ds(pl.multiple_of(base + n * 256, 256), 256)]
                 qkvs[s, t, rows_of(b), cols] = a.astype(BF)
 
-    left = lax.broadcasted_iota(jnp.int32, (1, 128), 1) < 64
-    live_col = lax.broadcasted_iota(jnp.int32, (1, LP), 1) < L
-
     def pick(h, v):
         return jnp.where(left if h == 0 else jnp.logical_not(left), v, jnp.zeros_like(v))
 
-    def softmax(q, k):
-        sc = dot(q, k, 1, 1) * (64.0 ** -0.5)
-        sc = jnp.where(live_col, sc, -1e30)
-        top = jnp.max(sc, axis=-1, keepdims=True)
-        e = jnp.exp(sc - top)
-        return e * (1.0 / jnp.sum(e, axis=-1, keepdims=True))
+    def scores(q, k):
+        return jnp.where(live_col, dot(q, k, 1, 1), -1e30)
 
     def attention(s, b):
         rows = rows_of(b)
@@ -683,8 +770,18 @@
         def _(i):
             cols = lanes(i)
             q, k, v = (qkvs[s, t, rows, cols] for t in range(3))
-            parts = [dot(softmax(pick(h, q), k).astype(BF), v, 1, 0) for h in range(2)]
-            mixs[s, rows, cols] = jnp.where(left, parts[0], parts[1]).astype(BF)
+            q = q * jnp.asarray(0.125, BF)
+            ones = jnp.ones_like(v)
+            tops, parts = [], []
+            for h in range(2):
+                sc = scores(pick(h, q), k)
+                tops.append(jnp.max(sc, axis=-1, keepdims=True))
+                e = jnp.exp(sc - tops[h]).astype(BF)
+                parts.append(dot(e, jnp.where(left, v, ones) if h == 0 else jnp.where(left, ones, v), 1, 0))
+            den = pltpu.roll(jnp.where(left, parts[1], parts[0]), 64, 1)
+            mixs[s, rows, cols] = (jnp.where(left, parts[0], parts[1]) / den).astype(BF)
+            lse = jnp.where(left, tops[0], tops[1]) + jnp.log(den)
+            stats[rows, :] = jnp.where(lax.rem(lane, 64) == 8 * s + i, lse, stats[rows, :])
 
     def out_project(s, b, k):
         @pl.loop(0, 4)
@@ -696,16 +793,16 @@
     def middle(s, b, k):
         shift, gain2, shift2 = row(s, 2), row(s, 3), row(s, 4)
 
-        @chunks(b)
+        @chunks(b, 2)
         def _(rows):
             v = xs[s, rows, :].astype(F32) + y_sum(k, rows) + shift
             if s == 0:
                 mid[rows, :] = v
             else:
                 gb[0, rows, :] = v.astype(BF)
-            nrm, inv = norm_chunk(v)
+            nrm, _, inv = norm_chunk(v)
             nrm2s[s, rows, :] = nrm.astype(BF)
-            inv2s[s, rows, :] = jnp.broadcast_to(inv, (CH, 128))
+            put_stats(rows, (stat_at(s, INV2), inv))
             low[rows, :] = (nrm * gain2 + shift2).astype(BF)
 
     def up_project(s, b):
@@ -746,54 +843,59 @@
         def _(rows):
             slps[1, rows, 1024:2048] = gb[0, rows, :]
 
-    def emit(which, s, src):
+    def emit_copies(which, s):
         target = (act_out, gin_out)[which].at[c]
-        q = which * 2 + s
+        src, q = woven.at[pl.ds(0, L)], which * 2 + s
+        return pltpu.make_async_copy(src, target, osem.at[q]), remote(src, target, osem_s.at[q], osem_r.at[q], to_c)
+
+    def emit(which, s):
+        here, there = emit_copies(which, s)
 
         @pl.when(c == s)
         def _():
-            pltpu.make_async_copy(src, target, osem.at[q]).start()
+            here.start()
 
         @pl.when(c != s)
         def _():
-            remote(src, target, osem_s.at[q], osem_r.at[q], to_c).start()
-
-    def emit_sent(which, s, src):
-        target = (act_out, gin_out)[which].at[c]
-        q = which * 2 + s
+            there.start()
+
+    def emit_sent(which, s):
+        here, there = emit_copies(which, s)
 
         @pl.when(c == s)
         def _():
-            pltpu.make_async_copy(src, target, osem.at[q]).wait()
+            here.wait()
 
         @pl.when(c != s)
         def _():
-            remote(src, target, osem_s.at[q], osem_r.at[q], to_c).wait_send()
-
-    def emit_got(which, s, src):
-        target = (act_out, gin_out)[which].at[1 - c]
-        q = which * 2 + s
-
+            there.wait_send()
+
+    def emit_got(which, s):
         @pl.when(c == s)
         def _():
-            remote(src, target, osem_s.at[q], osem_r.at[q], to_c).wait_recv()
-
-    def relower(s, b):
+            remote(
+                woven.at[pl.ds(0, L)], (act_out, gin_out)[which].at[1 - c], osem_s.at[which * 2 + s], osem_r.at[which * 2 + s], to_c
+            ).wait_recv()
+
+    def relower(s, b, dst):
         gain2, shift2 = row(s, 3), row(s, 4)
 
         @chunks(b)
         def _(rows):
-            low[rows, :] = (nrm2s[s, rows, :].astype(F32) * gain2 + shift2).astype(BF)
+            dst[rows, :] = (nrm2s[s, rows, :].astype(F32) * gain2 + shift2).astype(BF)
+
+    def fold8(v):
+        return jnp.sum(v.reshape(v.shape[0] // 8, 8, v.shape[1]), axis=0)
 
     def colsum(v):
         return jnp.sum(v, axis=0, keepdims=True)
 
     def sum_rows(ref_slice, width):
         def step(i, tot):
-            rows = pl.ds(pl.multiple_of(i * CH, CH), CH)
-            return tot + colsum(ref_slice(rows).astype(F32))
-
-        return lax.fori_loop(0, R // CH, step, jnp.zeros((1, width), F32))
+            rows = pl.ds(pl.multiple_of(i * 32, 32), 32)
+            return tot + fold8(ref_slice(rows).astype(F32))
+
+        return colsum(lax.fori_loop(0, R // 32, step, jnp.zeros((8, width), F32)))
 
     def total(s, r, b, v):
         sv[s, r : r + 1, :] = v if b == 0 else sv[s, r : r + 1, :] + v
@@ -811,12 +913,13 @@
         sv[s, 7:8, :] = sum_rows(lambda r: gpre[r, 0:1024], 1024)
         sv[s, 8:9, :] = sum_rows(lambda r: gpre[r, 1024:2048], 1024)
 
-    def grad_down(s):
-        @pl.loop(0, 8)
+    def grad_down(s, h, dst):
+        @pl.loop(0, 4)
         def _(i):
-            cols = lanes(i * 2, 256)
-            rows_w = pl.ds(pl.multiple_of(i * 256, 256), 256)
-            wdown[s, rows_w, :] = dot(gels[s, :, cols], gb[s], 0, 0).astype(BF)
+            first = h * 1024 + i * 256
+            cols = pl.ds(pl.multiple_of(first, 256), 256)
+            rows_w = pl.ds(pl.multiple_of(i * 256 if s == 1 else first, 256), 256)
+            dst[rows_w, :] = dot(gels[s, :, cols], gb[s], 0, 0).astype(BF)
 
     def grad_low_two(s, b, k):
         @pl.loop(0, 4)
@@ -826,40 +929,39 @@
             ys[rows_of(b), cols] = dot(gpre[rows_of(b), :], wup[s, rows_w, :], 1, 1).astype(BF)
             y_start(k, b, n)
 
-    def grad_up(s):
+    def grad_up(s, low2):
         @pl.loop(0, 4)
         def _(i):
             cols = lanes(i * 2, 256)
             rows_w = pl.ds(pl.multiple_of(i * 256, 256), 256)
             for q in range(2):
                 wup[s, rows_w, q * 1024 : q * 1024 + 1024] = dot(
-                    low[:, cols], gpre[:, q * 1024 : q * 1024 + 1024], 0, 0
+                    low2[:, cols], gpre[:, q * 1024 : q * 1024 + 1024], 0, 0
                 ).astype(BF)
 
     def loop_sums(b, count, step):
-        zero = jnp.zeros((1, 1024), F32)
+        zero = jnp.zeros((8, 1024), F32)
 
         def body(i, tots):
-            return step(pl.ds(pl.multiple_of(b * LP + i * CH, CH), CH), tots)
-
-        return lax.fori_loop(0, LP // CH, body, (zero,) * count)
+            new = step(pl.ds(pl.multiple_of(b * LP + i * CH, CH), CH))
+            return tuple(t + fold8(v) for t, v in zip(tots, new))
+
+        return [colsum(t) for t in lax.fori_loop(0, LP // CH, body, (zero,) * count)]
 
     def grad_middle(s, b, k):
         gain = row(s, 3)
 
-        def step(rows, tots):
-            t_gain, t_shift, t_out = tots
+        def step(rows):
             g2 = y_sum(k, rows)
             nrm = nrm2s[s, rows, :].astype(F32)
             t = g2 * gain
             m1 = jnp.mean(t, axis=-1, keepdims=True)
             m2 = jnp.mean(t * nrm, axis=-1, keepdims=True)
-            inv = inv2s[s, rows, :][:, 0:1]
-            gm = gb[s, rows, :].astype(F32) + inv * (t - m1 - nrm * m2)
+            gm = gb[s, rows, :].astype(F32) + stat(s, INV2, rows) * (t - m1 - nrm * m2)
             mid[rows, :] = gm
             ga = gm.astype(BF)
             low[rows, :] = ga
-            return (t_gain + colsum(g2 * nrm), t_shift + colsum(g2), t_out + colsum(ga.astype(F32)))
+            return g2 * nrm, g2, ga.astype(F32)
 
         for r, v in zip((3, 4, 2), loop_sums(b, 3, step)):
             total(s, r, b, v)
@@ -885,16 +987,17 @@
         def _(i):
             cols = lanes(i)
             q, k, v = (qkvs[s, t, rows, cols] for t in range(3))
+            q, k_low = q * jnp.asarray(0.125, BF), k * jnp.asarray(0.125, BF)
             gm = gpre[rows, cols]
+            kept = stats[rows, :]
             res = []
             for h in range(2):
-                probs = softmax(pick(h, q), k)
+                lse = jnp.sum(jnp.where(lane == 64 * h + 8 * s + i, kept, 0.0), axis=-1, keepdims=True)
+                probs = jnp.exp(scores(pick(h, q), k) - lse)
                 gp = dot(pick(h, gm), v, 1, 1)
                 gv = dot(probs.astype(BF), gm, 0, 0)
                 gs = (probs * (gp - jnp.sum(probs * gp, axis=-1, keepdims=True))).astype(BF)
-                gq = dot(gs, k, 1, 0) * (64.0 ** -0.5)
-                gk = dot(gs, q, 0, 0) * (64.0 ** -0.5)
-                res.append((gq, gk, gv))
+                res.append((dot(gs, k_low, 1, 0), dot(gs, q, 0, 0), gv))
             for t in range(3):
                 gqkv[t, rows, cols] = jnp.where(left, res[0][t], res[1][t]).astype(BF)
 
@@ -915,25 +1018,26 @@
             ys[rows, cols] = a.astype(BF)
             y_start(k, b, n)
 
-    def grad_qkv(s, t):
+    def grad_qkv(s, t, low1):
         @pl.loop(0, 4)
         def _(i):
             cols = lanes(i * 2, 256)
             rows_w = pl.ds(pl.multiple_of(i * 256, 256), 256)
-            wqkv[t][s, rows_w, :] = dot(low[:, cols], gqkv[t], 0, 0).astype(BF)
+            wqkv[t][s, rows_w, :] = dot(low1[:, cols], gqkv[t], 0, 0).astype(BF)
 
     def grad_stream(s, b, k, dst):
         gain = row(s, 0)
 
-        def step(rows, tots):
-            t_gain, t_shift = tots
+        def step(rows):
             g1 = y_sum(k, rows)
-            nrm, inv = norm_chunk(xs[s, rows, :].astype(F32))
+            nrm = norm1(s, rows)
             t = g1 * gain
             m1 = jnp.mean(t, axis=-1, keepdims=True)
             m2 = jnp.mean(t * nrm, axis=-1, keepdims=True)
-            dst[rows, :] = (mid[rows, :] + inv * (t - m1 - nrm * m2)).astype(BF)
-            return (t_gain + colsum(g1 * nrm), t_shift + colsum(g1))
+            dst[rows, :] = (mid[rows, :] + stat(s, INV1, rows) * (t - m1 - nrm * m2)).astype(BF)
+            if s == 1:
+                low[rows, :] = (nrm * gain + row(s, 1)).astype(BF)
+            return g1 * nrm, g1
 
         for r, v in zip((0, 1), loop_sums(b, 2, step)):
             total(s, r, b, v)
@@ -952,71 +1056,115 @@
     def add_block(m, dst, src):
         add_rows(dst, src, *shape_of(m))
 
+    def g_half(s, m):
+        return stage if (s, m) == (1, DOWN) else half(m, w[m], s, c)
+
+    def g_block(s, m, d):
+        if (s, m) == (1, DOWN):
+            return stage.at[:, pl.ds(pl.multiple_of(d * 128, 128), 128)]
+        return block(m, w[m], s, d, c)
+
     def r_view(s, m, h):
         return rbuf[m] if s == 1 else half(m, w[m], 1, h)
 
     def x_view(s, m, k, col):
         if m in X_FIRST:
             return xbuf[m].at[s]
+        if s == 0 and m in (Q, V):
+            return gels.at[1, pl.ds((m - Q) * 128, 128), pl.ds(k * 256, 256)]
         if s == 0:
             return block(m, w[m], 1, at_dp(k, col), c)
         at = pl.ds(k * 128, 128)
         return xbuf[m].at[at, :] if m in BY_ROWS else xbuf[m].at[:, at]
 
     def z_view(s, m, slot, col, place):
+        if s == 0 and m in (Q, K, V):
+            i = col * 4 + slot if m == K else 4 + slot
+            return gels.at[1, pl.ds((m - Q) * 128, 128), pl.ds(i * 256, 256)]
         if s == 0:
             return block(m, w[m], 1, place * 2 + (x if col == 0 else 1 - x), c)
+        if m in (UP, DOWN):
+            at = pl.ds(slot * 128, 128)
+            return rbuf[m].at[at, :] if m == UP else rbuf[m].at[:, at]
         return zbuf[m].at[col * 4 + slot]
 
     def rs_c(s, m):
         q = s * 6 + m - 1
         if s == 0:
             pl.semaphore_wait(free_c.at[m - 1], 1)
-        remote(half(m, w[m], s, 1 - c), r_view(s, m, c), rsem_cs.at[q], rsem_c.at[q], to_c).start()
+        if (s, m) == (1, UP):
+            pl.semaphore_wait(free_up, 1)
+        src = rup if (s, m) == (1, DOWN) else half(m, w[m], s, 1 - c)
+        remote(src, r_view(s, m, c), rsem_cs.at[q], rsem_c.at[q], to_c).start()
 
     def rs_sum(s, m):
         q = s * 6 + m - 1
-        mine, got = half(m, w[m], s, c), r_view(s, m, 1 - c)
+        mine, got = g_half(s, m), r_view(s, m, 1 - c)
         cp = remote(mine, got, rsem_cs.at[q], rsem_c.at[q], to_c)
         cp.wait_recv()
         cp.wait_send()
-        if s == 1:
+        if (s, m) == (1, DOWN):
+            pl.semaphore_signal(free_up, inc=1, device_id=to_c, device_id_type=MESH)
+        elif s == 1:
             pl.semaphore_signal(free_c.at[m - 1], inc=1, device_id=to_c, device_id_type=MESH)
         rows = 1024 if m in BY_ROWS else WIDTH[m] // 2
         add_rows(mine, got, rows, 16 if m not in (Q, K, V) else 64)
+        if s == 1 and m in (UP, DOWN):
+            z_credit(free_r.at[m - UP])
 
     def rs_to_x(s, m):
         if s == 0:
             pl.semaphore_wait(free_x.at[m - 1], 1)
         for k in (INNER, FAR, NEAR, SELF):
             q = s * 6 + m - 1
-            b = block(m, w[m], s, at_dp(k, 1), c)
+            b = g_block(s, m, at_dp(k, 1))
             remote(b, x_view(s, m, k, 0), rsem_xs.at[q], rsem_x.at[rx[(s, m), k]], to_x).start()
 
     def rs_from_x(s, m, k):
         q = s * 6 + m - 1
-        b = block(m, w[m], s, at_dp(k, 0), c)
+        b = g_block(s, m, at_dp(k, 0))
         got = x_view(s, m, k, 1)
         remote(b, got, rsem_xs.at[q], rsem_x.at[rx[(s, m), k]], to_x).wait_recv()
         if k == SELF:
             wait_bytes(m, 4, rsem_xs.at[q])
         add_block(m, b, got)
 
+    def down_freed():
+        pl.semaphore_signal(free_c.at[DOWN - 1], inc=1, device_id=to_c, device_id_type=MESH)
+        x_freed(DOWN)
+        z_freed(DOWN)
+
+    def gelu_freed():
+        for m in (Q, V):
+            x_freed(m)
+        for m in (Q, K, V):
+            z_freed(m)
+
     def x_freed(m):
         pl.semaphore_signal(free_x.at[m - 1], inc=1, device_id=to_x, device_id_type=MESH)
 
-    def z_ready(m):
+    def z_wait_credits(sem):
         @pl.when(inner)
         def _():
-            pl.semaphore_wait(free_z.at[m - 1], 3)
+            pl.semaphore_wait(sem, 3)
 
         @pl.when(jnp.logical_not(inner))
         def _():
-            pl.semaphore_wait(free_z.at[m - 1], 1)
+            pl.semaphore_wait(sem, 1)
+
+    def z_credit(sem):
+        for k in (NEAR, INNER):
+            pl.semaphore_signal(sem, inc=1, device_id=to_z(places[k]), device_id_type=MESH)
+
+    def z_ready(s, m):
+        if s == 0:
+            z_wait_credits(free_z.at[m - 1])
+        elif m in (UP, DOWN):
+            z_wait_credits(free_r.at[m - UP])
 
     def rs_to_z(s, m, k, col):
         q = s * 6 + m - 1
-        b = block(m, w[m], s, at_dp(k, col), c)
+        b = g_block(s, m, at_dp(k, col))
         if k == NEAR:
             remote(b, z_view(s, m, 0, col, z), rsem_zs.at[q, col], rsem_z.at[rz[(s, m), col * 4]], to_z(near)).start()
         else:
@@ -1030,7 +1178,7 @@
 
         @pl.when(inner)
         def _():
-            b = block(m, w[m], s, at_dp(k, col), c)
+            b = g_block(s, m, at_dp(k, col))
             got = z_view(s, m, k, col, places[k])
             remote(b, got, rsem_zs.at[q, col], rsem_z.at[rz[(s, m), col * 4 + k]], to_z(near)).wait_recv()
             add_block(m, b, got)
@@ -1047,12 +1195,11 @@
         wait_bytes(m, 3, rsem_zs.at[s * 6 + m - 1, col])
 
     def z_freed(m):
-        for k in (NEAR, INNER):
-            pl.semaphore_signal(free_z.at[m - 1], inc=1, device_id=to_z(places[k]), device_id_type=MESH)
+        z_credit(free_z.at[m - 1])
 
     def rs_fold(s, m):
         q = s * 6 + m - 1
-        b = block(m, w[m], s, at_dp(SELF, 1), c)
+        b = g_block(s, m, at_dp(SELF, 1))
         for got in z_arrived(s, m, 1):
             add_block(m, b, got)
         remote(b, xbuf[m].at[s], rsem_xs.at[q], rsem_x.at[rx[(s, m), 0]], to_x).start()
@@ -1068,7 +1215,7 @@
 
     def rs_f(s, m):
         q = s * 6 + m - 1
-        mine = block(m, w[m], s, me, c)
+        mine = g_block(s, m, me)
         parts = [mine] + z_arrived(s, m, 0)
         if m in X_FIRST:
             cp = remote(mine, xbuf[m].at[s], rsem_xs.at[q], rsem_x.at[rx[(s, m), 0]], to_x)
@@ -1088,7 +1235,7 @@
 
         for col in range(2) if m in X_FIRST else (0,):
             z_sent(s, m, col)
-        if s == 1:
+        if s == 1 and m in (UP, OUT):
             z_freed(m)
 
         @pl.when(c == s)
@@ -1127,7 +1274,7 @@
                 remote(svc, svz.at[j - 1], vsem_s.at[1 + j], vsem.at[1 + j], to_z(lax.rem(z + j, Z)))
                 for j in range(1, Z)
             ]
-        return [pltpu.make_async_copy(sv.at[c], gvec_out, isem.at[2])]
+        return [pltpu.make_async_copy(sv.at[c], gvec_out, isem.at[0])]
 
     def vec_step(i):
         if i:
@@ -1145,7 +1292,7 @@
 
     clock = Clock()
     size = {SMALL: 8e3, Q: 131e3, K: 131e3, V: 131e3, OUT: 131e3, UP: 524e3, DOWN: 524e3}
-    RATE = 88e3
+    RATE = 82e3
     HOP = 1.8
     free = {"x": 0.0, "z": 0.0, "y": 0.0}
     got = {}
@@ -1154,16 +1301,16 @@
         free[name] = max(free[name], clock.now) + nbytes / RATE
         return free[name] + HOP
 
-    in_x = pltpu.make_async_copy(x_ref.at[c], ys, isem.at[0])
-    in_g = pltpu.make_async_copy(cot_ref.at[c], gpre.at[:, pl.ds(0, 1024)], isem.at[1])
-    in_x.start()
-    in_g.start()
-
     order = (SMALL, Q, K, V, OUT, UP, DOWN)
+    for cp in small_in:
+        cp.start()
     for s in range(2):
-        for m in order:
+        for m in order[1:]:
             ag_share(s, m)
-    clock.now = 2.0
+    pack_small()
+    for s in range(2):
+        ag_share(s, SMALL)
+    clock.now = 6.5
 
     def plan_gather(s, m):
         x_first = m in X_FIRST
@@ -1186,7 +1333,8 @@
             t = size[m] / RATE
             free["z"] = begin + 3 * t
             for k in (NEAR, INNER, FAR):
-                clock.add(begin + k * t + (HOP if k == NEAR else 2 * HOP), functools.partial(at_z, k, col))
+                late = HOP if k == NEAR else 2 * HOP
+                clock.add(begin + k * t + late, functools.partial(at_z, k, col))
 
         def own():
             if not x_first:
@@ -1204,15 +1352,15 @@
 
         if x_first:
             clock.add(x_begin[s, m], early)
-        clock.add(max(z_begin[s, m] - LEAD, 2.0), own)
-
-    LEAD = 5.0
-    z_begin, x_begin, at = {}, {}, 3.0
+        clock.add(max(z_begin[s, m] - LEAD, clock.now), own)
+
+    LEAD, AHEAD = 23.0, 2.0
+    z_begin, x_begin, at = {}, {}, 7.0
     for s in range(2):
         for m in order:
             z_begin[s, m] = at
             at += size[m] / RATE * (6 if m in X_FIRST else 3)
-            x_begin[s, m] = max(2.0, z_begin[s, m] - 14.0)
+            x_begin[s, m] = max(clock.now, z_begin[s, m] - LEAD - AHEAD)
     for s in range(2):
         for m in order:
             plan_gather(s, m)
@@ -1242,7 +1390,7 @@
             rs_pass(s, m, k, col)
             done.append((k, col))
             if len([d for d in done if d[1] == col]) == 2:
-                ready = max(clock.now, free["z"] - 2 * t) + 2 * t + 2 * HOP
+                ready = clock.now + t + 2 * HOP + 4.0
                 if x_first and col == 1:
                     clock.add(ready, fold, 0.4)
                 elif not x_first:
@@ -1260,7 +1408,7 @@
             if x_first:
                 if s == 0:
                     clock.drain(lambda: ("z", m) in passed)
-                    z_ready(m)
+                z_ready(s, m)
                 for col in (1, 0):
                     for k in order:
                         z_start(k, col)
@@ -1269,46 +1417,47 @@
                     clock.drain(lambda: ("x", m) in passed)
                 rs_to_x(s, m)
                 for k in order + (SELF,):
-                    clock.add(link("x", size[m]), functools.partial(from_x, k), 0.3)
+                    clock.add(link("x", size[m]) + 1.5, functools.partial(from_x, k), 0.3)
 
         def from_x(k):
             rs_from_x(s, m, k)
             if k == SELF:
                 done.append((SELF, -1))
                 if s == 1:
-                    x_freed(m)
-                    passed.add(("x", m))
+                    if m == UP:
+                        x_freed(m)
+                        passed.add(("x", m))
                 return
-            if k == INNER and s == 0:
-                clock.drain(lambda: ("z", m) in passed)
-                z_ready(m)
+            if k == INNER:
+                if s == 0:
+                    clock.drain(lambda: ("z", m) in passed)
+                z_ready(s, m)
             z_start(k, 0)
 
         def finish_sum():
             clock.drain(lambda: ready_to_finish())
             if s == 0:
+                clock.drain(lambda: ("f", m) in passed)
                 rs_f_sent(1, m)
             rs_f(s, m)
             if s == 1:
-                passed.add(("z", m))
+                passed.add(("f", m))
+                if m in (UP, OUT):
+                    passed.add(("z", m))
 
         def ready_to_finish():
             return x_first or (SELF, -1) in done
 
         if s == 0:
             clock.drain(lambda: ("c", 1, m) in passed)
+        elif m == UP:
+            clock.drain(lambda: ("c", 1, DOWN) in passed)
         rs_c(s, m)
         clock.add(clock.now + 4 * size[m] / 500e3 + 2.0, sum_step, 0.8)
 
-    for i in range(5):
-        clock.flush(clock.now)
-        clock.now += 0.4
-    in_x.wait()
-    in_g.wait()
+    clock.run(2.0, load_woven, x_ref, isem.at[0], gpre)
     for b in range(2):
-        clock.run(0.6, unweave, ys, xs.at[0], b, None)
-    for b in range(2):
-        clock.run(0.6, unweave, gpre, gb.at[1], b, alive_of(b))
+        clock.run(0.6, unweave, gpre, xs.at[0], b, None)
     y_at = {}
     for s in range(2):
         last = s == 1
@@ -1318,86 +1467,123 @@
             if last:
                 clock.wait(y_at[1, b], y_wait, 1, b)
                 clock.run(1.0, finish, 0, b, 1, xs.at[1])
-                if b == 1:
-                    emit(0, 0, xs.at[1])
-            clock.run(2.3, ln1, s, b)
+            clock.run(1.7, ln1, s, b)
             if b == 0:
                 for m in (Q, K, V):
                     need(s, m)
-            clock.run(1.4, project, s, b)
-            clock.run(3.6, attention, s, b)
+            clock.run(1.7, project, s, b)
+            clock.run(3.0, attention, s, b)
             if b == 0:
                 need(s, OUT)
-            clock.run(0.7, out_project, s, b, s * 2)
+            clock.run(0.9, out_project, s, b, s * 2)
             y_at[s * 2, b] = y_sent()
+        if last:
+            clock.run(1.5, weave, xs.at[1], gpre)
+            emit(0, 0)
         for b in range(2):
             clock.wait(y_at[s * 2, b], y_wait, s * 2, b)
-            clock.run(2.5, middle, s, b, s * 2)
+            clock.run(1.5, middle, s, b, s * 2)
             if b == 0:
                 need(s, UP)
-            clock.run(2.7, up_project, s, b)
-        need(s, DOWN)
+            clock.run(4.0, up_project, s, b)
         if not last:
+            need(0, DOWN)
             for b in range(2):
                 clock.run(1.5, down_project, 0, b, 1, True)
                 y_at[1, b] = y_sent()
-
-    for s in range(2):
+            clock.run(2.0, load_woven, cot_ref, isem.at[1], gpre)
+            for b in range(2):
+                clock.run(0.6, unweave, gpre, gb.at[1], b, alive_of(b))
+
+    clock.run(1.9, grad_down, 1, 1 - c, rup)
+    reduce(1, DOWN)
+    clock.run(1.9, grad_down, 1, c, stage)
+    need(1, DOWN)
+    for b in range(2):
+        clock.run(2.7, grad_gelu, 1, b)
+        clock.run(2.0, grad_low_two, 1, b, 3)
+        y_at[3, b] = y_sent()
+    for q in range(2):
         for m in order:
-            ag_sent(s, m)
+            ag_sent(q, m)
     for s in (1, 0):
         k = 3 if s == 1 else 5
-        for b in range(2):
-            if s == 0:
-                clock.wait(y_at[4, b], y_wait, 4, b)
-                clock.run(3.5, grad_stream, 1, b, 4, gb.at[0])
-                if b == 1:
-                    emit(1, 1, gb.at[0])
-            clock.run(2.2, grad_gelu, s, b)
-            clock.run(1.5, grad_low_two, s, b, k)
-            y_at[k, b] = y_sent()
+        clock.run(3.0, grad_up, s, low if s == 1 else gb.at[1])
+        reduce(s, UP)
         if s == 0:
             for b in range(2):
-                clock.run(0.5, relower, 0, b)
-        clock.run(3.0, grad_up, s)
-        reduce(s, UP)
+                clock.run(1.7, down_project, 1, b, 7, False)
+            down_freed()
+            gelu_freed()
+            passed.update({("c", 1, DOWN), ("x", DOWN), ("z", DOWN), ("x", Q), ("x", V), ("z", Q), ("z", K), ("z", V)})
+            clock.run(1.9, grad_down, 0, 1 - c, wdown.at[0])
+            reduce(0, DOWN)
+            clock.run(1.9, grad_down, 0, c, wdown.at[0])
+            for t in range(3):
+                clock.run(1.4, grad_qkv, 1, t, low)
+                reduce(1, Q + t)
+            clock.run(0.5, grad_qv_bias, 1)
+        clock.run(0.6, grad_mlp_biases, s)
         if s == 1:
             for b in range(2):
                 clock.run(0.3, keep_middle, b)
-                clock.run(1.5, down_project, 1, b, 7, False)
-        clock.run(3.8, grad_down, s)
-        reduce(s, DOWN)
-        clock.run(1.0, grad_mlp_biases, s)
+        if s == 0:
+            emit_sent(0, 0)
+            clock.run(1.5, weave, gb.at[0], gpre)
+            emit(1, 1)
+        if s == 0:
+            for b in range(2):
+                clock.run(0.8, relow1, 0, b, gb.at[1])
         for b in range(2):
             clock.wait(y_at[k, b], y_wait, k, b)
-            clock.run(1.6, grad_middle, s, b, k)
+            clock.run(1.9, grad_middle, s, b, k)
             clock.run(0.5, grad_mixed, s, b)
             if b == 1:
                 clock.run(0.9, grad_out, s)
                 reduce(s, OUT)
-            clock.run(5.1, grad_attention, s, b)
-            clock.run(1.2, grad_lowered, s, b, k + 1)
+            clock.run(3.8, grad_attention, s, b)
+            clock.run(1.6, grad_lowered, s, b, k + 1)
             y_at[k + 1, b] = y_sent()
-        for b in range(2):
-            clock.run(2.3, ln1, s, b)
-        for t in range(3):
-            clock.run(1.4, grad_qkv, s, t)
-            reduce(s, Q + t)
-        clock.run(0.5, grad_qv_bias, s)
+        if s == 1:
+            for b in range(2):
+                clock.wait(y_at[4, b], y_wait, 4, b)
+                clock.run(2.2, grad_stream, 1, b, 4, gb.at[0])
+                clock.run(2.7, grad_gelu, 0, b)
+                clock.run(2.0, grad_low_two, 0, b, 5)
+                y_at[5, b] = y_sent()
+                if b == 0:
+                    for q in range(2):
+                        clock.run(0.5, relower, 0, q, gb.at[1])
+        else:
+            pl.semaphore_signal(free_y, inc=1, device_id=to_y, device_id_type=MESH)
+            pl.semaphore_wait(free_y, 1)
+            for b in range(2):
+                for n in range(4):
+                    y_start(7, b, n)
+                y_at[7, b] = y_sent()
+            for t in range(3):
+                clock.run(1.4, grad_qkv, 0, t, gb.at[1])
+                reduce(0, Q + t)
+            clock.run(0.5, grad_qv_bias, 0)
     for b in range(2):
         clock.wait(y_at[6, b], y_wait, 6, b)
-        clock.run(3.5, grad_stream, 0, b, 6, low)
-    emit(1, 0, low)
-    for i in range(4):
-        clock.add(clock.now + 3.0 * i, functools.partial(vec_step, i), 0.5)
-    for b in range(2):
-        for n in range(4):
-            y_start(7, b, n)
-        y_at[7, b] = y_sent()
+        clock.run(2.2, grad_stream, 0, b, 6, low)
+    def vec_chain(i):
+        vec_step(i)
+        if i < 3:
+            ready = (clock.now + 3.0, link("x", 131e3) + 1.0, link("z", 262e3) + 4.0)[i]
+            clock.add(ready, functools.partial(vec_chain, i + 1), 0.5)
+
+    vec_chain(0)
+    emit_sent(1, 1)
+    clock.run(2.0, weave, low, gpre)
+    emit(1, 0)
     for b in range(2):
         clock.wait(y_at[7, b], y_wait, 7, b)
         clock.run(1.0, finish, 1, b, 7, gb.at[1])
-    emit(0, 1, gb.at[1])
+    emit_sent(1, 0)
+    clock.run(2.0, weave, gb.at[1], gpre)
+    emit(0, 1)
     clock.drain(lambda: not clock.queue)
     for cp in vec_copies(3):
         cp.wait()
@@ -1406,16 +1592,13 @@
     for s in range(2):
         for m in MATS:
             rs_end(s, m)
-    emit_sent(0, 0, xs.at[1])
-    emit_sent(0, 1, gb.at[1])
-    emit_sent(1, 1, gb.at[0])
-    emit_sent(1, 0, low)
+    emit_sent(0, 1)
     for which in range(2):
         for s in range(2):
-            emit_got(which, s, low)
-
-
-def run_kernel(small, qkv, out, up, down, xin, cot, live):
+            emit_got(which, s)
+
+
+def run_kernel(*args):
     any_spec = pl.BlockSpec(memory_space=pl.ANY)
     V = pltpu.VMEM
     D_ = pltpu.SemaphoreType.DMA
@@ -1435,33 +1618,34 @@
         V((2,) + halved(shape, rows, 8) if f else halved(shape, rows, 2), BF)
         for shape, rows, f in zip(mats, by_rows, first)
     ]
-    scratch += [V((8 if f else 4,) + halved(shape, rows, 8), BF) for shape, rows, f in zip(mats, by_rows, first)]
+    scratch += [V((8 if f else 4,) + halved(shape, rows, 8), BF) for shape, rows, f in zip(mats[:4], by_rows, first)]
     scratch += [V(halved(shape, rows, 8), F32) for shape, rows in zip(mats, by_rows)]
     scratch += [
         V((2, R, 1024), BF), V((2, 3, R, 512), BF), V((2, R, 512), BF), V((2, R, 1024), BF),
-        V((2, R, 2048), BF), V((2, R, 2048), BF), V((2, R, 128), F32),
+        V((2, R, 2048), BF), V((2, R, 2048), BF), V((R, 128), F32),
         V((R, 1024), BF), V((R, 1024), F32), V((2, R, 1024), BF), V((R, 2048), BF), V((3, R, 512), BF),
         V((R, 1024), BF), V((2, R, 1024), BF), V((LP, 256), F32),
         V((2, 16, 1024), F32), V((2, 16, 1024), F32), V((16, 1024), F32), V((16, 1024), F32), V((3, 16, 1024), F32),
+        V((LP, 2, 1024), BF), V((1024, 1024), BF), V((32, 128), BF), V((6, 1, 128), BF), V((2, 8, 8), BF), V((8, 32), BF),
         D_((14,)), D_((14, 2)), D_((54,)), D_((44,)),
         D_((12,)), D_((12,)), D_((12,)), D_((36,)), D_((12, 2)), D_((64,)), D_((12,)), D_((12,)),
-        D_((16,)), D_((16,)), D_((4,)), D_((4,)), D_((4,)), D_((3,)), D_((5,)), D_((5,)),
-        REG((6,)), REG((6,)), REG((6,)),
+        D_((16,)), D_((16,)), D_((4,)), D_((4,)), D_((4,)), D_((10,)), D_((5,)), D_((5,)),
+        REG((6,)), REG((6,)), REG((6,)), REG, REG((2,)), REG,
     ]
     return pl.pallas_call(
         kernel,
         out_shape=[
-            S((2, R, 1024), BF), S((2, R, 1024), BF), S((3, 128, 512), F32), S((512, 128), F32),
+            S((2, L, 2, 1024), BF), S((2, L, 2, 1024), BF), S((3, 128, 512), F32), S((512, 128), F32),
             S((128, 2048), F32), S((2048, 128), F32), S((16, 1024), F32),
         ],
-        in_specs=[any_spec] * 7 + [pl.BlockSpec(memory_space=pltpu.SMEM)],
+        in_specs=[any_spec] * 14 + [pl.BlockSpec(memory_space=pltpu.SMEM)],
         out_specs=[any_spec] * 7,
         scratch_shapes=scratch,
         compiler_params=pltpu.CompilerParams(
             collective_id=1, has_side_effects=True, vmem_limit_bytes=67043328
         ),
         name="sections",
-    )(small, qkv, out, up, down, xin, cot, live)
+    )(*args)
 
 
 def local_fast(images, cotangent, live_count, ln1_gain, ln1_bias, qkv_weight, qv_bias, out_weight, out_bias,
@@ -1469,28 +1653,17 @@
     d = lax.axis_index("dp")
 
     def woven(a):
-        a = jnp.transpose(a, (0, 2, 1, 3)).reshape(2, 2 * L, 1024)
-        return jnp.pad(a, ((0, 0), (0, R - 2 * L), (0, 0)))
-
-    def spread(a, width):
-        n = a.shape[-1]
-        z8 = jnp.where((jnp.arange(8) == d)[:, None], a[..., None, :], jnp.zeros_like(a[..., None, :]))
-        return z8.reshape(a.shape[:-1] + (8 * n,))
-
-    at = lax.broadcasted_iota(jnp.int32, (32, 128), 0)
-    small = jnp.pad(spread(qv_bias[0], 64).reshape(8, 128), ((6, 18), (0, 0)))
-    small = small + jnp.pad(spread(up_bias[0], 256).reshape(16, 128), ((14, 2), (0, 0)))
-    for i, v in enumerate((ln1_gain, ln1_bias, out_bias, ln2_gain, ln2_bias, down_bias)):
-        small = jnp.where(at == i, v, small)
+        return jnp.transpose(a, (0, 2, 1, 3))
+
     act, gin, gqkv, gout, gup, gdown, gvec = run_kernel(
-        small, qkv_weight[0], out_weight[0], up_weight[0], down_weight[0], woven(images), woven(cotangent), live_count
+        ln1_gain, ln1_bias, out_bias, ln2_gain, ln2_bias, down_bias, qv_bias[0], up_bias[0],
+        qkv_weight[0], out_weight[0], up_weight[0], down_weight[0], woven(images), woven(cotangent), live_count.reshape(2),
     )
 
     def cut(v, axis, n):
         return lax.dynamic_slice_in_dim(v, d * n, n, axis=axis)
 
-    act = act.reshape(2, 2, LP, 1024)[None, :, :, :L]
-    gin = gin.reshape(2, 2, LP, 1024)[None, :, :, :L]
+    act, gin = woven(act)[None], woven(gin)[None]
     vecs = cut(gvec[:6], 1, 128)
     qv = cut(gvec[6].reshape(2, 8, 64), 2, 8)
     upb = cut(gvec[7:9].reshape(8, 256), 1, 32)

time: 361 us -> 319 us (0.88)
  Pallas kernels: 332 us -> 305 us
  local copies, waits for them, and re-layouts: 25.1 us -> 13.4 us
    pallas_call x1, Pallas kernels: 332 us -> 305 us  [run_kernel(): pl.pallas_call(kernel, out_shape=[S((2, L, 2, 1024), BF), S((2, L, 2, 102...]
    transpose x2 -> x0, local copies, waits for them, and re-layouts: 4.74 us -> none  [woven(): a = jnp.transpose(a, (0, 2, 1, 3)).reshape(2, 2 * L, 1024)]
    unnamed x21 -> x16, local copies, waits for them, and re-layouts: 10.5 us -> 9.02 us
where the time goes in v3:
time: 319 us
  Pallas kernels  305 us (96%)
  local copies, waits for them, and re-layouts  13.4 us (4%)
    pallas_call x1, Pallas kernels, run_kernel(): pl.pallas_call(kernel, out_shape=[S((2, L, 2, 1024), BF), S((2, L, 2, 102...  305 us
    unnamed x16, local copies, waits for them, and re-layouts  9.02 us

profile of v3, /device:TPU:0, one launch (start us, length us, event | category | flops | bytes accessed | tf_op | source)
XLA Modules:
  0.0 318.7 jit_solution(17964029256905485177)
XLA Ops:
  0.7 304.7 %sections.1 = (bf16[2,197,2,1024]{3,2,1,0:T(2,128)(2,1)}, bf16[2,197,2,1024]{3,2,1,0:T(2,128)(2,1)}, f32[3,128,512]{2,1,0:T(8,128)}, f32[512,128]{1,0:T(8,128)},...) custom-call(bf16[1,128]{1,0:T(2,128)(2,1)} %gain1_ref.1, bf16[1,128]{1,0:T(2,128)(2,1)} %shift1_ref.1, ...), custom_call_target="tpu_custom_call" | custom-call | tf_op jit(solution)/shard_map/sections/pallas_call | solution.py:1635
  305.4 0.8 slice.27
  306.1 0.5 fusion
  306.7 0.8 slice_reduce_fusion
  307.4 0.1 reshape_squeeze.3
  307.5 0.7 dynamic-slice_bitcast_fusion
  308.2 0.8 slice.34
  309.0 0.7 dynamic-slice_bitcast_fusion.1
  309.7 0.0 copy-start
  309.7 3.8 %copy.35 = bf16[1,2,2,197,1024]{4,2,3,1,0:T(2,128)(2,1)} copy(bf16[1,2,2,197,1024]{4,2,3,1,0:T(2,128)(2,1)} %bitcast.26) | data formatting | bytes 3227648
  313.5 0.0 copy-done
  313.5 0.0 copy-start.3
  313.5 0.0 copy-start.4
  313.5 1.2 copy.36
  314.7 0.5 copy-done.3
  315.2 0.0 copy-start.2
  315.2 0.9 copy.37
  316.1 0.0 copy-done.4
  316.1 0.0 copy-start.1
  316.1 0.7 copy.38
  316.8 0.0 copy-done.2
  316.8 1.0 copy.39
  317.8 0.0 copy-done.1
  317.8 1.0 copy.40
  (2 shorter events, 0.0 us)
Async XLA Ops:
  309.7 3.8 %copy-start = (bf16[2,197,2,1024]{3,2,1,0:T(2,128)(2,1)S(1)}, bf16[2,197,2,1024]{3,2,1,0:T(2,128)(2,1)}, u32[]{:S(2)}) copy-start(bf16[2,197,2,1024]{3,2,1,0:T(2,128)(2,1)} %get-tuple-element.22) | copy-start | bytes 4841476
  313.5 1.7 copy-start.3
  313.5 2.6 copy-start.4
  315.2 1.6 copy-start.2
  316.1 1.7 copy-start.1

commit v4 on v3

--- a/solution.py
+++ b/solution.py
@@ -385,6 +385,7 @@
 MATS = (Q, K, V, OUT, UP, DOWN)
 BY_ROWS = (Q, K, V, UP)
 X_FIRST = (K, OUT)
+Z_FIRST = ((1, K), (1, OUT), (0, OUT))
 WIDTH = {Q: 512, K: 512, V: 512, OUT: 512, UP: 2048, DOWN: 2048}
 SELF, NEAR, INNER, FAR = range(4)
 
@@ -448,12 +449,12 @@
 def kernel(
     gain1_ref, shift1_ref, bias_o_ref, gain2_ref, shift2_ref, bias_d_ref, qv_ref, upb_ref,
     qkv_ref, out_ref, up_ref, down_ref, x_ref, cot_ref, live_ref,
-    act_out, gin_out, gqkv_out, gout_out, gup_out, gdown_out, gvec_out,
+    act_out, gin_out, gqkv_out, gout_out, gup_out, gdown_out, gvec_out, gqv_out, gupb_out,
     wsmall, wq, wk, wv, wout, wup, wdown,
     rq, rk, rv, rout, rup, rdown, xq, xk, xv, xout, xup, xdown,
     zq, zk, zv, zout, fq, fk, fv, fout, fup, fdown,
     xs, qkvs, mixs, nrm2s, gels, slps, stats,
-    low, mid, gb, gpre, gqkv, ys, yr, acc, vec, sv, svc, svx, svz, woven, stage, pack, raw, rawq, rawu,
+    low, mid, gb, gpre, gqkv, ys, yr, acc, vec, sv, svc, svx, svz, woven, stage, pack, raw, rawq, rawu, vq, vu,
     asem_s, asem_c, asem_z, asem_x, rsem_cs, rsem_c, rsem_xs, rsem_x, rsem_zs, rsem_z, rsem_fs, rsem_f,
     ysem, ysem_s, osem, osem_r, osem_s, isem, vsem, vsem_s, free_c, free_x, free_z, free_up, free_r, free_y,
 ):
@@ -505,8 +506,8 @@
     pieces = [(s, m) for s in range(2) for m in range(7)]
     az = number((p, 6 if p[1] in X_FIRST else 3) for p in pieces)
     ax = number((p, 1 if p[1] in X_FIRST else 4) for p in pieces)
-    rz = number((p, 8 if p[1] in X_FIRST else 4) for p in pieces if p[1])
-    rx = number((p, 1 if p[1] in X_FIRST else 4) for p in pieces if p[1])
+    rz = number((p, 8 if p in Z_FIRST else 4) for p in pieces if p[1])
+    rx = number((p, 1 if p in Z_FIRST else 4) for p in pieces if p[1])
 
     def wait_bytes(m, count, sem):
         if m == SMALL:
@@ -1068,9 +1069,9 @@
         return rbuf[m] if s == 1 else half(m, w[m], 1, h)
 
     def x_view(s, m, k, col):
-        if m in X_FIRST:
+        if (s, m) in Z_FIRST:
             return xbuf[m].at[s]
-        if s == 0 and m in (Q, V):
+        if s == 0 and m in (Q, K, V):
             return gels.at[1, pl.ds((m - Q) * 128, 128), pl.ds(k * 256, 256)]
         if s == 0:
             return block(m, w[m], 1, at_dp(k, col), c)
@@ -1079,7 +1080,7 @@
 
     def z_view(s, m, slot, col, place):
         if s == 0 and m in (Q, K, V):
-            i = col * 4 + slot if m == K else 4 + slot
+            i = col * 4 + slot if (s, m) in Z_FIRST else 4 + slot
             return gels.at[1, pl.ds((m - Q) * 128, 128), pl.ds(i * 256, 256)]
         if s == 0:
             return block(m, w[m], 1, place * 2 + (x if col == 0 else 1 - x), c)
@@ -1135,8 +1136,9 @@
         z_freed(DOWN)
 
     def gelu_freed():
-        for m in (Q, V):
-            x_freed(m)
+        for m in (Q, K, V):
+            if (0, m) not in Z_FIRST:
+                x_freed(m)
         for m in (Q, K, V):
             z_freed(m)
 
@@ -1217,7 +1219,7 @@
         q = s * 6 + m - 1
         mine = g_block(s, m, me)
         parts = [mine] + z_arrived(s, m, 0)
-        if m in X_FIRST:
+        if (s, m) in Z_FIRST:
             cp = remote(mine, xbuf[m].at[s], rsem_xs.at[q], rsem_x.at[rx[(s, m), 0]], to_x)
             cp.wait_recv()
             cp.wait_send()
@@ -1233,7 +1235,7 @@
                 a = a + part[rows, :].astype(F32)
             fbuf[m][rows, :] = a
 
-        for col in range(2) if m in X_FIRST else (0,):
+        for col in range(2) if (s, m) in Z_FIRST else (0,):
             z_sent(s, m, col)
         if s == 1 and m in (UP, OUT):
             z_freed(m)
@@ -1274,7 +1276,11 @@
                 remote(svc, svz.at[j - 1], vsem_s.at[1 + j], vsem.at[1 + j], to_z(lax.rem(z + j, Z)))
                 for j in range(1, Z)
             ]
-        return [pltpu.make_async_copy(sv.at[c], gvec_out, isem.at[0])]
+        return [
+            pltpu.make_async_copy(sv.at[c, pl.ds(0, 8)], gvec_out, isem.at[0]),
+            pltpu.make_async_copy(vq, gqv_out, isem.at[1]),
+            pltpu.make_async_copy(vu, gupb_out, isem.at[2]),
+        ]
 
     def vec_step(i):
         if i:
@@ -1287,6 +1293,12 @@
             svc[...] = sv[c] + svx[...]
         if i == 3:
             sv[c] = svc[...] + svz[0] + svz[1] + svz[2]
+            for t in range(2):
+                for h in range(8):
+                    at = (t * 8 + h) * 64
+                    vq[t, h : h + 1, :] = sv[c, 6:7, at : at + 64]
+            for g in range(8):
+                vu[g : g + 1, :] = sv[c, 7 + g // 4 : 8 + g // 4, g % 4 * 256 : g % 4 * 256 + 256]
         for cp in vec_copies(i):
             cp.start()
 
@@ -1376,7 +1388,7 @@
     passed = set()
 
     def reduce(s, m):
-        x_first = m in X_FIRST
+        x_first = (s, m) in Z_FIRST
         t = size[m] / RATE
         order = (INNER, FAR, NEAR)
 
@@ -1390,7 +1402,7 @@
             rs_pass(s, m, k, col)
             done.append((k, col))
             if len([d for d in done if d[1] == col]) == 2:
-                ready = clock.now + t + 2 * HOP + 4.0
+                ready = clock.now + t + 2 * HOP + 8.0
                 if x_first and col == 1:
                     clock.add(ready, fold, 0.4)
                 elif not x_first:
@@ -1515,7 +1527,7 @@
                 clock.run(1.7, down_project, 1, b, 7, False)
             down_freed()
             gelu_freed()
-            passed.update({("c", 1, DOWN), ("x", DOWN), ("z", DOWN), ("x", Q), ("x", V), ("z", Q), ("z", K), ("z", V)})
+            passed.update({("c", 1, DOWN), ("x", DOWN), ("z", DOWN), ("x", Q), ("x", K), ("x", V), ("z", Q), ("z", K), ("z", V)})
             clock.run(1.9, grad_down, 0, 1 - c, wdown.at[0])
             reduce(0, DOWN)
             clock.run(1.9, grad_down, 0, c, wdown.at[0])
@@ -1626,9 +1638,9 @@
         V((R, 1024), BF), V((R, 1024), F32), V((2, R, 1024), BF), V((R, 2048), BF), V((3, R, 512), BF),
         V((R, 1024), BF), V((2, R, 1024), BF), V((LP, 256), F32),
         V((2, 16, 1024), F32), V((2, 16, 1024), F32), V((16, 1024), F32), V((16, 1024), F32), V((3, 16, 1024), F32),
-        V((LP, 2, 1024), BF), V((1024, 1024), BF), V((32, 128), BF), V((6, 1, 128), BF), V((2, 8, 8), BF), V((8, 32), BF),
+        V((LP, 2, 1024), BF), V((1024, 1024), BF), V((32, 128), BF), V((6, 1, 128), BF), V((2, 8, 8), BF), V((8, 32), BF), V((2, 8, 64), F32), V((8, 256), F32),
         D_((14,)), D_((14, 2)), D_((54,)), D_((44,)),
-        D_((12,)), D_((12,)), D_((12,)), D_((36,)), D_((12, 2)), D_((64,)), D_((12,)), D_((12,)),
+        D_((12,)), D_((12,)), D_((12,)), D_((48,)), D_((12, 2)), D_((64,)), D_((12,)), D_((12,)),
         D_((16,)), D_((16,)), D_((4,)), D_((4,)), D_((4,)), D_((10,)), D_((5,)), D_((5,)),
         REG((6,)), REG((6,)), REG((6,)), REG, REG((2,)), REG,
     ]
@@ -1636,10 +1648,10 @@
         kernel,
         out_shape=[
             S((2, L, 2, 1024), BF), S((2, L, 2, 1024), BF), S((3, 128, 512), F32), S((512, 128), F32),
-            S((128, 2048), F32), S((2048, 128), F32), S((16, 1024), F32),
+            S((128, 2048), F32), S((2048, 128), F32), S((8, 1024), F32), S((2, 8, 64), F32), S((8, 256), F32),
         ],
         in_specs=[any_spec] * 14 + [pl.BlockSpec(memory_space=pltpu.SMEM)],
-        out_specs=[any_spec] * 7,
+        out_specs=[any_spec] * 9,
         scratch_shapes=scratch,
         compiler_params=pltpu.CompilerParams(
             collective_id=1, has_side_effects=True, vmem_limit_bytes=67043328
@@ -1655,7 +1667,7 @@
     def woven(a):
         return jnp.transpose(a, (0, 2, 1, 3))
 
-    act, gin, gqkv, gout, gup, gdown, gvec = run_kernel(
+    act, gin, gqkv, gout, gup, gdown, gvec, gqv, gupb = run_kernel(
         ln1_gain, ln1_bias, out_bias, ln2_gain, ln2_bias, down_bias, qv_bias[0], up_bias[0],
         qkv_weight[0], out_weight[0], up_weight[0], down_weight[0], woven(images), woven(cotangent), live_count.reshape(2),
     )
@@ -1664,9 +1676,9 @@
         return lax.dynamic_slice_in_dim(v, d * n, n, axis=axis)
 
     act, gin = woven(act)[None], woven(gin)[None]
-    vecs = cut(gvec[:6], 1, 128)
-    qv = cut(gvec[6].reshape(2, 8, 64), 2, 8)
-    upb = cut(gvec[7:9].reshape(8, 256), 1, 32)
+    vecs = cut(gvec, 1, 128)
+    qv = cut(gqv, 2, 8)
+    upb = cut(gupb, 1, 32)
     return (
         act, gin, vecs[0:1], vecs[1:2], gqkv[None], qv[None], gout[None], vecs[2:3], vecs[3:4], vecs[4:5],
         gup[None], upb[None], gdown[None], vecs[5:6],

time: 319 us -> 318 us (level)
  no operation moved by 1% of the time
where the time goes in v4:
time: 318 us
  Pallas kernels  304 us (96%)
  local copies, waits for them, and re-layouts  13 us (4%)
    pallas_call x1, Pallas kernels, run_kernel(): pl.pallas_call(kernel, out_shape=[S((2, L, 2, 1024), BF), S((2, L, 2, 102...  304 us
    unnamed x16, local copies, waits for them, and re-layouts  9.02 us

profile of v4, /device:TPU:0, one launch (start us, length us, event | category | flops | bytes accessed | tf_op | source)
XLA Modules:
  0.0 317.7 jit_solution(9928240729705608219)
XLA Ops:
  0.7 304.0 %sections.1 = (bf16[2,197,2,1024]{3,2,1,0:T(2,128)(2,1)}, bf16[2,197,2,1024]{3,2,1,0:T(2,128)(2,1)}, f32[3,128,512]{2,1,0:T(8,128)}, f32[512,128]{1,0:T(8,128)},...) custom-call(bf16[1,128]{1,0:T(2,128)(2,1)} %gain1_ref.1, ...), custom_call_target="tpu_custom_call" | custom-call | tf_op jit(solution)/shard_map/sections/pallas_call | solution.py:1647
  304.7 0.7 constant_dynamic-slice_fusion
  305.4 0.5 fusion
  305.9 1.4 dynamic-slice_bitcast_fusion
  307.3 1.3 dynamic-slice_bitcast_fusion.1
  308.7 0.0 copy-start
  308.7 3.8 %copy.35 = bf16[1,2,2,197,1024]{4,2,3,1,0:T(2,128)(2,1)} copy(bf16[1,2,2,197,1024]{4,2,3,1,0:T(2,128)(2,1)} %bitcast.26) | data formatting | bytes 3227648
  312.5 0.0 copy-done
  312.5 0.0 copy-start.3
  312.5 0.0 copy-start.4
  312.5 1.2 copy.36
  313.6 0.5 copy-done.3
  314.1 0.0 copy-start.2
  314.1 0.9 copy.37
  315.0 0.0 copy-done.4
  315.0 0.0 copy-start.1
  315.0 0.7 copy.38
  315.7 0.0 copy-done.2
  315.7 1.0 copy.39
  316.7 0.0 copy-done.1
  316.7 1.0 copy.40
Async XLA Ops:
  308.7 3.8 %copy-start = (bf16[2,197,2,1024]{3,2,1,0:T(2,128)(2,1)S(1)}, bf16[2,197,2,1024]{3,2,1,0:T(2,128)(2,1)}, u32[]{:S(2)}) copy-start(bf16[2,197,2,1024]{3,2,1,0:T(2,128)(2,1)} %get-tuple-element.24) | copy-start | bytes 4841476
  312.5 1.7 copy-start.3
  312.5 2.6 copy-start.4
  314.1 1.6 copy-start.2
  315.0 1.7 copy-start.1

commit v5 on v4

--- a/solution.py
+++ b/solution.py
@@ -1366,7 +1366,7 @@
             clock.add(x_begin[s, m], early)
         clock.add(max(z_begin[s, m] - LEAD, clock.now), own)
 
-    LEAD, AHEAD = 23.0, 2.0
+    LEAD, AHEAD = 23.0, 8.0
     z_begin, x_begin, at = {}, {}, 7.0
     for s in range(2):
         for m in order:

time: 318 us -> 317 us (level)
  no operation moved by 1% of the time
where the time goes in v5:
time: 317 us
  Pallas kernels  303 us (96%)
  local copies, waits for them, and re-layouts  13 us (4%)
    pallas_call x1, Pallas kernels, run_kernel(): pl.pallas_call(kernel, out_shape=[S((2, L, 2, 1024), BF), S((2, L, 2, 102...  303 us
    unnamed x16, local copies, waits for them, and re-layouts  9.02 us

profile of v5, /device:TPU:0, one launch (start us, length us, event | category | flops | bytes accessed | tf_op | source)
XLA Modules:
  0.0 316.6 jit_solution(13543141102131172306)
XLA Ops:
  0.7 303.0 %sections.1 = (bf16[2,197,2,1024]{3,2,1,0:T(2,128)(2,1)}, bf16[2,197,2,1024]{3,2,1,0:T(2,128)(2,1)}, f32[3,128,512]{2,1,0:T(8,128)}, f32[512,128]{1,0:T(8,128)},...) custom-call(bf16[1,128]{1,0:T(2,128)(2,1)} %gain1_ref.1, ...), custom_call_target="tpu_custom_call" | custom-call | tf_op jit(solution)/shard_map/sections/pallas_call | solution.py:1647
  303.7 0.7 constant_dynamic-slice_fusion
  304.4 0.5 fusion
  304.9 1.4 dynamic-slice_bitcast_fusion
  306.3 1.3 dynamic-slice_bitcast_fusion.1
  307.6 0.0 copy-start
  307.6 3.8 %copy.35 = bf16[1,2,2,197,1024]{4,2,3,1,0:T(2,128)(2,1)} copy(bf16[1,2,2,197,1024]{4,2,3,1,0:T(2,128)(2,1)} %bitcast.26) | data formatting | bytes 3227648
  311.4 0.0 copy-done
  311.4 0.0 copy-start.3
  311.4 0.0 copy-start.4
  311.4 1.2 copy.36
  312.6 0.5 copy-done.3
  313.1 0.0 copy-start.2
  313.1 0.9 copy.37
  314.0 0.0 copy-done.4
  314.0 0.0 copy-start.1
  314.0 0.7 copy.38
  314.7 0.0 copy-done.2
  314.7 1.0 copy.39
  315.7 0.0 copy-done.1
  315.7 1.0 copy.40
Async XLA Ops:
  307.6 3.8 %copy-start = (bf16[2,197,2,1024]{3,2,1,0:T(2,128)(2,1)S(1)}, bf16[2,197,2,1024]{3,2,1,0:T(2,128)(2,1)}, u32[]{:S(2)}) copy-start(bf16[2,197,2,1024]{3,2,1,0:T(2,128)(2,1)} %get-tuple-element.24) | copy-start | bytes 4841476
  311.4 1.7 copy-start.3
  311.4 2.6 copy-start.4
  313.1 1.6 copy-start.2
  314.0 1.7 copy-start.1
